TPU v7x, 512 devices: a whole 4x8x8 slice. The times are simulated.
512 devices in a mesh: dp: 2 (over core), layer: 8 (over z), col: 32 (over x, y).
Axes of the slice: x: 4, y: 8, z: 8, core: 2. Of those that a mesh axis runs over, the one named last changes fastest.
Arguments:
- tokens: bfloat16 [16, 256, 1024], P(None, 'dp', 'col'), parts along dimension 1, may hold values from -6 to 6
- w_input: bfloat16 [8, 1024, 4096], P('layer', None, 'col'), may hold values from -0.1875 to 0.1875
- w_recur: bfloat16 [8, 1024, 4096], P('layer', None, 'col'), may hold values from -0.1875 to 0.1875
- bias: float32 [8, 4096], P('layer', 'col'), may hold values from -1 to 5
Outputs:
- top_states: bfloat16 [16, 256, 1024], P('layer', 'dp', 'col'), parts along dimension 1
- final_h: bfloat16 [8, 256, 1024], P('layer', 'dp', 'col'), parts along dimension 1
- final_c: float32 [8, 256, 1024], P('layer', 'dp', 'col'), parts along dimension 1
There are 2 independent parts, one for each index of `dp`. A program takes and returns all parts, laid end to end along the dimension named above; an argument that names none is the same for every part. Nothing has to cross between parts.
All inputs are finite; a program needn't handle non-finite values.
Results may differ from a plain program's by a relative error of at most 0.008.
Values may be sent and summed in bfloat16 or wider, within the bound.
No kernel may reach another device: no remote copies, remote signals or barrier semaphores. Data moves between devices by JAX's collectives and lax.ppermute only.
A program may use at most 64 MiB of HBM per device.

v0:
```python
import jax
import jax.numpy as jnp
from jax import lax
from jax.sharding import PartitionSpec as P


def passed_along(block, axis, distance):
    devices = range(lax.axis_size(axis))
    route = [(i - distance, i) for i in devices if i - distance in devices]
    return lax.ppermute(block, axis, route)


def from_everyone(x, axis):
    copies = jnp.broadcast_to(x, (lax.axis_size(axis), *x.shape))
    return lax.all_to_all(copies, axis, split_axis=0, concat_axis=0, tiled=True)


def joined_along(pieces, dim):
    shape = list(pieces.shape[1:])
    shape[dim] *= pieces.shape[0]
    return jnp.moveaxis(pieces, 0, dim).reshape(shape)


def gather_directly(x, axis, dim):
    pieces = from_everyone(x, axis)
    return joined_along(pieces, dim)


def in_one_piece(arrays, axis, dim, along):
    widths = [a.shape[along] for a in arrays]
    both = jnp.concatenate(arrays, axis=along)
    filled = gather_directly(both, axis, dim)
    return tuple(jnp.split(filled, [sum(widths[:k]) for k in range(1, len(widths))], axis=along))


def from_root(x, axis, root):
    return lax.dynamic_index_in_dim(lax.all_gather(x, axis), root, 0, keepdims=False)


def shards(tokens, w_input, w_recur, bias):
    steps_count, sentences, units = tokens.shape
    w_local = w_input[0]
    r_local = w_recur[0]
    b_local = bias[0]
    layers = lax.axis_size("layer")
    level = lax.axis_index("layer")
    sections = steps_count + layers - 1
    is_first = level == 0
    has_skip = level >= 1
    is_last = level == layers - 1

    def cell_step(gates, cell):
        gates = gates.reshape(sentences, units, 4)
        in_gate = jax.nn.sigmoid(gates[:, :, 0])
        forget = jax.nn.sigmoid(gates[:, :, 1])
        update = jnp.tanh(gates[:, :, 2])
        out_gate = jax.nn.sigmoid(gates[:, :, 3])
        cell_new = forget * cell + in_gate * update
        hidden_new = (out_gate * jnp.tanh(cell_new)).astype(jnp.bfloat16)
        return (hidden_new, cell_new)

    def advance(in_full, h_full, cell):
        gates = jnp.dot(in_full, w_local, preferred_element_type=jnp.float32)
        gates = gates + jnp.dot(h_full, r_local, preferred_element_type=jnp.float32) + b_local
        return cell_step(gates, cell)

    def token_at(moment):
        where_at = jnp.clip(moment, 0, steps_count - 1)
        return lax.dynamic_index_in_dim(tokens, where_at, 0, keepdims=False)

    def record(buffer, hidden_new, moment, active):
        where_at = jnp.clip(moment, 0, steps_count - 1)
        written = lax.dynamic_update_index_in_dim(buffer, hidden_new, where_at, 0)
        return jnp.where(active & is_last, written, buffer)

    def skip_sum(hidden_new, in_part):
        summed = (hidden_new.astype(jnp.float32) + in_part.astype(jnp.float32)).astype(jnp.bfloat16)
        return jnp.where(has_skip, summed, hidden_new)

    zero_h = jnp.zeros((sentences, units), jnp.bfloat16)
    zero_c = jnp.zeros((sentences, units), jnp.float32)
    buffer = jnp.zeros((steps_count, sentences, units), jnp.bfloat16)

    def section_slice(section, carry):
        hidden, cell, outgoing, kept = carry
        moment = section - level
        active = (moment >= 0) & (moment < steps_count)
        received = passed_along(outgoing, "layer", 1)
        in_part = jnp.where(is_first, token_at(moment), received)
        h_full, in_full = in_one_piece((hidden, in_part), "col", 1, 0)
        hidden_new, cell_new = advance(in_full, h_full, cell)
        outgoing = skip_sum(hidden_new, in_part)
        kept = record(kept, hidden_new, moment, active)
        hidden = jnp.where(active, hidden_new, hidden)
        cell = jnp.where(active, cell_new, cell)
        return (hidden, cell, outgoing, kept)

    hidden, cell, outgoing, buffer = lax.fori_loop(
        0, sections, section_slice, (zero_h, zero_c, zero_h, buffer)
    )
    everything = from_root(buffer, "layer", layers - 1)
    block = steps_count // layers
    top_states = lax.dynamic_slice_in_dim(everything, level * block, block, 0)
    return (top_states, hidden[None], cell[None])


def solution(mesh):
    in_specs = (
        P(None, "dp", "col"),
        P("layer", None, "col"),
        P("layer", None, "col"),
        P("layer", "col"),
    )
    out_specs = (P("layer", "dp", "col"), P("layer", "dp", "col"), P("layer", "dp", "col"))
    return jax.shard_map(shards, mesh=mesh, in_specs=in_specs, out_specs=out_specs, check_vma=False)
```

profile of v0, /device:TPU:2, one launch (start us, length us, event | category | flops | bytes accessed | tf_op | source)
XLA Modules:
  0.0 750.2 jit_solution(9231002011546703083)
XLA Ops:
  7.9 685.7 %while.20 = (s32[]{:T(128)}, bf16[128,32]{0,1:T(8,128)(2,1)S(1)}, f32[128,32]{0,1:T(8,128)S(1)}, bf16[128,32]{0,1:T(8,128)(2,1)S(1)}, bf16[16,128,32]{1,2,0:T(8,...) while((s32[]{:T(128)}, bf16[128,32]{0,1:T(8,128)(2,1)S(1)}, ...), condition=%wide.region_1.2_spmd.clone, body=%wide.region_0.1_spmd.clone.sunk | while | flops 67289096 | bytes 6972276 | solution.py:98
  25.4 14.6 %all-to-all-done = bf16[32,256,32]{1,2,0:T(8,128)(2,1)S(1)} async-done(((bf16[32,256,32]{1,2,0:T(8,128)(2,1)}), bf16[32,256,32]{1,2,0:T(8,128)(2,1)S(1)}, u32[]{:S(2)}, u32[]{:S(2)}) %all-to-all-start) | async-done | bytes 524320 | tf_op jit(solution)/shard_map/while/body/eval_jaxpr/all_to_all | solution.py:15
  56.6 13.7 %all-to-all-done = bf16[32,256,32]{1,2,0:T(8,128)(2,1)S(1)} async-done(((bf16[32,256,32]{1,2,0:T(8,128)(2,1)}), bf16[32,256,32]{1,2,0:T(8,128)(2,1)S(1)}, u32[]{:S(2)}, u32[]{:S(2)}) %all-to-all-start) | async-done | bytes 524320 | tf_op jit(solution)/shard_map/while/body/eval_jaxpr/all_to_all | solution.py:15
  86.9 12.4 %all-to-all-done = bf16[32,256,32]{1,2,0:T(8,128)(2,1)S(1)} async-done(((bf16[32,256,32]{1,2,0:T(8,128)(2,1)}), bf16[32,256,32]{1,2,0:T(8,128)(2,1)S(1)}, u32[]{:S(2)}, u32[]{:S(2)}) %all-to-all-start) | async-done | bytes 524320 | tf_op jit(solution)/shard_map/while/body/eval_jaxpr/all_to_all | solution.py:15
  117.1 11.7 %all-to-all-done = bf16[32,256,32]{1,2,0:T(8,128)(2,1)S(1)} async-done(((bf16[32,256,32]{1,2,0:T(8,128)(2,1)}), bf16[32,256,32]{1,2,0:T(8,128)(2,1)S(1)}, u32[]{:S(2)}, u32[]{:S(2)}) %all-to-all-start) | async-done | bytes 524320 | tf_op jit(solution)/shard_map/while/body/eval_jaxpr/all_to_all | solution.py:15
  144.9 11.3 %all-to-all-done = bf16[32,256,32]{1,2,0:T(8,128)(2,1)S(1)} async-done(((bf16[32,256,32]{1,2,0:T(8,128)(2,1)}), bf16[32,256,32]{1,2,0:T(8,128)(2,1)S(1)}, u32[]{:S(2)}, u32[]{:S(2)}) %all-to-all-start) | async-done | bytes 524320 | tf_op jit(solution)/shard_map/while/body/eval_jaxpr/all_to_all | solution.py:15
  172.9 11.3 %all-to-all-done = bf16[32,256,32]{1,2,0:T(8,128)(2,1)S(1)} async-done(((bf16[32,256,32]{1,2,0:T(8,128)(2,1)}), bf16[32,256,32]{1,2,0:T(8,128)(2,1)S(1)}, u32[]{:S(2)}, u32[]{:S(2)}) %all-to-all-start) | async-done | bytes 524320 | tf_op jit(solution)/shard_map/while/body/eval_jaxpr/all_to_all | solution.py:15
  201.7 11.3 %all-to-all-done = bf16[32,256,32]{1,2,0:T(8,128)(2,1)S(1)} async-done(((bf16[32,256,32]{1,2,0:T(8,128)(2,1)}), bf16[32,256,32]{1,2,0:T(8,128)(2,1)S(1)}, u32[]{:S(2)}, u32[]{:S(2)}) %all-to-all-start) | async-done | bytes 524320 | tf_op jit(solution)/shard_map/while/body/eval_jaxpr/all_to_all | solution.py:15
  230.7 11.3 %all-to-all-done = bf16[32,256,32]{1,2,0:T(8,128)(2,1)S(1)} async-done(((bf16[32,256,32]{1,2,0:T(8,128)(2,1)}), bf16[32,256,32]{1,2,0:T(8,128)(2,1)S(1)}, u32[]{:S(2)}, u32[]{:S(2)}) %all-to-all-start) | async-done | bytes 524320 | tf_op jit(solution)/shard_map/while/body/eval_jaxpr/all_to_all | solution.py:15
  259.6 11.4 %all-to-all-done = bf16[32,256,32]{1,2,0:T(8,128)(2,1)S(1)} async-done(((bf16[32,256,32]{1,2,0:T(8,128)(2,1)}), bf16[32,256,32]{1,2,0:T(8,128)(2,1)S(1)}, u32[]{:S(2)}, u32[]{:S(2)}) %all-to-all-start) | async-done | bytes 524320 | tf_op jit(solution)/shard_map/while/body/eval_jaxpr/all_to_all | solution.py:15
  288.6 11.7 %all-to-all-done = bf16[32,256,32]{1,2,0:T(8,128)(2,1)S(1)} async-done(((bf16[32,256,32]{1,2,0:T(8,128)(2,1)}), bf16[32,256,32]{1,2,0:T(8,128)(2,1)S(1)}, u32[]{:S(2)}, u32[]{:S(2)}) %all-to-all-start) | async-done | bytes 524320 | tf_op jit(solution)/shard_map/while/body/eval_jaxpr/all_to_all | solution.py:15
  319.5 13.8 %all-to-all-done = bf16[32,256,32]{1,2,0:T(8,128)(2,1)S(1)} async-done(((bf16[32,256,32]{1,2,0:T(8,128)(2,1)}), bf16[32,256,32]{1,2,0:T(8,128)(2,1)S(1)}, u32[]{:S(2)}, u32[]{:S(2)}) %all-to-all-start) | async-done | bytes 524320 | tf_op jit(solution)/shard_map/while/body/eval_jaxpr/all_to_all | solution.py:15
  354.3 14.9 %all-to-all-done = bf16[32,256,32]{1,2,0:T(8,128)(2,1)S(1)} async-done(((bf16[32,256,32]{1,2,0:T(8,128)(2,1)}), bf16[32,256,32]{1,2,0:T(8,128)(2,1)S(1)}, u32[]{:S(2)}, u32[]{:S(2)}) %all-to-all-start) | async-done | bytes 524320 | tf_op jit(solution)/shard_map/while/body/eval_jaxpr/all_to_all | solution.py:15
  387.0 13.9 %all-to-all-done = bf16[32,256,32]{1,2,0:T(8,128)(2,1)S(1)} async-done(((bf16[32,256,32]{1,2,0:T(8,128)(2,1)}), bf16[32,256,32]{1,2,0:T(8,128)(2,1)S(1)}, u32[]{:S(2)}, u32[]{:S(2)}) %all-to-all-start) | async-done | bytes 524320 | tf_op jit(solution)/shard_map/while/body/eval_jaxpr/all_to_all | solution.py:15
  419.0 12.5 %all-to-all-done = bf16[32,256,32]{1,2,0:T(8,128)(2,1)S(1)} async-done(((bf16[32,256,32]{1,2,0:T(8,128)(2,1)}), bf16[32,256,32]{1,2,0:T(8,128)(2,1)S(1)}, u32[]{:S(2)}, u32[]{:S(2)}) %all-to-all-start) | async-done | bytes 524320 | tf_op jit(solution)/shard_map/while/body/eval_jaxpr/all_to_all | solution.py:15
  449.4 11.6 %all-to-all-done = bf16[32,256,32]{1,2,0:T(8,128)(2,1)S(1)} async-done(((bf16[32,256,32]{1,2,0:T(8,128)(2,1)}), bf16[32,256,32]{1,2,0:T(8,128)(2,1)S(1)}, u32[]{:S(2)}, u32[]{:S(2)}) %all-to-all-start) | async-done | bytes 524320 | tf_op jit(solution)/shard_map/while/body/eval_jaxpr/all_to_all | solution.py:15
  478.0 11.3 %all-to-all-done = bf16[32,256,32]{1,2,0:T(8,128)(2,1)S(1)} async-done(((bf16[32,256,32]{1,2,0:T(8,128)(2,1)}), bf16[32,256,32]{1,2,0:T(8,128)(2,1)S(1)}, u32[]{:S(2)}, u32[]{:S(2)}) %all-to-all-start) | async-done | bytes 524320 | tf_op jit(solution)/shard_map/while/body/eval_jaxpr/all_to_all | solution.py:15
  506.5 11.3 %all-to-all-done = bf16[32,256,32]{1,2,0:T(8,128)(2,1)S(1)} async-done(((bf16[32,256,32]{1,2,0:T(8,128)(2,1)}), bf16[32,256,32]{1,2,0:T(8,128)(2,1)S(1)}, u32[]{:S(2)}, u32[]{:S(2)}) %all-to-all-start) | async-done | bytes 524320 | tf_op jit(solution)/shard_map/while/body/eval_jaxpr/all_to_all | solution.py:15
  564.1 11.3 %all-to-all-done = bf16[32,256,32]{1,2,0:T(8,128)(2,1)S(1)} async-done(((bf16[32,256,32]{1,2,0:T(8,128)(2,1)}), bf16[32,256,32]{1,2,0:T(8,128)(2,1)S(1)}, u32[]{:S(2)}, u32[]{:S(2)}) %all-to-all-start) | async-done | bytes 524320 | tf_op jit(solution)/shard_map/while/body/eval_jaxpr/all_to_all | solution.py:15
  593.1 11.3 %all-to-all-done = bf16[32,256,32]{1,2,0:T(8,128)(2,1)S(1)} async-done(((bf16[32,256,32]{1,2,0:T(8,128)(2,1)}), bf16[32,256,32]{1,2,0:T(8,128)(2,1)S(1)}, u32[]{:S(2)}, u32[]{:S(2)}) %all-to-all-start) | async-done | bytes 524320 | tf_op jit(solution)/shard_map/while/body/eval_jaxpr/all_to_all | solution.py:15
  622.1 11.3 %all-to-all-done = bf16[32,256,32]{1,2,0:T(8,128)(2,1)S(1)} async-done(((bf16[32,256,32]{1,2,0:T(8,128)(2,1)}), bf16[32,256,32]{1,2,0:T(8,128)(2,1)S(1)}, u32[]{:S(2)}, u32[]{:S(2)}) %all-to-all-start) | async-done | bytes 524320 | tf_op jit(solution)/shard_map/while/body/eval_jaxpr/all_to_all | solution.py:15
  651.0 11.3 %all-to-all-done = bf16[32,256,32]{1,2,0:T(8,128)(2,1)S(1)} async-done(((bf16[32,256,32]{1,2,0:T(8,128)(2,1)}), bf16[32,256,32]{1,2,0:T(8,128)(2,1)S(1)}, u32[]{:S(2)}, u32[]{:S(2)}) %all-to-all-start) | async-done | bytes 524320 | tf_op jit(solution)/shard_map/while/body/eval_jaxpr/all_to_all | solution.py:15
  680.0 11.3 %all-to-all-done = bf16[32,256,32]{1,2,0:T(8,128)(2,1)S(1)} async-done(((bf16[32,256,32]{1,2,0:T(8,128)(2,1)}), bf16[32,256,32]{1,2,0:T(8,128)(2,1)S(1)}, u32[]{:S(2)}, u32[]{:S(2)}) %all-to-all-start) | async-done | bytes 524320 | tf_op jit(solution)/shard_map/while/body/eval_jaxpr/all_to_all | solution.py:15
  694.4 47.5 %all-gather.3.cloned.1.call-done = bf16[128,128,32]{1,2,0:T(8,128)(2,1)} async-done(((bf16[16,128,32]{1,2,0:T(8,128)(2,1)}), bf16[128,128,32]{1,2,0:T(8,128)(2,1)}) %all-gather.3.cloned.1.call-update) | async-done | bytes 1048592 | tf_op jit(solution)/shard_map/all_gather | solution.py:37
  (455 shorter events, 419.4 us)
Async XLA Ops:
  7.2 734.7 %all-gather.3.cloned.1.call-start = ((), (), s32[]{:S(2)}) async-start(), calls=%async_computation.1 | async-start | bytes 1179648 | tf_op jit(solution)/shard_map/all_gather | solution.py:37
  15.1 24.9 %all-to-all-start = ((bf16[32,256,32]{1,2,0:T(8,128)(2,1)}), bf16[32,256,32]{1,2,0:T(8,128)(2,1)S(1)}, u32[]{:S(2)}, u32[]{:S(2)}) async-start(bf16[32,256,32]{1,2,0:T(8,128)(2,1)} %broadcast_in_dim.38), calls=%async_computation | async-start | bytes 1048576 | tf_op jit(solution)/shard_map/while/body/eval_jaxpr/all_to_all | solution.py:15
  49.6 20.7 %all-to-all-start = ((bf16[32,256,32]{1,2,0:T(8,128)(2,1)}), bf16[32,256,32]{1,2,0:T(8,128)(2,1)S(1)}, u32[]{:S(2)}, u32[]{:S(2)}) async-start(bf16[32,256,32]{1,2,0:T(8,128)(2,1)} %broadcast_in_dim.38), calls=%async_computation | async-start | bytes 1048576 | tf_op jit(solution)/shard_map/while/body/eval_jaxpr/all_to_all | solution.py:15
  79.8 19.4 %all-to-all-start = ((bf16[32,256,32]{1,2,0:T(8,128)(2,1)}), bf16[32,256,32]{1,2,0:T(8,128)(2,1)S(1)}, u32[]{:S(2)}, u32[]{:S(2)}) async-start(bf16[32,256,32]{1,2,0:T(8,128)(2,1)} %broadcast_in_dim.38), calls=%async_computation | async-start | bytes 1048576 | tf_op jit(solution)/shard_map/while/body/eval_jaxpr/all_to_all | solution.py:15
  110.0 18.7 %all-to-all-start = ((bf16[32,256,32]{1,2,0:T(8,128)(2,1)}), bf16[32,256,32]{1,2,0:T(8,128)(2,1)S(1)}, u32[]{:S(2)}, u32[]{:S(2)}) async-start(bf16[32,256,32]{1,2,0:T(8,128)(2,1)} %broadcast_in_dim.38), calls=%async_computation | async-start | bytes 1048576 | tf_op jit(solution)/shard_map/while/body/eval_jaxpr/all_to_all | solution.py:15
  138.3 18.0 %all-to-all-start = ((bf16[32,256,32]{1,2,0:T(8,128)(2,1)}), bf16[32,256,32]{1,2,0:T(8,128)(2,1)S(1)}, u32[]{:S(2)}, u32[]{:S(2)}) async-start(bf16[32,256,32]{1,2,0:T(8,128)(2,1)} %broadcast_in_dim.38), calls=%async_computation | async-start | bytes 1048576 | tf_op jit(solution)/shard_map/while/body/eval_jaxpr/all_to_all | solution.py:15
  165.9 18.3 %all-to-all-start = ((bf16[32,256,32]{1,2,0:T(8,128)(2,1)}), bf16[32,256,32]{1,2,0:T(8,128)(2,1)S(1)}, u32[]{:S(2)}, u32[]{:S(2)}) async-start(bf16[32,256,32]{1,2,0:T(8,128)(2,1)} %broadcast_in_dim.38), calls=%async_computation | async-start | bytes 1048576 | tf_op jit(solution)/shard_map/while/body/eval_jaxpr/all_to_all | solution.py:15
  194.7 18.3 %all-to-all-start = ((bf16[32,256,32]{1,2,0:T(8,128)(2,1)}), bf16[32,256,32]{1,2,0:T(8,128)(2,1)S(1)}, u32[]{:S(2)}, u32[]{:S(2)}) async-start(bf16[32,256,32]{1,2,0:T(8,128)(2,1)} %broadcast_in_dim.38), calls=%async_computation | async-start | bytes 1048576 | tf_op jit(solution)/shard_map/while/body/eval_jaxpr/all_to_all | solution.py:15
  223.7 18.3 %all-to-all-start = ((bf16[32,256,32]{1,2,0:T(8,128)(2,1)}), bf16[32,256,32]{1,2,0:T(8,128)(2,1)S(1)}, u32[]{:S(2)}, u32[]{:S(2)}) async-start(bf16[32,256,32]{1,2,0:T(8,128)(2,1)} %broadcast_in_dim.38), calls=%async_computation | async-start | bytes 1048576 | tf_op jit(solution)/shard_map/while/body/eval_jaxpr/all_to_all | solution.py:15
  252.7 18.3 %all-to-all-start = ((bf16[32,256,32]{1,2,0:T(8,128)(2,1)}), bf16[32,256,32]{1,2,0:T(8,128)(2,1)S(1)}, u32[]{:S(2)}, u32[]{:S(2)}) async-start(bf16[32,256,32]{1,2,0:T(8,128)(2,1)} %broadcast_in_dim.38), calls=%async_computation | async-start | bytes 1048576 | tf_op jit(solution)/shard_map/while/body/eval_jaxpr/all_to_all | solution.py:15
  281.7 18.6 %all-to-all-start = ((bf16[32,256,32]{1,2,0:T(8,128)(2,1)}), bf16[32,256,32]{1,2,0:T(8,128)(2,1)S(1)}, u32[]{:S(2)}, u32[]{:S(2)}) async-start(bf16[32,256,32]{1,2,0:T(8,128)(2,1)} %broadcast_in_dim.38), calls=%async_computation | async-start | bytes 1048576 | tf_op jit(solution)/shard_map/while/body/eval_jaxpr/all_to_all | solution.py:15
  310.9 22.4 %all-to-all-start = ((bf16[32,256,32]{1,2,0:T(8,128)(2,1)}), bf16[32,256,32]{1,2,0:T(8,128)(2,1)S(1)}, u32[]{:S(2)}, u32[]{:S(2)}) async-start(bf16[32,256,32]{1,2,0:T(8,128)(2,1)} %broadcast_in_dim.38), calls=%async_computation | async-start | bytes 1048576 | tf_op jit(solution)/shard_map/while/body/eval_jaxpr/all_to_all | solution.py:15
  345.5 23.8 %all-to-all-start = ((bf16[32,256,32]{1,2,0:T(8,128)(2,1)}), bf16[32,256,32]{1,2,0:T(8,128)(2,1)S(1)}, u32[]{:S(2)}, u32[]{:S(2)}) async-start(bf16[32,256,32]{1,2,0:T(8,128)(2,1)} %broadcast_in_dim.38), calls=%async_computation | async-start | bytes 1048576 | tf_op jit(solution)/shard_map/while/body/eval_jaxpr/all_to_all | solution.py:15
  380.0 20.9 %all-to-all-start = ((bf16[32,256,32]{1,2,0:T(8,128)(2,1)}), bf16[32,256,32]{1,2,0:T(8,128)(2,1)S(1)}, u32[]{:S(2)}, u32[]{:S(2)}) async-start(bf16[32,256,32]{1,2,0:T(8,128)(2,1)} %broadcast_in_dim.38), calls=%async_computation | async-start | bytes 1048576 | tf_op jit(solution)/shard_map/while/body/eval_jaxpr/all_to_all | solution.py:15
  412.0 19.6 %all-to-all-start = ((bf16[32,256,32]{1,2,0:T(8,128)(2,1)}), bf16[32,256,32]{1,2,0:T(8,128)(2,1)S(1)}, u32[]{:S(2)}, u32[]{:S(2)}) async-start(bf16[32,256,32]{1,2,0:T(8,128)(2,1)} %broadcast_in_dim.38), calls=%async_computation | async-start | bytes 1048576 | tf_op jit(solution)/shard_map/while/body/eval_jaxpr/all_to_all | solution.py:15
  442.5 18.5 %all-to-all-start = ((bf16[32,256,32]{1,2,0:T(8,128)(2,1)}), bf16[32,256,32]{1,2,0:T(8,128)(2,1)S(1)}, u32[]{:S(2)}, u32[]{:S(2)}) async-start(bf16[32,256,32]{1,2,0:T(8,128)(2,1)} %broadcast_in_dim.38), calls=%async_computation | async-start | bytes 1048576 | tf_op jit(solution)/shard_map/while/body/eval_jaxpr/all_to_all | solution.py:15
  471.3 18.0 %all-to-all-start = ((bf16[32,256,32]{1,2,0:T(8,128)(2,1)}), bf16[32,256,32]{1,2,0:T(8,128)(2,1)S(1)}, u32[]{:S(2)}, u32[]{:S(2)}) async-start(bf16[32,256,32]{1,2,0:T(8,128)(2,1)} %broadcast_in_dim.38), calls=%async_computation | async-start | bytes 1048576 | tf_op jit(solution)/shard_map/while/body/eval_jaxpr/all_to_all | solution.py:15
  499.6 18.3 %all-to-all-start = ((bf16[32,256,32]{1,2,0:T(8,128)(2,1)}), bf16[32,256,32]{1,2,0:T(8,128)(2,1)S(1)}, u32[]{:S(2)}, u32[]{:S(2)}) async-start(bf16[32,256,32]{1,2,0:T(8,128)(2,1)} %broadcast_in_dim.38), calls=%async_computation | async-start | bytes 1048576 | tf_op jit(solution)/shard_map/while/body/eval_jaxpr/all_to_all | solution.py:15
  528.2 18.3 %all-to-all-start = ((bf16[32,256,32]{1,2,0:T(8,128)(2,1)}), bf16[32,256,32]{1,2,0:T(8,128)(2,1)S(1)}, u32[]{:S(2)}, u32[]{:S(2)}) async-start(bf16[32,256,32]{1,2,0:T(8,128)(2,1)} %broadcast_in_dim.38), calls=%async_computation | async-start | bytes 1048576 | tf_op jit(solution)/shard_map/while/body/eval_jaxpr/all_to_all | solution.py:15
  557.2 18.3 %all-to-all-start = ((bf16[32,256,32]{1,2,0:T(8,128)(2,1)}), bf16[32,256,32]{1,2,0:T(8,128)(2,1)S(1)}, u32[]{:S(2)}, u32[]{:S(2)}) async-start(bf16[32,256,32]{1,2,0:T(8,128)(2,1)} %broadcast_in_dim.38), calls=%async_computation | async-start | bytes 1048576 | tf_op jit(solution)/shard_map/while/body/eval_jaxpr/all_to_all | solution.py:15
  586.1 18.3 %all-to-all-start = ((bf16[32,256,32]{1,2,0:T(8,128)(2,1)}), bf16[32,256,32]{1,2,0:T(8,128)(2,1)S(1)}, u32[]{:S(2)}, u32[]{:S(2)}) async-start(bf16[32,256,32]{1,2,0:T(8,128)(2,1)} %broadcast_in_dim.38), calls=%async_computation | async-start | bytes 1048576 | tf_op jit(solution)/shard_map/while/body/eval_jaxpr/all_to_all | solution.py:15
  615.1 18.3 %all-to-all-start = ((bf16[32,256,32]{1,2,0:T(8,128)(2,1)}), bf16[32,256,32]{1,2,0:T(8,128)(2,1)S(1)}, u32[]{:S(2)}, u32[]{:S(2)}) async-start(bf16[32,256,32]{1,2,0:T(8,128)(2,1)} %broadcast_in_dim.38), calls=%async_computation | async-start | bytes 1048576 | tf_op jit(solution)/shard_map/while/body/eval_jaxpr/all_to_all | solution.py:15
  644.1 18.3 %all-to-all-start = ((bf16[32,256,32]{1,2,0:T(8,128)(2,1)}), bf16[32,256,32]{1,2,0:T(8,128)(2,1)S(1)}, u32[]{:S(2)}, u32[]{:S(2)}) async-start(bf16[32,256,32]{1,2,0:T(8,128)(2,1)} %broadcast_in_dim.38), calls=%async_computation | async-start | bytes 1048576 | tf_op jit(solution)/shard_map/while/body/eval_jaxpr/all_to_all | solution.py:15
  673.0 18.3 %all-to-all-start = ((bf16[32,256,32]{1,2,0:T(8,128)(2,1)}), bf16[32,256,32]{1,2,0:T(8,128)(2,1)S(1)}, u32[]{:S(2)}, u32[]{:S(2)}) async-start(bf16[32,256,32]{1,2,0:T(8,128)(2,1)} %broadcast_in_dim.38), calls=%async_computation | async-start | bytes 1048576 | tf_op jit(solution)/shard_map/while/body/eval_jaxpr/all_to_all | solution.py:15
  (74 other events, 198.1 us)
Sparse Core Ops, SparseCore 0:
  694.5 47.3 all-gather.2
where the time goes:
time: 755 us; the launch traced here: 750 us
  waiting for transfers between devices  356 us (47%)
  starting transfers between devices  285 us (38%)
  local copies, waits for them, and re-layouts  61.1 us (8%)
  other arithmetic  18.3 us (2%)
  between operations  14.1 us (2%)
  matrix products  12.6 us (2%)
    all_to_all x23, waiting for transfers between devices, from_everyone(): return lax.all_to_all(copies, axis, split_axis=0, concat_axis=0, tiled=True)  278 us
    all_to_all x23, starting transfers between devices, from_everyone(): return lax.all_to_all(copies, axis, split_axis=0, concat_axis=0, tiled=True)  166 us
    ppermute x23, starting transfers between devices, passed_along(): return lax.ppermute(block, axis, route)  120 us
    all_gather x1, waiting for transfers between devices, from_root(): lax.all_gather(x, axis)  47.5 us
    while x92, local copies, waits for them, and re-layouts  35.1 us
    ppermute x23, waiting for transfers between devices, passed_along(): return lax.ppermute(block, axis, route)  30.5 us
    broadcast_in_dim x23, local copies, waits for them, and re-layouts, from_everyone(): copies = jnp.broadcast_to(x, (lax.axis_size(axis), *x.shape))  20 us
    select_n x23, other arithmetic, section_slice(): in_part = jnp.where(is_first, token_at(moment), received)  16.1 us
  transfers between devices with their start and end apart: 47, of which 47 were waited for; matrix products, arithmetic and copies ran while one was open for 0% of the time, Pallas kernels for 0%

commit v1 on v0

v1 whole, which is shorter than its diff:
```python
import jax
import jax.numpy as jnp
from jax import lax
from jax.experimental import pallas as pl
from jax.experimental.pallas import tpu as pltpu
from jax.sharding import PartitionSpec as P

H = 1024
ROWS = 4
STEPS = 2
LANES = 128
WIDE = 512
BLOCKS = 4 * H // WIDE


def passed_along(block, axis, distance):
    devices = range(lax.axis_size(axis))
    route = [(i - distance, i) for i in devices if i - distance in devices]
    return lax.ppermute(block, axis, route)


def segments_swapped(quad, lane):
    gates = []
    for k in range(4):
        out = None
        for j in range(4):
            shift = (32 * (j - k)) % LANES
            moved = quad[j] if shift == 0 else pltpu.roll(quad[j], shift, 1)
            out = moved if out is None else jnp.where(lane >= 32 * j, moved, out)
        gates.append(out)
    return gates


def stage_kernel(flags, x_got, x_token, h_was, c_was, bias, weights, hs_out, x_out, h_out, c_out, w_in, w_rec, gx, sems):
    active = flags[0] == 1

    @pl.when(active)
    def _():
        copies = []
        for m, target in ((0, w_in), (1, w_rec)):
            for p in range(H // 32):
                copies.append(
                    pltpu.make_async_copy(
                        weights.at[p, m],
                        target.at[:, pl.ds(LANES * p, LANES)],
                        sems.at[m, p],
                    )
                )
        for copy in copies:
            copy.start()
        x = jnp.where(flags[1] == 1, x_token[...].astype(jnp.float32), x_got[...].astype(jnp.float32))
        x_low = x.astype(jnp.bfloat16)
        lane = lax.broadcasted_iota(jnp.int32, (2 * ROWS, LANES), 1)
        row = lax.broadcasted_iota(jnp.int32, (2 * ROWS, H), 0)
        update = (lane >= 64) & (lane < 96)
        scale = jnp.where(update, 1.0, 0.5)
        shift = jnp.where(update, 0.0, 0.5)
        for q in range(BLOCKS):
            for p in range(4):
                copies[4 * q + p].wait()
            part = jnp.dot(x_low, w_in[:, WIDE * q : WIDE * (q + 1)], preferred_element_type=jnp.float32)
            for j in range(4):
                lanes = slice(WIDE * q + LANES * j, WIDE * q + LANES * (j + 1))
                gx[:, lanes] = (part[:, LANES * j : LANES * (j + 1)] + bias[:, lanes]) * scale
        hidden = h_was[...]
        states = []
        for step in range(STEPS):
            h_low = hidden.astype(jnp.bfloat16)
            pieces = []
            for q in range(BLOCKS):
                if step == 0:
                    for p in range(4):
                        copies[H // 32 + 4 * q + p].wait()
                gates = jnp.dot(h_low, w_rec[:, WIDE * q : WIDE * (q + 1)], preferred_element_type=jnp.float32)
                quad = []
                for j in range(4):
                    lanes = slice(WIDE * q + LANES * j, WIDE * q + LANES * (j + 1))
                    z = gates[:, LANES * j : LANES * (j + 1)] * scale + gx[:, lanes]
                    quad.append(jnp.tanh(z) * scale + shift)
                g_in, g_forget, g_update, g_out = segments_swapped(quad, lane)
                here = slice(LANES * q, LANES * (q + 1))
                cell = c_was[:, here] if step == 0 else c_out[:, here]
                cell = g_forget * cell + g_in * g_update
                c_out[:, here] = pltpu.roll(cell, ROWS, 0)
                pieces.append((g_out * jnp.tanh(cell)).astype(jnp.bfloat16).astype(jnp.float32))
            fresh = jnp.concatenate(pieces, axis=1)
            states.append(fresh)
            hidden = pltpu.roll(fresh, ROWS, 0)
        h_out[...] = hidden
        both = jnp.where(row < ROWS, states[0], states[1])
        hs_out[...] = both.astype(jnp.bfloat16)
        x_out[...] = jnp.where(flags[2] == 1, both + x, both).astype(jnp.bfloat16)

    @pl.when(jnp.logical_not(active))
    def _():
        h_out[...] = h_was[...]
        c_out[...] = c_was[...]
        hs_out[...] = x_got[...]
        x_out[...] = x_got[...]


def stage(flags, x_got, x_token, h_was, c_was, bias, weights):
    full = pl.BlockSpec(memory_space=pltpu.VMEM)
    low = jax.ShapeDtypeStruct((2 * ROWS, H), jnp.bfloat16)
    high = jax.ShapeDtypeStruct((2 * ROWS, H), jnp.float32)
    return pl.pallas_call(
        stage_kernel,
        out_shape=(low, low, high, high),
        in_specs=[pl.BlockSpec(memory_space=pltpu.SMEM), full, full, full, full, full, pl.BlockSpec(memory_space=pltpu.HBM)],
        out_specs=(full, full, full, full),
        scratch_shapes=[
            pltpu.VMEM((H, 4 * H), jnp.bfloat16),
            pltpu.VMEM((H, 4 * H), jnp.bfloat16),
            pltpu.VMEM((2 * ROWS, 4 * H), jnp.float32),
            pltpu.SemaphoreType.DMA((2, H // 32)),
        ],
        compiler_params=pltpu.CompilerParams(vmem_limit_bytes=40 * 1024 * 1024),
    )(flags, x_got, x_token, h_was, c_was, bias, weights)


def shards(tokens, w_input, w_recur, bias):
    steps_count, sentences, units = tokens.shape
    layers = lax.axis_size("layer")
    cols = lax.axis_size("col")
    level = lax.axis_index("layer")
    chunks = steps_count // STEPS
    stages = chunks + layers - 1

    at = jnp.arange(4 * units)
    order = (at[:, None] == 4 * (at % units) + at // units).astype(jnp.bfloat16)
    both = jnp.concatenate([w_input[0], w_recur[0]], axis=0)
    both = jnp.dot(both, order, preferred_element_type=jnp.float32).astype(jnp.bfloat16)
    weights = lax.all_gather(both.reshape(2, H, 4 * units), "col")

    local_bias = bias[0].reshape(units, 4).T.reshape(1, 4 * units)
    mine = tokens.reshape(steps_count, cols, ROWS, units).transpose(1, 0, 2, 3).astype(jnp.float32)
    sent = jnp.concatenate([mine.reshape(cols, -1), jnp.broadcast_to(local_bias, (cols, 4 * units))], axis=1)
    got = lax.all_to_all(sent, "col", 0, 0, tiled=True)
    x_first = got[:, : steps_count * ROWS * units].reshape(cols, steps_count * ROWS, units).transpose(1, 0, 2)
    x_first = x_first.reshape(chunks, STEPS * ROWS, H).astype(jnp.bfloat16)
    bias_full = got[:, steps_count * ROWS * units :].reshape(1, 4 * H)

    def section(carry, s):
        x_sent, hidden, cell = carry
        x_got = passed_along(x_sent, "layer", 1)
        chunk = s - level
        active = (chunk >= 0) & (chunk < chunks)
        flags = jnp.stack([active, level == 0, level >= 1]).astype(jnp.int32)
        x_token = lax.dynamic_index_in_dim(x_first, jnp.clip(chunk, 0, chunks - 1), 0, keepdims=False)
        hs, x_next, hidden, cell = stage(flags, x_got, x_token, hidden, cell, bias_full, weights)
        return (x_next, hidden, cell), hs

    zero_x = jnp.zeros((STEPS * ROWS, H), jnp.bfloat16)
    zero_s = jnp.zeros((STEPS * ROWS, H), jnp.float32)
    (_, hidden, cell), states = lax.scan(section, (zero_x, zero_s, zero_s), jnp.arange(stages))

    top = lax.all_to_all(states[layers - 1 :], "layer", 0, 0, tiled=True)[layers - 1]
    rows = jnp.concatenate([top.astype(jnp.float32), hidden[:ROWS], cell[:ROWS]], axis=0)
    sent = rows.reshape(4 * ROWS, cols, units).transpose(1, 0, 2)
    got = lax.all_to_all(sent, "col", 0, 0, tiled=True).reshape(cols, 4, ROWS, units).transpose(1, 0, 2, 3)
    got = got.reshape(4, sentences, units)
    return got[:2].astype(jnp.bfloat16), got[2:3].astype(jnp.bfloat16), got[3:]


def solution(mesh):
    in_specs = (
        P(None, "dp", "col"),
        P("layer", None, "col"),
        P("layer", None, "col"),
        P("layer", "col"),
    )
    out_specs = (P("layer", "dp", "col"), P("layer", "dp", "col"), P("layer", "dp", "col"))
    return jax.shard_map(shards, mesh=mesh, in_specs=in_specs, out_specs=out_specs, check_vma=False)
```

time: 755 us -> 419 us (0.55)
  the two profiles are of different devices: /device:TPU:2 before, /device:TPU:8 now
where the time goes in v1:
time: 419 us; the launch traced here: 418 us
  waiting for transfers between devices  144 us (34%)
  starting transfers between devices  130 us (31%)
  Pallas kernels  78 us (19%)
  local copies, waits for them, and re-layouts  18.9 us (5%)
  blocking collectives  16.3 us (4%)
  between operations  14.3 us (3%)
  loops' own time  10.7 us (3%)
    all_gather x1, waiting for transfers between devices, shards(): weights = lax.all_gather(both.reshape(2, H, 4 * units), 'col')  121 us
    ppermute x15, starting transfers between devices, passed_along(): return lax.ppermute(block, axis, route)  84 us
    pallas_call x15, Pallas kernels, stage(): pl.pallas_call(stage_kernel, out_shape=(low, low, high, high), in_specs=[...  78 us
    all_to_all x1, starting transfers between devices, shards(): lax.all_to_all(states[layers - 1:], 'layer', 0, 0, tiled=True)[layers - 1]  36.2 us
    all_to_all x1, blocking collectives, shards(): lax.all_to_all(sent, 'col', 0, 0, tiled=True).reshape(cols, 4, ROWS, units)  16.3 us
    all_to_all x1, waiting for transfers between devices, shards(): got = lax.all_to_all(sent, 'col', 0, 0, tiled=True)  12.6 us
    another operation x1, loops' own time, shards(): lax.scan(section, (zero_x, zero_s, zero_s), jnp.arange(stages))  10.7 us
    all_to_all x1, starting transfers between devices, shards(): got = lax.all_to_all(sent, 'col', 0, 0, tiled=True)  10.2 us
  transfers between devices with their start and end apart: 18, of which 18 were waited for; matrix products, arithmetic and copies ran while one was open for 4% of the time, Pallas kernels for 0%

profile of v1, /device:TPU:8, one launch (start us, length us, event | category | flops | bytes accessed | tf_op | source)
XLA Modules:
  0.0 418.0 jit_solution(6595753588960799398)
XLA Ops:
  15.4 10.2 %all-to-all-start = ((f32[32,1,2176]{2,1,0:T(1,128)}), f32[32,1,2176]{2,1,0:T(1,128)S(1)}, u32[]{:S(2)}, u32[]{:S(2)}) async-start(f32[32,1,2176]{2,1,0:T(1,128)} %copy.44), calls=%async_computation | async-start | bytes 557056 | tf_op jit(solution)/shard_map/all_to_all | solution.py:138
  25.5 12.6 %all-to-all-done = f32[32,1,2176]{2,1,0:T(1,128)S(1)} async-done(((f32[32,1,2176]{2,1,0:T(1,128)}), f32[32,1,2176]{2,1,0:T(1,128)S(1)}, u32[]{:S(2)}, u32[]{:S(2)}) %all-to-all-start) | async-done | bytes 278560 | tf_op jit(solution)/shard_map/all_to_all | solution.py:138
  39.5 121.1 %all-gather.2.cloned.1.call-done = bf16[32,2,1024,128]{3,2,1,0:T(8,128)(2,1)} async-done(((bf16[1,2,1024,128]{3,2,1,0:T(8,128)(2,1)}), bf16[32,2,1024,128]{3,2,1,0:T(8,128)(2,1)}) %all-gather.2.cloned.1.call-update) | async-done | bytes 16777232 | tf_op jit(solution)/shard_map/all_gather | solution.py:133
  160.6 184.0 %while.17 = (s32[]{:T(128)}, bf16[8,1024]{1,0:T(8,128)(2,1)S(1)}, f32[8,1024]{1,0:T(8,128)S(1)}, f32[8,1024]{1,0:T(8,128)S(1)}, bf16[15,8,1024]{2,1,0:T(8,128)(2...) while((s32[]{:T(128)}, bf16[8,1024]{1,0:T(8,128)(2,1)S(1)}, ...), condition=%wide.region_1.2_spmd, body=%wide.region_0.1_spmd.sunk | while | flops 17 | bytes 262433 | solution.py:155
  165.6 8.8 %eval_jaxpr.2 = (bf16[8,1024]{1,0:T(8,128)(2,1)S(1)}, bf16[8,1024]{1,0:T(8,128)(2,1)S(1)}, f32[8,1024]{1,0:T(8,128)S(1)}, f32[8,1024]{1,0:T(8,128)S(1)}) custom-call(s32[3]{0:T(128)S(1)} %add_convert_fusion.2.flags, bf16[8,1024]{1,0:T(8,128)(2,1)S(1)} %collective-permute-done.x_got, bf16[8,1024]{1,0:T(8,128)(2,1)S(1)} %dynamic-slice_bitcast_fusion.2.x_token, ...), custom_call_target="tpu_custom_call" | custom-call | tf_op jit(solution)/shard_map/while/body/eval_jaxpr/pallas_call | solution.py:106
  177.2 8.8 %eval_jaxpr.2 = (bf16[8,1024]{1,0:T(8,128)(2,1)S(1)}, bf16[8,1024]{1,0:T(8,128)(2,1)S(1)}, f32[8,1024]{1,0:T(8,128)S(1)}, f32[8,1024]{1,0:T(8,128)S(1)}) custom-call(s32[3]{0:T(128)S(1)} %add_convert_fusion.2.flags, bf16[8,1024]{1,0:T(8,128)(2,1)S(1)} %collective-permute-done.x_got, bf16[8,1024]{1,0:T(8,128)(2,1)S(1)} %dynamic-slice_bitcast_fusion.2.x_token, ...), custom_call_target="tpu_custom_call" | custom-call | tf_op jit(solution)/shard_map/while/body/eval_jaxpr/pallas_call | solution.py:106
  186.0 4.2 %collective-permute-start = (bf16[8,1024]{1,0:T(8,128)(2,1)S(1)}, bf16[8,1024]{1,0:T(8,128)(2,1)S(1)}, u32[]{:S(2)}, u32[]{:S(2)}) collective-permute-start(bf16[8,1024]{1,0:T(8,128)(2,1)S(1)} %get-tuple-element.242), channel_id=1, source_target_pairs={{0,32},{32,64},{64,96},{96,128},{128,160},{160,192},{192,224},{1,3... | collective-permute-start | bytes 49160 | tf_op jit(solution)/shard_map/while/body/eval_jaxpr/ppermute | solution.py:19
  191.6 8.8 %eval_jaxpr.2 = (bf16[8,1024]{1,0:T(8,128)(2,1)S(1)}, bf16[8,1024]{1,0:T(8,128)(2,1)S(1)}, f32[8,1024]{1,0:T(8,128)S(1)}, f32[8,1024]{1,0:T(8,128)S(1)}) custom-call(s32[3]{0:T(128)S(1)} %add_convert_fusion.2.flags, bf16[8,1024]{1,0:T(8,128)(2,1)S(1)} %collective-permute-done.x_got, bf16[8,1024]{1,0:T(8,128)(2,1)S(1)} %dynamic-slice_bitcast_fusion.2.x_token, ...), custom_call_target="tpu_custom_call" | custom-call | tf_op jit(solution)/shard_map/while/body/eval_jaxpr/pallas_call | solution.py:106
  200.4 4.2 %collective-permute-start = (bf16[8,1024]{1,0:T(8,128)(2,1)S(1)}, bf16[8,1024]{1,0:T(8,128)(2,1)S(1)}, u32[]{:S(2)}, u32[]{:S(2)}) collective-permute-start(bf16[8,1024]{1,0:T(8,128)(2,1)S(1)} %get-tuple-element.242), channel_id=1, source_target_pairs={{0,32},{32,64},{64,96},{96,128},{128,160},{160,192},{192,224},{1,3... | collective-permute-start | bytes 49160 | tf_op jit(solution)/shard_map/while/body/eval_jaxpr/ppermute | solution.py:19
  206.0 8.8 %eval_jaxpr.2 = (bf16[8,1024]{1,0:T(8,128)(2,1)S(1)}, bf16[8,1024]{1,0:T(8,128)(2,1)S(1)}, f32[8,1024]{1,0:T(8,128)S(1)}, f32[8,1024]{1,0:T(8,128)S(1)}) custom-call(s32[3]{0:T(128)S(1)} %add_convert_fusion.2.flags, bf16[8,1024]{1,0:T(8,128)(2,1)S(1)} %collective-permute-done.x_got, bf16[8,1024]{1,0:T(8,128)(2,1)S(1)} %dynamic-slice_bitcast_fusion.2.x_token, ...), custom_call_target="tpu_custom_call" | custom-call | tf_op jit(solution)/shard_map/while/body/eval_jaxpr/pallas_call | solution.py:106
  214.8 4.2 %collective-permute-start = (bf16[8,1024]{1,0:T(8,128)(2,1)S(1)}, bf16[8,1024]{1,0:T(8,128)(2,1)S(1)}, u32[]{:S(2)}, u32[]{:S(2)}) collective-permute-start(bf16[8,1024]{1,0:T(8,128)(2,1)S(1)} %get-tuple-element.242), channel_id=1, source_target_pairs={{0,32},{32,64},{64,96},{96,128},{128,160},{160,192},{192,224},{1,3... | collective-permute-start | bytes 49160 | tf_op jit(solution)/shard_map/while/body/eval_jaxpr/ppermute | solution.py:19
  220.5 8.8 %eval_jaxpr.2 = (bf16[8,1024]{1,0:T(8,128)(2,1)S(1)}, bf16[8,1024]{1,0:T(8,128)(2,1)S(1)}, f32[8,1024]{1,0:T(8,128)S(1)}, f32[8,1024]{1,0:T(8,128)S(1)}) custom-call(s32[3]{0:T(128)S(1)} %add_convert_fusion.2.flags, bf16[8,1024]{1,0:T(8,128)(2,1)S(1)} %collective-permute-done.x_got, bf16[8,1024]{1,0:T(8,128)(2,1)S(1)} %dynamic-slice_bitcast_fusion.2.x_token, ...), custom_call_target="tpu_custom_call" | custom-call | tf_op jit(solution)/shard_map/while/body/eval_jaxpr/pallas_call | solution.py:106
  229.3 4.2 %collective-permute-start = (bf16[8,1024]{1,0:T(8,128)(2,1)S(1)}, bf16[8,1024]{1,0:T(8,128)(2,1)S(1)}, u32[]{:S(2)}, u32[]{:S(2)}) collective-permute-start(bf16[8,1024]{1,0:T(8,128)(2,1)S(1)} %get-tuple-element.242), channel_id=1, source_target_pairs={{0,32},{32,64},{64,96},{96,128},{128,160},{160,192},{192,224},{1,3... | collective-permute-start | bytes 49160 | tf_op jit(solution)/shard_map/while/body/eval_jaxpr/ppermute | solution.py:19
  234.9 8.8 %eval_jaxpr.2 = (bf16[8,1024]{1,0:T(8,128)(2,1)S(1)}, bf16[8,1024]{1,0:T(8,128)(2,1)S(1)}, f32[8,1024]{1,0:T(8,128)S(1)}, f32[8,1024]{1,0:T(8,128)S(1)}) custom-call(s32[3]{0:T(128)S(1)} %add_convert_fusion.2.flags, bf16[8,1024]{1,0:T(8,128)(2,1)S(1)} %collective-permute-done.x_got, bf16[8,1024]{1,0:T(8,128)(2,1)S(1)} %dynamic-slice_bitcast_fusion.2.x_token, ...), custom_call_target="tpu_custom_call" | custom-call | tf_op jit(solution)/shard_map/while/body/eval_jaxpr/pallas_call | solution.py:106
  249.3 8.8 %eval_jaxpr.2 = (bf16[8,1024]{1,0:T(8,128)(2,1)S(1)}, bf16[8,1024]{1,0:T(8,128)(2,1)S(1)}, f32[8,1024]{1,0:T(8,128)S(1)}, f32[8,1024]{1,0:T(8,128)S(1)}) custom-call(s32[3]{0:T(128)S(1)} %add_convert_fusion.2.flags, bf16[8,1024]{1,0:T(8,128)(2,1)S(1)} %collective-permute-done.x_got, bf16[8,1024]{1,0:T(8,128)(2,1)S(1)} %dynamic-slice_bitcast_fusion.2.x_token, ...), custom_call_target="tpu_custom_call" | custom-call | tf_op jit(solution)/shard_map/while/body/eval_jaxpr/pallas_call | solution.py:106
  263.8 8.8 %eval_jaxpr.2 = (bf16[8,1024]{1,0:T(8,128)(2,1)S(1)}, bf16[8,1024]{1,0:T(8,128)(2,1)S(1)}, f32[8,1024]{1,0:T(8,128)S(1)}, f32[8,1024]{1,0:T(8,128)S(1)}) custom-call(s32[3]{0:T(128)S(1)} %add_convert_fusion.2.flags, bf16[8,1024]{1,0:T(8,128)(2,1)S(1)} %collective-permute-done.x_got, bf16[8,1024]{1,0:T(8,128)(2,1)S(1)} %dynamic-slice_bitcast_fusion.2.x_token, ...), custom_call_target="tpu_custom_call" | custom-call | tf_op jit(solution)/shard_map/while/body/eval_jaxpr/pallas_call | solution.py:106
  279.4 11.8 %collective-permute-start = (bf16[8,1024]{1,0:T(8,128)(2,1)S(1)}, bf16[8,1024]{1,0:T(8,128)(2,1)S(1)}, u32[]{:S(2)}, u32[]{:S(2)}) collective-permute-start(bf16[8,1024]{1,0:T(8,128)(2,1)S(1)} %get-tuple-element.242), channel_id=1, source_target_pairs={{0,32},{32,64},{64,96},{96,128},{128,160},{160,192},{192,224},{1,3... | collective-permute-start | bytes 49160 | tf_op jit(solution)/shard_map/while/body/eval_jaxpr/ppermute | solution.py:19
  300.6 9.8 %collective-permute-start = (bf16[8,1024]{1,0:T(8,128)(2,1)S(1)}, bf16[8,1024]{1,0:T(8,128)(2,1)S(1)}, u32[]{:S(2)}, u32[]{:S(2)}) collective-permute-start(bf16[8,1024]{1,0:T(8,128)(2,1)S(1)} %get-tuple-element.242), channel_id=1, source_target_pairs={{0,32},{32,64},{64,96},{96,128},{128,160},{160,192},{192,224},{1,3... | collective-permute-start | bytes 49160 | tf_op jit(solution)/shard_map/while/body/eval_jaxpr/ppermute | solution.py:19
  313.0 5.4 %collective-permute-start = (bf16[8,1024]{1,0:T(8,128)(2,1)S(1)}, bf16[8,1024]{1,0:T(8,128)(2,1)S(1)}, u32[]{:S(2)}, u32[]{:S(2)}) collective-permute-start(bf16[8,1024]{1,0:T(8,128)(2,1)S(1)} %get-tuple-element.242), channel_id=1, source_target_pairs={{0,32},{32,64},{64,96},{96,128},{128,160},{160,192},{192,224},{1,3... | collective-permute-start | bytes 49160 | tf_op jit(solution)/shard_map/while/body/eval_jaxpr/ppermute | solution.py:19
  321.0 13.0 %collective-permute-start = (bf16[8,1024]{1,0:T(8,128)(2,1)S(1)}, bf16[8,1024]{1,0:T(8,128)(2,1)S(1)}, u32[]{:S(2)}, u32[]{:S(2)}) collective-permute-start(bf16[8,1024]{1,0:T(8,128)(2,1)S(1)} %get-tuple-element.242), channel_id=1, source_target_pairs={{0,32},{32,64},{64,96},{96,128},{128,160},{160,192},{192,224},{1,3... | collective-permute-start | bytes 49160 | tf_op jit(solution)/shard_map/while/body/eval_jaxpr/ppermute | solution.py:19
  336.7 5.4 %collective-permute-start = (bf16[8,1024]{1,0:T(8,128)(2,1)S(1)}, bf16[8,1024]{1,0:T(8,128)(2,1)S(1)}, u32[]{:S(2)}, u32[]{:S(2)}) collective-permute-start(bf16[8,1024]{1,0:T(8,128)(2,1)S(1)} %get-tuple-element.242), channel_id=1, source_target_pairs={{0,32},{32,64},{64,96},{96,128},{128,160},{160,192},{192,224},{1,3... | collective-permute-start | bytes 49160 | tf_op jit(solution)/shard_map/while/body/eval_jaxpr/ppermute | solution.py:19
  345.3 36.2 %all-to-all-start.1 = ((bf16[8,8,1024]{2,1,0:T(8,128)(2,1)}), bf16[8,8,1024]{2,1,0:T(8,128)(2,1)S(1)}, u32[]{:S(2)}, u32[]{:S(2)}) async-start(bf16[8,8,1024]{2,1,0:T(8,128)(2,1)} %slice.37), calls=%async_computation.1 | async-start | bytes 262144 | tf_op jit(solution)/shard_map/all_to_all | solution.py:157
  381.5 9.1 %all-to-all-done.1 = bf16[8,8,1024]{2,1,0:T(8,128)(2,1)S(1)} async-done(((bf16[8,8,1024]{2,1,0:T(8,128)(2,1)}), bf16[8,8,1024]{2,1,0:T(8,128)(2,1)S(1)}, u32[]{:S(2)}, u32[]{:S(2)}) %all-to-all-start.1) | async-done | bytes 131104 | tf_op jit(solution)/shard_map/all_to_all | solution.py:157
  391.1 16.3 %all_to_all.22 = f32[32,1,512]{2,1,0:T(1,128)S(1)} all-to-all(f32[32,1,512]{2,1,0:T(1,128)S(1)} %reshape.95), channel_id=1, replica_groups=mesh['dp'=2,'layer'=8,'col'=32] {'col'}, dimensions={0} | all-to-all | bytes 131072 | tf_op jit(solution)/shard_map/all_to_all | solution.py:160
  (167 shorter events, 55.2 us)
Async XLA Ops:
  7.2 153.5 %all-gather.2.cloned.1.call-start = ((), (), s32[]{:S(2)}) async-start(), calls=%async_computation.3 | async-start | bytes 17301504 | tf_op jit(solution)/shard_map/all_gather | solution.py:133
  15.4 22.8 %all-to-all-start = ((f32[32,1,2176]{2,1,0:T(1,128)}), f32[32,1,2176]{2,1,0:T(1,128)S(1)}, u32[]{:S(2)}, u32[]{:S(2)}) async-start(f32[32,1,2176]{2,1,0:T(1,128)} %copy.44), calls=%async_computation | async-start | bytes 557056 | tf_op jit(solution)/shard_map/all_to_all | solution.py:138
  160.7 5.0 %collective-permute-start = (bf16[8,1024]{1,0:T(8,128)(2,1)S(1)}, bf16[8,1024]{1,0:T(8,128)(2,1)S(1)}, u32[]{:S(2)}, u32[]{:S(2)}) collective-permute-start(bf16[8,1024]{1,0:T(8,128)(2,1)S(1)} %get-tuple-element.242), channel_id=1, source_target_pairs={{0,32},{32,64},{64,96},{96,128},{128,160},{160,192},{192,224},{1,3... | collective-permute-start | bytes 49160 | tf_op jit(solution)/shard_map/while/body/eval_jaxpr/ppermute | solution.py:19
  174.4 2.7 collective-permute-start
  186.0 5.6 %collective-permute-start = (bf16[8,1024]{1,0:T(8,128)(2,1)S(1)}, bf16[8,1024]{1,0:T(8,128)(2,1)S(1)}, u32[]{:S(2)}, u32[]{:S(2)}) collective-permute-start(bf16[8,1024]{1,0:T(8,128)(2,1)S(1)} %get-tuple-element.242), channel_id=1, source_target_pairs={{0,32},{32,64},{64,96},{96,128},{128,160},{160,192},{192,224},{1,3... | collective-permute-start | bytes 49160 | tf_op jit(solution)/shard_map/while/body/eval_jaxpr/ppermute | solution.py:19
  200.4 5.6 %collective-permute-start = (bf16[8,1024]{1,0:T(8,128)(2,1)S(1)}, bf16[8,1024]{1,0:T(8,128)(2,1)S(1)}, u32[]{:S(2)}, u32[]{:S(2)}) collective-permute-start(bf16[8,1024]{1,0:T(8,128)(2,1)S(1)} %get-tuple-element.242), channel_id=1, source_target_pairs={{0,32},{32,64},{64,96},{96,128},{128,160},{160,192},{192,224},{1,3... | collective-permute-start | bytes 49160 | tf_op jit(solution)/shard_map/while/body/eval_jaxpr/ppermute | solution.py:19
  214.8 5.6 %collective-permute-start = (bf16[8,1024]{1,0:T(8,128)(2,1)S(1)}, bf16[8,1024]{1,0:T(8,128)(2,1)S(1)}, u32[]{:S(2)}, u32[]{:S(2)}) collective-permute-start(bf16[8,1024]{1,0:T(8,128)(2,1)S(1)} %get-tuple-element.242), channel_id=1, source_target_pairs={{0,32},{32,64},{64,96},{96,128},{128,160},{160,192},{192,224},{1,3... | collective-permute-start | bytes 49160 | tf_op jit(solution)/shard_map/while/body/eval_jaxpr/ppermute | solution.py:19
  229.3 5.6 %collective-permute-start = (bf16[8,1024]{1,0:T(8,128)(2,1)S(1)}, bf16[8,1024]{1,0:T(8,128)(2,1)S(1)}, u32[]{:S(2)}, u32[]{:S(2)}) collective-permute-start(bf16[8,1024]{1,0:T(8,128)(2,1)S(1)} %get-tuple-element.242), channel_id=1, source_target_pairs={{0,32},{32,64},{64,96},{96,128},{128,160},{160,192},{192,224},{1,3... | collective-permute-start | bytes 49160 | tf_op jit(solution)/shard_map/while/body/eval_jaxpr/ppermute | solution.py:19
  243.7 5.6 %collective-permute-start = (bf16[8,1024]{1,0:T(8,128)(2,1)S(1)}, bf16[8,1024]{1,0:T(8,128)(2,1)S(1)}, u32[]{:S(2)}, u32[]{:S(2)}) collective-permute-start(bf16[8,1024]{1,0:T(8,128)(2,1)S(1)} %get-tuple-element.242), channel_id=1, source_target_pairs={{0,32},{32,64},{64,96},{96,128},{128,160},{160,192},{192,224},{1,3... | collective-permute-start | bytes 49160 | tf_op jit(solution)/shard_map/while/body/eval_jaxpr/ppermute | solution.py:19
  258.1 5.6 %collective-permute-start = (bf16[8,1024]{1,0:T(8,128)(2,1)S(1)}, bf16[8,1024]{1,0:T(8,128)(2,1)S(1)}, u32[]{:S(2)}, u32[]{:S(2)}) collective-permute-start(bf16[8,1024]{1,0:T(8,128)(2,1)S(1)} %get-tuple-element.242), channel_id=1, source_target_pairs={{0,32},{32,64},{64,96},{96,128},{128,160},{160,192},{192,224},{1,3... | collective-permute-start | bytes 49160 | tf_op jit(solution)/shard_map/while/body/eval_jaxpr/ppermute | solution.py:19
  272.6 5.6 %collective-permute-start = (bf16[8,1024]{1,0:T(8,128)(2,1)S(1)}, bf16[8,1024]{1,0:T(8,128)(2,1)S(1)}, u32[]{:S(2)}, u32[]{:S(2)}) collective-permute-start(bf16[8,1024]{1,0:T(8,128)(2,1)S(1)} %get-tuple-element.242), channel_id=1, source_target_pairs={{0,32},{32,64},{64,96},{96,128},{128,160},{160,192},{192,224},{1,3... | collective-permute-start | bytes 49160 | tf_op jit(solution)/shard_map/while/body/eval_jaxpr/ppermute | solution.py:19
  279.4 13.3 %collective-permute-start = (bf16[8,1024]{1,0:T(8,128)(2,1)S(1)}, bf16[8,1024]{1,0:T(8,128)(2,1)S(1)}, u32[]{:S(2)}, u32[]{:S(2)}) collective-permute-start(bf16[8,1024]{1,0:T(8,128)(2,1)S(1)} %get-tuple-element.242), channel_id=1, source_target_pairs={{0,32},{32,64},{64,96},{96,128},{128,160},{160,192},{192,224},{1,3... | collective-permute-start | bytes 49160 | tf_op jit(solution)/shard_map/while/body/eval_jaxpr/ppermute | solution.py:19
  293.8 5.6 %collective-permute-start = (bf16[8,1024]{1,0:T(8,128)(2,1)S(1)}, bf16[8,1024]{1,0:T(8,128)(2,1)S(1)}, u32[]{:S(2)}, u32[]{:S(2)}) collective-permute-start(bf16[8,1024]{1,0:T(8,128)(2,1)S(1)} %get-tuple-element.242), channel_id=1, source_target_pairs={{0,32},{32,64},{64,96},{96,128},{128,160},{160,192},{192,224},{1,3... | collective-permute-start | bytes 49160 | tf_op jit(solution)/shard_map/while/body/eval_jaxpr/ppermute | solution.py:19
  300.6 11.3 %collective-permute-start = (bf16[8,1024]{1,0:T(8,128)(2,1)S(1)}, bf16[8,1024]{1,0:T(8,128)(2,1)S(1)}, u32[]{:S(2)}, u32[]{:S(2)}) collective-permute-start(bf16[8,1024]{1,0:T(8,128)(2,1)S(1)} %get-tuple-element.242), channel_id=1, source_target_pairs={{0,32},{32,64},{64,96},{96,128},{128,160},{160,192},{192,224},{1,3... | collective-permute-start | bytes 49160 | tf_op jit(solution)/shard_map/while/body/eval_jaxpr/ppermute | solution.py:19
  313.0 6.8 %collective-permute-start = (bf16[8,1024]{1,0:T(8,128)(2,1)S(1)}, bf16[8,1024]{1,0:T(8,128)(2,1)S(1)}, u32[]{:S(2)}, u32[]{:S(2)}) collective-permute-start(bf16[8,1024]{1,0:T(8,128)(2,1)S(1)} %get-tuple-element.242), channel_id=1, source_target_pairs={{0,32},{32,64},{64,96},{96,128},{128,160},{160,192},{192,224},{1,3... | collective-permute-start | bytes 49160 | tf_op jit(solution)/shard_map/while/body/eval_jaxpr/ppermute | solution.py:19
  321.0 14.5 %collective-permute-start = (bf16[8,1024]{1,0:T(8,128)(2,1)S(1)}, bf16[8,1024]{1,0:T(8,128)(2,1)S(1)}, u32[]{:S(2)}, u32[]{:S(2)}) collective-permute-start(bf16[8,1024]{1,0:T(8,128)(2,1)S(1)} %get-tuple-element.242), channel_id=1, source_target_pairs={{0,32},{32,64},{64,96},{96,128},{128,160},{160,192},{192,224},{1,3... | collective-permute-start | bytes 49160 | tf_op jit(solution)/shard_map/while/body/eval_jaxpr/ppermute | solution.py:19
  336.7 6.8 %collective-permute-start = (bf16[8,1024]{1,0:T(8,128)(2,1)S(1)}, bf16[8,1024]{1,0:T(8,128)(2,1)S(1)}, u32[]{:S(2)}, u32[]{:S(2)}) collective-permute-start(bf16[8,1024]{1,0:T(8,128)(2,1)S(1)} %get-tuple-element.242), channel_id=1, source_target_pairs={{0,32},{32,64},{64,96},{96,128},{128,160},{160,192},{192,224},{1,3... | collective-permute-start | bytes 49160 | tf_op jit(solution)/shard_map/while/body/eval_jaxpr/ppermute | solution.py:19
  345.3 45.3 %all-to-all-start.1 = ((bf16[8,8,1024]{2,1,0:T(8,128)(2,1)}), bf16[8,8,1024]{2,1,0:T(8,128)(2,1)S(1)}, u32[]{:S(2)}, u32[]{:S(2)}) async-start(bf16[8,8,1024]{2,1,0:T(8,128)(2,1)} %slice.37), calls=%async_computation.1 | async-start | bytes 262144 | tf_op jit(solution)/shard_map/all_to_all | solution.py:157
Sparse Core Ops, SparseCore 0:
  11.1 149.4 all-gather.1

commit v2 on v1

v2 whole, which is shorter than its diff:
```python
import jax
import jax.numpy as jnp
from jax import lax
from jax.experimental import pallas as pl
from jax.experimental.pallas import tpu as pltpu
from jax.sharding import PartitionSpec as P

H = 1024
ROWS = 4
STEPS = 2
LANES = 128
WIDE = 512
BLOCKS = 4 * H // WIDE


def passed_along(block, axis, distance):
    devices = range(lax.axis_size(axis))
    route = [(i - distance, i) for i in devices if i - distance in devices]
    return lax.ppermute(block, axis, route)


def segments_swapped(quad, lane):
    gates = []
    for k in range(4):
        out = None
        for j in range(4):
            shift = (32 * (j - k)) % LANES
            moved = quad[j] if shift == 0 else pltpu.roll(quad[j], shift, 1)
            out = moved if out is None else jnp.where(lane >= 32 * j, moved, out)
        gates.append(out)
    return gates


def stage_kernel(place, x_got, x_tokens, h_was, c_was, top_was, bias, weights, place_out, x_out, h_out, c_out, top_out, gx, close, sems):
    chunk = place[0]
    level = place[1]
    chunks = x_tokens.shape[0]
    active = (chunk >= 0) & (chunk < chunks)
    place_out[0] = chunk + 1
    place_out[1] = level
    top_out[...] = top_was[...]

    def copy(m, p):
        lanes = pl.ds(LANES * p, LANES)
        return pltpu.make_async_copy(weights.at[p, m], close.at[m, :, lanes], sems.at[m, p])

    def columns(m, q, fresh):
        if fresh:
            for j in range(4):
                copy(m, 4 * q + j).wait()
        return close[m, :, WIDE * q : WIDE * (q + 1)]

    @pl.when(active)
    def _():
        for m in range(2):
            for p in range(H // 32):
                copy(m, p).start()
        x = jnp.where(level == 0, x_tokens[chunk].astype(jnp.float32), x_got[...].astype(jnp.float32))
        x_low = x.astype(jnp.bfloat16)
        lane = lax.broadcasted_iota(jnp.int32, (2 * ROWS, LANES), 1)
        row = lax.broadcasted_iota(jnp.int32, (2 * ROWS, H), 0)
        update = (lane >= 64) & (lane < 96)
        scale = jnp.where(update, 1.0, 0.5)
        shift = jnp.where(update, 0.0, 0.5)
        for q in range(BLOCKS):
            part = jnp.dot(x_low, columns(0, q, True), preferred_element_type=jnp.float32)
            for j in range(4):
                lanes = slice(WIDE * q + LANES * j, WIDE * q + LANES * (j + 1))
                gx[:, lanes] = (part[:, LANES * j : LANES * (j + 1)] + bias[:, lanes]) * scale
        hidden = h_was[...]
        states = []
        for step in range(STEPS):
            h_low = hidden.astype(jnp.bfloat16)
            pieces = []
            for q in range(BLOCKS):
                gates = jnp.dot(h_low, columns(1, q, step == 0), preferred_element_type=jnp.float32)
                quad = []
                for j in range(4):
                    lanes = slice(WIDE * q + LANES * j, WIDE * q + LANES * (j + 1))
                    z = gates[:, LANES * j : LANES * (j + 1)] * scale + gx[:, lanes]
                    quad.append(jnp.tanh(z) * scale + shift)
                g_in, g_forget, g_update, g_out = segments_swapped(quad, lane)
                here = slice(LANES * q, LANES * (q + 1))
                cell = c_was[:, here] if step == 0 else c_out[:, here]
                cell = g_forget * cell + g_in * g_update
                c_out[:, here] = pltpu.roll(cell, ROWS, 0)
                pieces.append((g_out * jnp.tanh(cell)).astype(jnp.bfloat16).astype(jnp.float32))
            fresh = jnp.concatenate(pieces, axis=1)
            states.append(fresh)
            hidden = pltpu.roll(fresh, ROWS, 0)
        h_out[...] = hidden
        both = jnp.where(row < ROWS, states[0], states[1])
        top_out[chunk] = both.astype(jnp.bfloat16)
        x_out[...] = jnp.where(level >= 1, both + x, both).astype(jnp.bfloat16)

    @pl.when(jnp.logical_not(active))
    def _():
        h_out[...] = h_was[...]
        c_out[...] = c_was[...]
        x_out[...] = x_got[...]


def stage(place, x_got, x_tokens, h_was, c_was, top_was, bias, weights):
    full = pl.BlockSpec(memory_space=pltpu.VMEM)
    scalars = pl.BlockSpec(memory_space=pltpu.SMEM)

    def like(x):
        return jax.ShapeDtypeStruct(x.shape, x.dtype)

    return pl.pallas_call(
        stage_kernel,
        out_shape=(like(place), like(x_got), like(h_was), like(c_was), like(top_was)),
        in_specs=[scalars, full, full, full, full, full, full, pl.BlockSpec(memory_space=pltpu.HBM)],
        out_specs=(scalars, full, full, full, full),
        input_output_aliases={0: 0, 3: 2, 4: 3, 5: 4},
        scratch_shapes=[
            pltpu.VMEM((2 * ROWS, 4 * H), jnp.float32),
            pltpu.VMEM((2, H, 4 * H), jnp.bfloat16),
            pltpu.SemaphoreType.DMA((2, H // 32)),
        ],
        compiler_params=pltpu.CompilerParams(vmem_limit_bytes=24 * 1024 * 1024),
    )(place, x_got, x_tokens, h_was, c_was, top_was, bias, weights)


def shards(tokens, w_input, w_recur, bias):
    steps_count, sentences, units = tokens.shape
    layers = lax.axis_size("layer")
    cols = lax.axis_size("col")
    level = lax.axis_index("layer")
    chunks = steps_count // STEPS
    stages = chunks + layers - 1

    at = jnp.arange(4 * units)
    order = (at[:, None] == 4 * (at % units) + at // units).astype(jnp.bfloat16)
    half = jnp.where(lax.axis_index("dp") == 0, w_input[0], w_recur[0])
    half = jnp.dot(half, order, preferred_element_type=jnp.float32).astype(jnp.bfloat16)
    weights = lax.all_gather(half, ("col", "dp")).reshape(cols, 2, H, 4 * units)

    local_bias = bias[0].reshape(units, 4).T.reshape(1, 4 * units)
    mine = tokens.reshape(steps_count, cols, ROWS, units).transpose(1, 0, 2, 3).astype(jnp.float32)
    sent = jnp.concatenate([mine.reshape(cols, -1), jnp.broadcast_to(local_bias, (cols, 4 * units))], axis=1)
    got = lax.all_to_all(sent, "col", 0, 0, tiled=True)
    x_first = got[:, : steps_count * ROWS * units].reshape(cols, steps_count * ROWS, units).transpose(1, 0, 2)
    x_first = x_first.reshape(chunks, STEPS * ROWS, H).astype(jnp.bfloat16)
    bias_full = got[:, steps_count * ROWS * units :].reshape(1, 4 * H)

    def section(_, carry):
        place, x_sent, hidden, cell, top = carry
        x_got = passed_along(x_sent, "layer", 1)
        return tuple(stage(place, x_got, x_first, hidden, cell, top, bias_full, weights))

    place = jnp.stack([-level, level])
    zero_x = jnp.zeros((STEPS * ROWS, H), jnp.bfloat16)
    zero_s = jnp.zeros((STEPS * ROWS, H), jnp.float32)
    zero_t = jnp.zeros((chunks, STEPS * ROWS, H), jnp.bfloat16)
    _, _, hidden, cell, top = lax.fori_loop(0, stages, section, (place, zero_x, zero_s, zero_s, zero_t))

    top = lax.all_to_all(top, "layer", 0, 0, tiled=True)[layers - 1]
    rows = jnp.concatenate([top.astype(jnp.float32), hidden[:ROWS], cell[:ROWS]], axis=0)
    sent = rows.reshape(4 * ROWS, cols, units).transpose(1, 0, 2)
    got = lax.all_to_all(sent, "col", 0, 0, tiled=True).reshape(cols, 4, ROWS, units).transpose(1, 0, 2, 3)
    got = got.reshape(4, sentences, units)
    return got[:2].astype(jnp.bfloat16), got[2:3].astype(jnp.bfloat16), got[3:]


def solution(mesh):
    in_specs = (
        P(None, "dp", "col"),
        P("layer", None, "col"),
        P("layer", None, "col"),
        P("layer", "col"),
    )
    out_specs = (P("layer", "dp", "col"), P("layer", "dp", "col"), P("layer", "dp", "col"))
    return jax.shard_map(shards, mesh=mesh, in_specs=in_specs, out_specs=out_specs, check_vma=False)
```

time: 419 us -> 393 us (0.938)
  waiting for transfers between devices: 144 us -> 123 us
  Pallas kernels: 78 us -> 93.5 us
  loops' own time: 10.7 us -> 0.45 us
  local copies, waits for them, and re-layouts: 18.9 us -> 9.75 us
    all_gather x1, waiting for transfers between devices: 121 us -> 80.1 us  [shards(): weights = lax.all_gather(half, ('col', 'dp')).reshape(cols, 2, H, 4 * units)]
    ppermute x15, waiting for transfers between devices: 1.04 us -> 21.4 us  [passed_along(): return lax.ppermute(block, axis, route)]
    pallas_call x15, Pallas kernels: 78 us -> 93.5 us  [stage(): pl.pallas_call(stage_kernel, out_shape=(like(place), like(x_got), like(h_...]
    another operation x1, loops' own time: 10.7 us -> 0.45 us  [shards(): lax.fori_loop(0, stages, section, (place, zero_x, zero_s, zero_s, zero_t))]
    dynamic_slice x15 -> x0, local copies, waits for them, and re-layouts: 8.83 us -> none  [shards(): lax.scan(section, (zero_x, zero_s, zero_s), jnp.arange(stages))]
  transfers between devices with their start and end apart: 18 -> 18, of which waited for: 18 -> 18; matrix products, arithmetic and copies ran while one was open for 4% -> 2% of each run, Pallas kernels for 0% -> 0%
where the time goes in v2:
time: 393 us; the launch traced here: 392 us
  starting transfers between devices  130 us (33%)
  waiting for transfers between devices  123 us (31%)
  Pallas kernels  93.5 us (24%)
  blocking collectives  16.3 us (4%)
  between operations  14.2 us (4%)
  local copies, waits for them, and re-layouts  9.75 us (2%)
    pallas_call x15, Pallas kernels, stage(): pl.pallas_call(stage_kernel, out_shape=(like(place), like(x_got), like(h_...  93.5 us
    ppermute x15, starting transfers between devices, passed_along(): return lax.ppermute(block, axis, route)  83.9 us
    all_gather x1, waiting for transfers between devices, shards(): weights = lax.all_gather(half, ('col', 'dp')).reshape(cols, 2, H, 4 * units)  80.1 us
    all_to_all x1, starting transfers between devices, shards(): top = lax.all_to_all(top, 'layer', 0, 0, tiled=True)[layers - 1]  36.2 us
    ppermute x15, waiting for transfers between devices, passed_along(): return lax.ppermute(block, axis, route)  21.4 us
    all_to_all x1, blocking collectives, shards(): lax.all_to_all(sent, 'col', 0, 0, tiled=True).reshape(cols, 4, ROWS, units)  16.3 us
    all_to_all x1, waiting for transfers between devices, shards(): got = lax.all_to_all(sent, 'col', 0, 0, tiled=True)  12.5 us
    all_to_all x1, starting transfers between devices, shards(): got = lax.all_to_all(sent, 'col', 0, 0, tiled=True)  10.2 us
  transfers between devices with their start and end apart: 18, of which 18 were waited for; matrix products, arithmetic and copies ran while one was open for 2% of the time, Pallas kernels for 0%

profile of v2, /device:TPU:8, one launch (start us, length us, event | category | flops | bytes accessed | tf_op | source)
XLA Modules:
  0.0 392.0 jit_solution(12951006703423087943)
XLA Ops:
  15.1 10.2 %all-to-all-start = ((f32[32,1,2176]{2,1,0:T(1,128)}), f32[32,1,2176]{2,1,0:T(1,128)S(1)}, u32[]{:S(2)}, u32[]{:S(2)}) async-start(f32[32,1,2176]{2,1,0:T(1,128)} %copy.48), calls=%async_computation | async-start | bytes 557056 | tf_op jit(solution)/shard_map/all_to_all | solution.py:142
  25.4 12.5 %all-to-all-done = f32[32,1,2176]{2,1,0:T(1,128)S(1)} async-done(((f32[32,1,2176]{2,1,0:T(1,128)}), f32[32,1,2176]{2,1,0:T(1,128)S(1)}, u32[]{:S(2)}, u32[]{:S(2)}) %all-to-all-start) | async-done | bytes 278560 | tf_op jit(solution)/shard_map/all_to_all | solution.py:142
  39.2 80.1 %all-gather.3.cloned.1.call-done = bf16[65536,128]{1,0:T(8,128)(2,1)} async-done(((bf16[1024,128]{1,0:T(8,128)(2,1)}), bf16[65536,128]{1,0:T(8,128)(2,1)}) %all-gather.3.cloned.1.call-update) | async-done | bytes 16777232 | tf_op jit(solution)/shard_map/all_gather | solution.py:137
  120.0 199.3 %while.18 = (s32[]{:T(128)}, s32[2]{0:T(128)S(1)}, bf16[8,1024]{1,0:T(8,128)(2,1)S(1)}, f32[8,1024]{1,0:T(8,128)S(1)}, f32[8,1024]{1,0:T(8,128)S(1)}, /*index=5*...) while((s32[]{:T(128)}, s32[2]{0:T(128)S(1)}, ...), condition=%wide.region_1.2_spmd, body=%wide.region_0.1_spmd.sunk | while | flops 2 | bytes 65677 | solution.py:156
  125.0 9.8 %eval_jaxpr.1 = (s32[2]{0:T(128)S(1)}, bf16[8,1024]{1,0:T(8,128)(2,1)S(1)}, f32[8,1024]{1,0:T(8,128)S(1)}, f32[8,1024]{1,0:T(8,128)S(1)}, bf16[8,8,1024]{2,1,0:T(8,128)(2,1)}) custom-call(s32[2]{0:T(128)S(1)} %get-tuple-element.166.place, ...), custom_call_target="tpu_custom_call", output_to_operand_aliasing={{0}: (0, {}), {2}: (3, {}), {3}: (4, {}), {4}: (5, {})} | custom-call | tf_op jit(solution)/shard_map/while/body/eval_jaxpr/pallas_call | solution.py:110
  137.5 9.8 %eval_jaxpr.1 = (s32[2]{0:T(128)S(1)}, bf16[8,1024]{1,0:T(8,128)(2,1)S(1)}, f32[8,1024]{1,0:T(8,128)S(1)}, f32[8,1024]{1,0:T(8,128)S(1)}, bf16[8,8,1024]{2,1,0:T(8,128)(2,1)}) custom-call(s32[2]{0:T(128)S(1)} %get-tuple-element.166.place, ...), custom_call_target="tpu_custom_call", output_to_operand_aliasing={{0}: (0, {}), {2}: (3, {}), {3}: (4, {}), {4}: (5, {})} | custom-call | tf_op jit(solution)/shard_map/while/body/eval_jaxpr/pallas_call | solution.py:110
  147.3 4.2 %collective-permute-start = (bf16[8,1024]{1,0:T(8,128)(2,1)S(1)}, bf16[8,1024]{1,0:T(8,128)(2,1)S(1)}, u32[]{:S(2)}, u32[]{:S(2)}) collective-permute-start(bf16[8,1024]{1,0:T(8,128)(2,1)S(1)} %get-tuple-element.167), channel_id=1, source_target_pairs={{0,32},{32,64},{64,96},{96,128},{128,160},{160,192},{192,224},{1,3... | collective-permute-start | bytes 49160 | tf_op jit(solution)/shard_map/while/body/eval_jaxpr/ppermute | solution.py:19
  153.0 9.8 %eval_jaxpr.1 = (s32[2]{0:T(128)S(1)}, bf16[8,1024]{1,0:T(8,128)(2,1)S(1)}, f32[8,1024]{1,0:T(8,128)S(1)}, f32[8,1024]{1,0:T(8,128)S(1)}, bf16[8,8,1024]{2,1,0:T(8,128)(2,1)}) custom-call(s32[2]{0:T(128)S(1)} %get-tuple-element.166.place, ...), custom_call_target="tpu_custom_call", output_to_operand_aliasing={{0}: (0, {}), {2}: (3, {}), {3}: (4, {}), {4}: (5, {})} | custom-call | tf_op jit(solution)/shard_map/while/body/eval_jaxpr/pallas_call | solution.py:110
  162.8 4.2 %collective-permute-start = (bf16[8,1024]{1,0:T(8,128)(2,1)S(1)}, bf16[8,1024]{1,0:T(8,128)(2,1)S(1)}, u32[]{:S(2)}, u32[]{:S(2)}) collective-permute-start(bf16[8,1024]{1,0:T(8,128)(2,1)S(1)} %get-tuple-element.167), channel_id=1, source_target_pairs={{0,32},{32,64},{64,96},{96,128},{128,160},{160,192},{192,224},{1,3... | collective-permute-start | bytes 49160 | tf_op jit(solution)/shard_map/while/body/eval_jaxpr/ppermute | solution.py:19
  168.4 9.8 %eval_jaxpr.1 = (s32[2]{0:T(128)S(1)}, bf16[8,1024]{1,0:T(8,128)(2,1)S(1)}, f32[8,1024]{1,0:T(8,128)S(1)}, f32[8,1024]{1,0:T(8,128)S(1)}, bf16[8,8,1024]{2,1,0:T(8,128)(2,1)}) custom-call(s32[2]{0:T(128)S(1)} %get-tuple-element.166.place, ...), custom_call_target="tpu_custom_call", output_to_operand_aliasing={{0}: (0, {}), {2}: (3, {}), {3}: (4, {}), {4}: (5, {})} | custom-call | tf_op jit(solution)/shard_map/while/body/eval_jaxpr/pallas_call | solution.py:110
  178.3 4.2 %collective-permute-start = (bf16[8,1024]{1,0:T(8,128)(2,1)S(1)}, bf16[8,1024]{1,0:T(8,128)(2,1)S(1)}, u32[]{:S(2)}, u32[]{:S(2)}) collective-permute-start(bf16[8,1024]{1,0:T(8,128)(2,1)S(1)} %get-tuple-element.167), channel_id=1, source_target_pairs={{0,32},{32,64},{64,96},{96,128},{128,160},{160,192},{192,224},{1,3... | collective-permute-start | bytes 49160 | tf_op jit(solution)/shard_map/while/body/eval_jaxpr/ppermute | solution.py:19
  183.9 9.8 %eval_jaxpr.1 = (s32[2]{0:T(128)S(1)}, bf16[8,1024]{1,0:T(8,128)(2,1)S(1)}, f32[8,1024]{1,0:T(8,128)S(1)}, f32[8,1024]{1,0:T(8,128)S(1)}, bf16[8,8,1024]{2,1,0:T(8,128)(2,1)}) custom-call(s32[2]{0:T(128)S(1)} %get-tuple-element.166.place, ...), custom_call_target="tpu_custom_call", output_to_operand_aliasing={{0}: (0, {}), {2}: (3, {}), {3}: (4, {}), {4}: (5, {})} | custom-call | tf_op jit(solution)/shard_map/while/body/eval_jaxpr/pallas_call | solution.py:110
  193.7 4.2 %collective-permute-start = (bf16[8,1024]{1,0:T(8,128)(2,1)S(1)}, bf16[8,1024]{1,0:T(8,128)(2,1)S(1)}, u32[]{:S(2)}, u32[]{:S(2)}) collective-permute-start(bf16[8,1024]{1,0:T(8,128)(2,1)S(1)} %get-tuple-element.167), channel_id=1, source_target_pairs={{0,32},{32,64},{64,96},{96,128},{128,160},{160,192},{192,224},{1,3... | collective-permute-start | bytes 49160 | tf_op jit(solution)/shard_map/while/body/eval_jaxpr/ppermute | solution.py:19
  199.3 9.8 %eval_jaxpr.1 = (s32[2]{0:T(128)S(1)}, bf16[8,1024]{1,0:T(8,128)(2,1)S(1)}, f32[8,1024]{1,0:T(8,128)S(1)}, f32[8,1024]{1,0:T(8,128)S(1)}, bf16[8,8,1024]{2,1,0:T(8,128)(2,1)}) custom-call(s32[2]{0:T(128)S(1)} %get-tuple-element.166.place, ...), custom_call_target="tpu_custom_call", output_to_operand_aliasing={{0}: (0, {}), {2}: (3, {}), {3}: (4, {}), {4}: (5, {})} | custom-call | tf_op jit(solution)/shard_map/while/body/eval_jaxpr/pallas_call | solution.py:110
  214.8 9.8 %eval_jaxpr.1 = (s32[2]{0:T(128)S(1)}, bf16[8,1024]{1,0:T(8,128)(2,1)S(1)}, f32[8,1024]{1,0:T(8,128)S(1)}, f32[8,1024]{1,0:T(8,128)S(1)}, bf16[8,8,1024]{2,1,0:T(8,128)(2,1)}) custom-call(s32[2]{0:T(128)S(1)} %get-tuple-element.166.place, ...), custom_call_target="tpu_custom_call", output_to_operand_aliasing={{0}: (0, {}), {2}: (3, {}), {3}: (4, {}), {4}: (5, {})} | custom-call | tf_op jit(solution)/shard_map/while/body/eval_jaxpr/pallas_call | solution.py:110
  230.2 9.8 %eval_jaxpr.1 = (s32[2]{0:T(128)S(1)}, bf16[8,1024]{1,0:T(8,128)(2,1)S(1)}, f32[8,1024]{1,0:T(8,128)S(1)}, f32[8,1024]{1,0:T(8,128)S(1)}, bf16[8,8,1024]{2,1,0:T(8,128)(2,1)}) custom-call(s32[2]{0:T(128)S(1)} %get-tuple-element.166.place, ...), custom_call_target="tpu_custom_call", output_to_operand_aliasing={{0}: (0, {}), {2}: (3, {}), {3}: (4, {}), {4}: (5, {})} | custom-call | tf_op jit(solution)/shard_map/while/body/eval_jaxpr/pallas_call | solution.py:110
  247.9 11.8 %collective-permute-start = (bf16[8,1024]{1,0:T(8,128)(2,1)S(1)}, bf16[8,1024]{1,0:T(8,128)(2,1)S(1)}, u32[]{:S(2)}, u32[]{:S(2)}) collective-permute-start(bf16[8,1024]{1,0:T(8,128)(2,1)S(1)} %get-tuple-element.167), channel_id=1, source_target_pairs={{0,32},{32,64},{64,96},{96,128},{128,160},{160,192},{192,224},{1,3... | collective-permute-start | bytes 49160 | tf_op jit(solution)/shard_map/while/body/eval_jaxpr/ppermute | solution.py:19
  271.2 9.8 %collective-permute-start = (bf16[8,1024]{1,0:T(8,128)(2,1)S(1)}, bf16[8,1024]{1,0:T(8,128)(2,1)S(1)}, u32[]{:S(2)}, u32[]{:S(2)}) collective-permute-start(bf16[8,1024]{1,0:T(8,128)(2,1)S(1)} %get-tuple-element.167), channel_id=1, source_target_pairs={{0,32},{32,64},{64,96},{96,128},{128,160},{160,192},{192,224},{1,3... | collective-permute-start | bytes 49160 | tf_op jit(solution)/shard_map/while/body/eval_jaxpr/ppermute | solution.py:19
  284.6 5.4 %collective-permute-start = (bf16[8,1024]{1,0:T(8,128)(2,1)S(1)}, bf16[8,1024]{1,0:T(8,128)(2,1)S(1)}, u32[]{:S(2)}, u32[]{:S(2)}) collective-permute-start(bf16[8,1024]{1,0:T(8,128)(2,1)S(1)} %get-tuple-element.167), channel_id=1, source_target_pairs={{0,32},{32,64},{64,96},{96,128},{128,160},{160,192},{192,224},{1,3... | collective-permute-start | bytes 49160 | tf_op jit(solution)/shard_map/while/body/eval_jaxpr/ppermute | solution.py:19
  293.6 13.0 %collective-permute-start = (bf16[8,1024]{1,0:T(8,128)(2,1)S(1)}, bf16[8,1024]{1,0:T(8,128)(2,1)S(1)}, u32[]{:S(2)}, u32[]{:S(2)}) collective-permute-start(bf16[8,1024]{1,0:T(8,128)(2,1)S(1)} %get-tuple-element.167), channel_id=1, source_target_pairs={{0,32},{32,64},{64,96},{96,128},{128,160},{160,192},{192,224},{1,3... | collective-permute-start | bytes 49160 | tf_op jit(solution)/shard_map/while/body/eval_jaxpr/ppermute | solution.py:19
  310.3 5.4 %collective-permute-start = (bf16[8,1024]{1,0:T(8,128)(2,1)S(1)}, bf16[8,1024]{1,0:T(8,128)(2,1)S(1)}, u32[]{:S(2)}, u32[]{:S(2)}) collective-permute-start(bf16[8,1024]{1,0:T(8,128)(2,1)S(1)} %get-tuple-element.167), channel_id=1, source_target_pairs={{0,32},{32,64},{64,96},{96,128},{128,160},{160,192},{192,224},{1,3... | collective-permute-start | bytes 49160 | tf_op jit(solution)/shard_map/while/body/eval_jaxpr/ppermute | solution.py:19
  319.3 36.2 %all-to-all-start.1 = ((bf16[8,8,1024]{2,1,0:T(8,128)(2,1)}), bf16[8,8,1024]{2,1,0:T(8,128)(2,1)S(1)}, u32[]{:S(2)}, u32[]{:S(2)}) async-start(bf16[8,8,1024]{2,1,0:T(8,128)(2,1)} %get-tuple-element.57), calls=%async_computation.1 | async-start | bytes 262144 | tf_op jit(solution)/shard_map/all_to_all | solution.py:158
  355.5 9.1 %all-to-all-done.1 = bf16[8,8,1024]{2,1,0:T(8,128)(2,1)S(1)} async-done(((bf16[8,8,1024]{2,1,0:T(8,128)(2,1)}), bf16[8,8,1024]{2,1,0:T(8,128)(2,1)S(1)}, u32[]{:S(2)}, u32[]{:S(2)}) %all-to-all-start.1) | async-done | bytes 131104 | tf_op jit(solution)/shard_map/all_to_all | solution.py:158
  365.0 16.3 %all_to_all.22 = f32[32,1,512]{2,1,0:T(1,128)S(1)} all-to-all(f32[32,1,512]{2,1,0:T(1,128)S(1)} %reshape.103), channel_id=1, replica_groups=mesh['dp'=2,'layer'=8,'col'=32] {'col'}, dimensions={0} | all-to-all | bytes 131072 | tf_op jit(solution)/shard_map/all_to_all | solution.py:161
  (76 shorter events, 72.2 us)
Async XLA Ops:
  7.2 112.2 %all-gather.3.cloned.1.call-start = ((), (), s32[]{:S(2)}) async-start(), calls=%async_computation.3 | async-start | bytes 17039360 | tf_op jit(solution)/shard_map/all_gather | solution.py:137
  15.1 22.8 %all-to-all-start = ((f32[32,1,2176]{2,1,0:T(1,128)}), f32[32,1,2176]{2,1,0:T(1,128)S(1)}, u32[]{:S(2)}, u32[]{:S(2)}) async-start(f32[32,1,2176]{2,1,0:T(1,128)} %copy.48), calls=%async_computation | async-start | bytes 557056 | tf_op jit(solution)/shard_map/all_to_all | solution.py:142
  120.0 5.0 %collective-permute-start = (bf16[8,1024]{1,0:T(8,128)(2,1)S(1)}, bf16[8,1024]{1,0:T(8,128)(2,1)S(1)}, u32[]{:S(2)}, u32[]{:S(2)}) collective-permute-start(bf16[8,1024]{1,0:T(8,128)(2,1)S(1)} %get-tuple-element.167), channel_id=1, source_target_pairs={{0,32},{32,64},{64,96},{96,128},{128,160},{160,192},{192,224},{1,3... | collective-permute-start | bytes 49160 | tf_op jit(solution)/shard_map/while/body/eval_jaxpr/ppermute | solution.py:19
  134.8 2.7 collective-permute-start
  147.3 5.6 %collective-permute-start = (bf16[8,1024]{1,0:T(8,128)(2,1)S(1)}, bf16[8,1024]{1,0:T(8,128)(2,1)S(1)}, u32[]{:S(2)}, u32[]{:S(2)}) collective-permute-start(bf16[8,1024]{1,0:T(8,128)(2,1)S(1)} %get-tuple-element.167), channel_id=1, source_target_pairs={{0,32},{32,64},{64,96},{96,128},{128,160},{160,192},{192,224},{1,3... | collective-permute-start | bytes 49160 | tf_op jit(solution)/shard_map/while/body/eval_jaxpr/ppermute | solution.py:19
  162.8 5.6 %collective-permute-start = (bf16[8,1024]{1,0:T(8,128)(2,1)S(1)}, bf16[8,1024]{1,0:T(8,128)(2,1)S(1)}, u32[]{:S(2)}, u32[]{:S(2)}) collective-permute-start(bf16[8,1024]{1,0:T(8,128)(2,1)S(1)} %get-tuple-element.167), channel_id=1, source_target_pairs={{0,32},{32,64},{64,96},{96,128},{128,160},{160,192},{192,224},{1,3... | collective-permute-start | bytes 49160 | tf_op jit(solution)/shard_map/while/body/eval_jaxpr/ppermute | solution.py:19
  178.3 5.6 %collective-permute-start = (bf16[8,1024]{1,0:T(8,128)(2,1)S(1)}, bf16[8,1024]{1,0:T(8,128)(2,1)S(1)}, u32[]{:S(2)}, u32[]{:S(2)}) collective-permute-start(bf16[8,1024]{1,0:T(8,128)(2,1)S(1)} %get-tuple-element.167), channel_id=1, source_target_pairs={{0,32},{32,64},{64,96},{96,128},{128,160},{160,192},{192,224},{1,3... | collective-permute-start | bytes 49160 | tf_op jit(solution)/shard_map/while/body/eval_jaxpr/ppermute | solution.py:19
  193.7 5.6 %collective-permute-start = (bf16[8,1024]{1,0:T(8,128)(2,1)S(1)}, bf16[8,1024]{1,0:T(8,128)(2,1)S(1)}, u32[]{:S(2)}, u32[]{:S(2)}) collective-permute-start(bf16[8,1024]{1,0:T(8,128)(2,1)S(1)} %get-tuple-element.167), channel_id=1, source_target_pairs={{0,32},{32,64},{64,96},{96,128},{128,160},{160,192},{192,224},{1,3... | collective-permute-start | bytes 49160 | tf_op jit(solution)/shard_map/while/body/eval_jaxpr/ppermute | solution.py:19
  209.2 5.6 %collective-permute-start = (bf16[8,1024]{1,0:T(8,128)(2,1)S(1)}, bf16[8,1024]{1,0:T(8,128)(2,1)S(1)}, u32[]{:S(2)}, u32[]{:S(2)}) collective-permute-start(bf16[8,1024]{1,0:T(8,128)(2,1)S(1)} %get-tuple-element.167), channel_id=1, source_target_pairs={{0,32},{32,64},{64,96},{96,128},{128,160},{160,192},{192,224},{1,3... | collective-permute-start | bytes 49160 | tf_op jit(solution)/shard_map/while/body/eval_jaxpr/ppermute | solution.py:19
  224.6 5.6 %collective-permute-start = (bf16[8,1024]{1,0:T(8,128)(2,1)S(1)}, bf16[8,1024]{1,0:T(8,128)(2,1)S(1)}, u32[]{:S(2)}, u32[]{:S(2)}) collective-permute-start(bf16[8,1024]{1,0:T(8,128)(2,1)S(1)} %get-tuple-element.167), channel_id=1, source_target_pairs={{0,32},{32,64},{64,96},{96,128},{128,160},{160,192},{192,224},{1,3... | collective-permute-start | bytes 49160 | tf_op jit(solution)/shard_map/while/body/eval_jaxpr/ppermute | solution.py:19
  240.1 5.6 %collective-permute-start = (bf16[8,1024]{1,0:T(8,128)(2,1)S(1)}, bf16[8,1024]{1,0:T(8,128)(2,1)S(1)}, u32[]{:S(2)}, u32[]{:S(2)}) collective-permute-start(bf16[8,1024]{1,0:T(8,128)(2,1)S(1)} %get-tuple-element.167), channel_id=1, source_target_pairs={{0,32},{32,64},{64,96},{96,128},{128,160},{160,192},{192,224},{1,3... | collective-permute-start | bytes 49160 | tf_op jit(solution)/shard_map/while/body/eval_jaxpr/ppermute | solution.py:19
  247.9 13.3 %collective-permute-start = (bf16[8,1024]{1,0:T(8,128)(2,1)S(1)}, bf16[8,1024]{1,0:T(8,128)(2,1)S(1)}, u32[]{:S(2)}, u32[]{:S(2)}) collective-permute-start(bf16[8,1024]{1,0:T(8,128)(2,1)S(1)} %get-tuple-element.167), channel_id=1, source_target_pairs={{0,32},{32,64},{64,96},{96,128},{128,160},{160,192},{192,224},{1,3... | collective-permute-start | bytes 49160 | tf_op jit(solution)/shard_map/while/body/eval_jaxpr/ppermute | solution.py:19
  263.3 5.6 %collective-permute-start = (bf16[8,1024]{1,0:T(8,128)(2,1)S(1)}, bf16[8,1024]{1,0:T(8,128)(2,1)S(1)}, u32[]{:S(2)}, u32[]{:S(2)}) collective-permute-start(bf16[8,1024]{1,0:T(8,128)(2,1)S(1)} %get-tuple-element.167), channel_id=1, source_target_pairs={{0,32},{32,64},{64,96},{96,128},{128,160},{160,192},{192,224},{1,3... | collective-permute-start | bytes 49160 | tf_op jit(solution)/shard_map/while/body/eval_jaxpr/ppermute | solution.py:19
  271.2 11.3 %collective-permute-start = (bf16[8,1024]{1,0:T(8,128)(2,1)S(1)}, bf16[8,1024]{1,0:T(8,128)(2,1)S(1)}, u32[]{:S(2)}, u32[]{:S(2)}) collective-permute-start(bf16[8,1024]{1,0:T(8,128)(2,1)S(1)} %get-tuple-element.167), channel_id=1, source_target_pairs={{0,32},{32,64},{64,96},{96,128},{128,160},{160,192},{192,224},{1,3... | collective-permute-start | bytes 49160 | tf_op jit(solution)/shard_map/while/body/eval_jaxpr/ppermute | solution.py:19
  284.6 6.8 %collective-permute-start = (bf16[8,1024]{1,0:T(8,128)(2,1)S(1)}, bf16[8,1024]{1,0:T(8,128)(2,1)S(1)}, u32[]{:S(2)}, u32[]{:S(2)}) collective-permute-start(bf16[8,1024]{1,0:T(8,128)(2,1)S(1)} %get-tuple-element.167), channel_id=1, source_target_pairs={{0,32},{32,64},{64,96},{96,128},{128,160},{160,192},{192,224},{1,3... | collective-permute-start | bytes 49160 | tf_op jit(solution)/shard_map/while/body/eval_jaxpr/ppermute | solution.py:19
  293.6 14.5 %collective-permute-start = (bf16[8,1024]{1,0:T(8,128)(2,1)S(1)}, bf16[8,1024]{1,0:T(8,128)(2,1)S(1)}, u32[]{:S(2)}, u32[]{:S(2)}) collective-permute-start(bf16[8,1024]{1,0:T(8,128)(2,1)S(1)} %get-tuple-element.167), channel_id=1, source_target_pairs={{0,32},{32,64},{64,96},{96,128},{128,160},{160,192},{192,224},{1,3... | collective-permute-start | bytes 49160 | tf_op jit(solution)/shard_map/while/body/eval_jaxpr/ppermute | solution.py:19
  310.3 6.8 %collective-permute-start = (bf16[8,1024]{1,0:T(8,128)(2,1)S(1)}, bf16[8,1024]{1,0:T(8,128)(2,1)S(1)}, u32[]{:S(2)}, u32[]{:S(2)}) collective-permute-start(bf16[8,1024]{1,0:T(8,128)(2,1)S(1)} %get-tuple-element.167), channel_id=1, source_target_pairs={{0,32},{32,64},{64,96},{96,128},{128,160},{160,192},{192,224},{1,3... | collective-permute-start | bytes 49160 | tf_op jit(solution)/shard_map/while/body/eval_jaxpr/ppermute | solution.py:19
  319.3 45.2 %all-to-all-start.1 = ((bf16[8,8,1024]{2,1,0:T(8,128)(2,1)}), bf16[8,8,1024]{2,1,0:T(8,128)(2,1)S(1)}, u32[]{:S(2)}, u32[]{:S(2)}) async-start(bf16[8,8,1024]{2,1,0:T(8,128)(2,1)} %get-tuple-element.57), calls=%async_computation.1 | async-start | bytes 262144 | tf_op jit(solution)/shard_map/all_to_all | solution.py:158
Sparse Core Ops, SparseCore 0:
  11.3 107.9 all-gather.2

commit v3 on v2

v3 whole, which is shorter than its diff:
```python
import jax
import jax.numpy as jnp
from jax import lax
from jax.experimental import pallas as pl
from jax.experimental.pallas import tpu as pltpu
from jax.sharding import PartitionSpec as P

H = 1024
ROWS = 4
STEPS = 2
LANES = 128
WIDE = 512
BLOCKS = 4 * H // WIDE


def passed_along(block, axis, distance):
    devices = range(lax.axis_size(axis))
    route = [(i - distance, i) for i in devices if i - distance in devices]
    return lax.ppermute(block, axis, route)


def segments_swapped(quad, lane):
    gates = []
    for k in range(4):
        out = None
        for j in range(4):
            shift = (32 * (j - k)) % LANES
            moved = quad[j] if shift == 0 else pltpu.roll(quad[j], shift, 1)
            out = moved if out is None else jnp.where(lane >= 32 * j, moved, out)
        gates.append(out)
    return gates


def fetch(weights, close, sems, m, p):
    return pltpu.make_async_copy(weights.at[p, m], close.at[m, :, pl.ds(LANES * p, LANES)], sems.at[m, p])


def columns(weights, close, sems, m, q):
    for j in range(4):
        fetch(weights, close, sems, m, 4 * q + j).wait()
    return close[m, :, WIDE * q : WIDE * (q + 1)]


def early_kernel(h_was, weights, product_out, close, sems):
    for p in range(H // 32):
        fetch(weights, close, sems, 0, p).start()
    h_low = h_was[...].astype(jnp.bfloat16)
    for q in range(BLOCKS):
        part = jnp.dot(h_low, columns(weights, close, sems, 0, q), preferred_element_type=jnp.float32)
        product_out[:, WIDE * q : WIDE * (q + 1)] = part


def late_kernel(place, x_got, x_tokens, product, h_was, c_was, bias, weights, place_out, hs_out, x_out, h_out, c_out, gx, close, sems):
    spot = place[...]
    chunk = jnp.max(spot[0:1, :]).astype(jnp.int32)
    level = jnp.max(spot[4:5, :]).astype(jnp.int32)
    chunks = x_tokens.shape[0]
    active = (chunk >= 0) & (chunk < chunks)
    spot_row = lax.broadcasted_iota(jnp.int32, (2 * ROWS, LANES), 0)
    place_out[...] = jnp.where(spot_row < 4, spot + 1.0, spot)

    @pl.when(active)
    def _():
        for m in (1, 0):
            for p in range(H // 32):
                fetch(weights, close, sems, m, p).start()
        x = jnp.where(level == 0, x_tokens[chunk].astype(jnp.float32), x_got[...].astype(jnp.float32))
        x_low = x.astype(jnp.bfloat16)
        lane = lax.broadcasted_iota(jnp.int32, (2 * ROWS, LANES), 1)
        row = lax.broadcasted_iota(jnp.int32, (2 * ROWS, H), 0)
        update = (lane >= 64) & (lane < 96)
        scale = jnp.where(update, 1.0, 0.5)
        shift = jnp.where(update, 0.0, 0.5)

        def cells(gates, q, cell):
            quad = []
            for j in range(4):
                lanes = slice(WIDE * q + LANES * j, WIDE * q + LANES * (j + 1))
                z = gates[:, LANES * j : LANES * (j + 1)] * scale + gx[:, lanes]
                quad.append(jnp.tanh(z) * scale + shift)
            g_in, g_forget, g_update, g_out = segments_swapped(quad, lane)
            cell = g_forget * cell + g_in * g_update
            c_out[:, LANES * q : LANES * (q + 1)] = pltpu.roll(cell, ROWS, 0)
            return (g_out * jnp.tanh(cell)).astype(jnp.bfloat16).astype(jnp.float32)

        pieces = []
        for q in range(BLOCKS):
            part = jnp.dot(x_low, columns(weights, close, sems, 1, q), preferred_element_type=jnp.float32)
            for j in range(4):
                lanes = slice(WIDE * q + LANES * j, WIDE * q + LANES * (j + 1))
                gx[:, lanes] = (part[:, LANES * j : LANES * (j + 1)] + bias[:, lanes]) * scale
            here = slice(LANES * q, LANES * (q + 1))
            pieces.append(cells(product[:, WIDE * q : WIDE * (q + 1)], q, c_was[:, here]))
        first = jnp.concatenate(pieces, axis=1)
        h_low = pltpu.roll(first, ROWS, 0).astype(jnp.bfloat16)
        pieces = []
        for q in range(BLOCKS):
            part = jnp.dot(h_low, columns(weights, close, sems, 0, q), preferred_element_type=jnp.float32)
            here = slice(LANES * q, LANES * (q + 1))
            pieces.append(cells(part, q, c_out[:, here]))
        second = jnp.concatenate(pieces, axis=1)
        h_out[...] = pltpu.roll(second, ROWS, 0)
        both = jnp.where(row < ROWS, first, second)
        hs_out[...] = both.astype(jnp.bfloat16)
        x_out[...] = jnp.where(level >= 1, both + x, both).astype(jnp.bfloat16)

    @pl.when(jnp.logical_not(active))
    def _():
        h_out[...] = h_was[...]
        c_out[...] = c_was[...]
        hs_out[...] = x_got[...]
        x_out[...] = x_got[...]


FULL = pl.BlockSpec(memory_space=pltpu.VMEM)
FAR = pl.BlockSpec(memory_space=pltpu.HBM)


def early(h_was, weights):
    return pl.pallas_call(
        early_kernel,
        out_shape=jax.ShapeDtypeStruct((2 * ROWS, 4 * H), jnp.float32),
        in_specs=[FULL, FAR],
        out_specs=FULL,
        scratch_shapes=[pltpu.VMEM((1, H, 4 * H), jnp.bfloat16), pltpu.SemaphoreType.DMA((1, H // 32))],
        compiler_params=pltpu.CompilerParams(vmem_limit_bytes=16 * 1024 * 1024),
        cost_estimate=pl.CostEstimate(flops=8_000_000_000, bytes_accessed=8_000_000, transcendentals=0),
    )(h_was, weights)


def late(place, x_got, x_tokens, product, h_was, c_was, bias, weights):
    def like(x):
        return jax.ShapeDtypeStruct(x.shape, x.dtype)

    return pl.pallas_call(
        late_kernel,
        out_shape=(like(place), like(x_got), like(x_got), like(h_was), like(c_was)),
        in_specs=[FULL] * 7 + [FAR],
        out_specs=(FULL,) * 5,
        input_output_aliases={0: 0, 4: 3, 5: 4},
        scratch_shapes=[
            pltpu.VMEM((2 * ROWS, 4 * H), jnp.float32),
            pltpu.VMEM((2, H, 4 * H), jnp.bfloat16),
            pltpu.SemaphoreType.DMA((2, H // 32)),
        ],
        compiler_params=pltpu.CompilerParams(vmem_limit_bytes=24 * 1024 * 1024),
    )(place, x_got, x_tokens, product, h_was, c_was, bias, weights)


def shards(tokens, w_input, w_recur, bias):
    steps_count, sentences, units = tokens.shape
    layers = lax.axis_size("layer")
    cols = lax.axis_size("col")
    level = lax.axis_index("layer")
    chunks = steps_count // STEPS
    stages = chunks + layers - 1

    at = jnp.arange(4 * units)
    order = (at[:, None] == 4 * (at % units) + at // units).astype(jnp.bfloat16)
    half = jnp.where(lax.axis_index("dp") == 0, w_recur[0], w_input[0])
    half = jnp.dot(half, order, preferred_element_type=jnp.float32).astype(jnp.bfloat16)
    weights = lax.all_gather(half, ("col", "dp")).reshape(cols, 2, H, 4 * units)

    local_bias = bias[0].reshape(units, 4).T.reshape(1, 4 * units)
    mine = tokens.reshape(steps_count, cols, ROWS, units).transpose(1, 0, 2, 3).astype(jnp.float32)
    sent = jnp.concatenate([mine.reshape(cols, -1), jnp.broadcast_to(local_bias, (cols, 4 * units))], axis=1)
    got = lax.all_to_all(sent, "col", 0, 0, tiled=True)
    x_first = got[:, : steps_count * ROWS * units].reshape(cols, steps_count * ROWS, units).transpose(1, 0, 2)
    x_first = x_first.reshape(chunks, STEPS * ROWS, H).astype(jnp.bfloat16)
    bias_full = got[:, steps_count * ROWS * units :].reshape(1, 4 * H)

    def section(s, carry):
        place, x_sent, hidden, cell, states = carry
        x_got = passed_along(x_sent, "layer", 1)
        product = early(hidden, weights)
        place, hs, x_next, hidden, cell = late(place, x_got, x_first, product, hidden, cell, bias_full, weights)
        states = lax.dynamic_update_index_in_dim(states, hs, s, 0)
        return place, x_next, hidden, cell, states

    row = jnp.arange(2 * ROWS)[:, None]
    place = jnp.where(row < 4, -level, level) * jnp.ones((1, LANES), jnp.float32)
    zero_x = jnp.zeros((STEPS * ROWS, H), jnp.bfloat16)
    zero_s = jnp.zeros((STEPS * ROWS, H), jnp.float32)
    zero_t = jnp.zeros((stages, STEPS * ROWS, H), jnp.bfloat16)
    _, _, hidden, cell, states = lax.fori_loop(0, stages, section, (place, zero_x, zero_s, zero_s, zero_t))

    top = lax.all_to_all(states[layers - 1 :], "layer", 0, 0, tiled=True)[layers - 1]
    rows = jnp.concatenate([top.astype(jnp.float32), hidden[:ROWS], cell[:ROWS]], axis=0)
    sent = rows.reshape(4 * ROWS, cols, units).transpose(1, 0, 2)
    got = lax.all_to_all(sent, "col", 0, 0, tiled=True).reshape(cols, 4, ROWS, units).transpose(1, 0, 2, 3)
    got = got.reshape(4, sentences, units)
    return got[:2].astype(jnp.bfloat16), got[2:3].astype(jnp.bfloat16), got[3:]


def solution(mesh):
    in_specs = (
        P(None, "dp", "col"),
        P("layer", None, "col"),
        P("layer", None, "col"),
        P("layer", "col"),
    )
    out_specs = (P("layer", "dp", "col"), P("layer", "dp", "col"), P("layer", "dp", "col"))
    return jax.shard_map(shards, mesh=mesh, in_specs=in_specs, out_specs=out_specs, check_vma=False)
```

time: 393 us -> 362 us (0.921)
  starting transfers between devices: 130 us -> 89.9 us
  Pallas kernels: 93.5 us -> 124 us
  waiting for transfers between devices: 123 us -> 102 us
    pallas_call x15 -> x30, Pallas kernels: 93.5 us -> 124 us  [the longest x15 65.2 us: late(): pl.pallas_call(late_kernel, out_shape=(like(place), like(x_got), like(x_g...]
    ppermute x15, starting transfers between devices: 83.9 us -> 56.6 us  [passed_along(): return lax.ppermute(block, axis, route)]
    ppermute x15, waiting for transfers between devices: 21.4 us -> 0.04 us  [passed_along(): return lax.ppermute(block, axis, route)]
    all_to_all x1, starting transfers between devices: 36.2 us -> 23.1 us  [shards(): lax.all_to_all(states[layers - 1:], 'layer', 0, 0, tiled=True)[layers - 1]]
  transfers between devices with their start and end apart: 18 -> 18, of which waited for: 18 -> 3; matrix products, arithmetic and copies ran while one was open for 2% -> 2% of each run, Pallas kernels for 0% -> 16%
where the time goes in v3:
time: 362 us; the launch traced here: 361 us
  Pallas kernels  124 us (34%)
  waiting for transfers between devices  102 us (28%)
  starting transfers between devices  89.9 us (25%)
  blocking collectives  16.3 us (5%)
  between operations  14.3 us (4%)
  local copies, waits for them, and re-layouts  9.95 us (3%)
    all_gather x1, waiting for transfers between devices, shards(): weights = lax.all_gather(half, ('col', 'dp')).reshape(cols, 2, H, 4 * units)  80.1 us
    pallas_call x15, Pallas kernels, late(): pl.pallas_call(late_kernel, out_shape=(like(place), like(x_got), like(x_g...  65.2 us
    pallas_call x15, Pallas kernels, early(): pl.pallas_call(early_kernel, out_shape=jax.ShapeDtypeStruct((2 * ROWS, 4...  58.4 us
    ppermute x15, starting transfers between devices, passed_along(): return lax.ppermute(block, axis, route)  56.6 us
    all_to_all x1, starting transfers between devices, shards(): lax.all_to_all(states[layers - 1:], 'layer', 0, 0, tiled=True)[layers - 1]  23.1 us
    all_to_all x1, blocking collectives, shards(): lax.all_to_all(sent, 'col', 0, 0, tiled=True).reshape(cols, 4, ROWS, units)  16.3 us
    all_to_all x1, waiting for transfers between devices, shards(): got = lax.all_to_all(sent, 'col', 0, 0, tiled=True)  12.6 us
    all_to_all x1, starting transfers between devices, shards(): got = lax.all_to_all(sent, 'col', 0, 0, tiled=True)  10.2 us
  transfers between devices with their start and end apart: 18, of which 3 were waited for; matrix products, arithmetic and copies ran while one was open for 2% of the time, Pallas kernels for 16%

profile of v3, /device:TPU:8, one launch (start us, length us, event | category | flops | bytes accessed | tf_op | source)
XLA Modules:
  0.0 360.8 jit_solution(16292489708793872152)
XLA Ops:
  15.1 10.2 %all-to-all-start = ((f32[32,1,2176]{2,1,0:T(1,128)}), f32[32,1,2176]{2,1,0:T(1,128)S(1)}, u32[]{:S(2)}, u32[]{:S(2)}) async-start(f32[32,1,2176]{2,1,0:T(1,128)} %copy.47), calls=%async_computation | async-start | bytes 557056 | tf_op jit(solution)/shard_map/all_to_all | solution.py:167
  25.3 12.6 %all-to-all-done = f32[32,1,2176]{2,1,0:T(1,128)S(1)} async-done(((f32[32,1,2176]{2,1,0:T(1,128)}), f32[32,1,2176]{2,1,0:T(1,128)S(1)}, u32[]{:S(2)}, u32[]{:S(2)}) %all-to-all-start) | async-done | bytes 278560 | tf_op jit(solution)/shard_map/all_to_all | solution.py:167
  39.2 80.1 %all-gather.3.cloned.1.call-done = bf16[65536,128]{1,0:T(8,128)(2,1)} async-done(((bf16[1024,128]{1,0:T(8,128)(2,1)}), bf16[65536,128]{1,0:T(8,128)(2,1)}) %all-gather.3.cloned.1.call-update) | async-done | bytes 16777232 | tf_op jit(solution)/shard_map/all_gather | solution.py:162
  119.4 181.2 %while.21 = (s32[]{:T(128)}, f32[8,128]{1,0:T(8,128)S(1)}, bf16[8,1024]{1,0:T(8,128)(2,1)S(1)}, f32[8,1024]{1,0:T(8,128)S(1)}, f32[8,1024]{1,0:T(8,128)S(1)}, /*...) while((s32[]{:T(128)}, f32[8,128]{1,0:T(8,128)S(1)}, ...), condition=%wide.region_1.2_spmd, body=%wide.region_0.1_spmd.sunk | while | flops 8000000000 | bytes 8098457 | solution.py:185
  123.0 3.9 %eval_jaxpr.6.product = f32[8,4096]{1,0:T(8,128)S(1)} custom-call(f32[8,1024]{1,0:T(8,128)S(1)} %get-tuple-element.268.h_was, bf16[32,2,1024,128]{3,2,1,0:T(8,128)(2,1)} %get-tuple-element.281.weights), custom_call_target="tpu_custom_call" | custom-call | flops 8000000000 | bytes 8000000 | tf_op jit(solution)/shard_map/while/body/eval_jaxpr/pallas_call | solution.py:120
  126.9 7.5 %eval_jaxpr.7 = (f32[8,128]{1,0:T(8,128)S(1)}, bf16[8,1024]{1,0:T(8,128)(2,1)S(1)}, bf16[8,1024]{1,0:T(8,128)(2,1)S(1)}, f32[8,1024]{1,0:T(8,128)S(1)}, f32[8,1024]{1,0:T(8,128)S(1)}) custom-call(f32[8,128]{1,0:T(8,128)S(1)} %get-tuple-element.266.place, ...), custom_call_target="tpu_custom_call", output_to_operand_aliasing={{0}: (0, {}), {3}: (4, {}), {4}: (5, {})} | custom-call | tf_op jit(solution)/shard_map/while/body/eval_jaxpr/pallas_call | solution.py:135
  135.8 3.9 %eval_jaxpr.6.product = f32[8,4096]{1,0:T(8,128)S(1)} custom-call(f32[8,1024]{1,0:T(8,128)S(1)} %get-tuple-element.268.h_was, bf16[32,2,1024,128]{3,2,1,0:T(8,128)(2,1)} %get-tuple-element.281.weights), custom_call_target="tpu_custom_call" | custom-call | flops 8000000000 | bytes 8000000 | tf_op jit(solution)/shard_map/while/body/eval_jaxpr/pallas_call | solution.py:120
  139.7 7.5 %eval_jaxpr.7 = (f32[8,128]{1,0:T(8,128)S(1)}, bf16[8,1024]{1,0:T(8,128)(2,1)S(1)}, bf16[8,1024]{1,0:T(8,128)(2,1)S(1)}, f32[8,1024]{1,0:T(8,128)S(1)}, f32[8,1024]{1,0:T(8,128)S(1)}) custom-call(f32[8,128]{1,0:T(8,128)S(1)} %get-tuple-element.266.place, ...), custom_call_target="tpu_custom_call", output_to_operand_aliasing={{0}: (0, {}), {3}: (4, {}), {4}: (5, {})} | custom-call | tf_op jit(solution)/shard_map/while/body/eval_jaxpr/pallas_call | solution.py:135
  152.9 7.5 %eval_jaxpr.7 = (f32[8,128]{1,0:T(8,128)S(1)}, bf16[8,1024]{1,0:T(8,128)(2,1)S(1)}, bf16[8,1024]{1,0:T(8,128)(2,1)S(1)}, f32[8,1024]{1,0:T(8,128)S(1)}, f32[8,1024]{1,0:T(8,128)S(1)}) custom-call(f32[8,128]{1,0:T(8,128)S(1)} %get-tuple-element.266.place, ...), custom_call_target="tpu_custom_call", output_to_operand_aliasing={{0}: (0, {}), {3}: (4, {}), {4}: (5, {})} | custom-call | tf_op jit(solution)/shard_map/while/body/eval_jaxpr/pallas_call | solution.py:135
  166.3 7.5 %eval_jaxpr.7 = (f32[8,128]{1,0:T(8,128)S(1)}, bf16[8,1024]{1,0:T(8,128)(2,1)S(1)}, bf16[8,1024]{1,0:T(8,128)(2,1)S(1)}, f32[8,1024]{1,0:T(8,128)S(1)}, f32[8,1024]{1,0:T(8,128)S(1)}) custom-call(f32[8,128]{1,0:T(8,128)S(1)} %get-tuple-element.266.place, ...), custom_call_target="tpu_custom_call", output_to_operand_aliasing={{0}: (0, {}), {3}: (4, {}), {4}: (5, {})} | custom-call | tf_op jit(solution)/shard_map/while/body/eval_jaxpr/pallas_call | solution.py:135
  175.8 3.9 %eval_jaxpr.6.product = f32[8,4096]{1,0:T(8,128)S(1)} custom-call(f32[8,1024]{1,0:T(8,128)S(1)} %get-tuple-element.268.h_was, bf16[32,2,1024,128]{3,2,1,0:T(8,128)(2,1)} %get-tuple-element.281.weights), custom_call_target="tpu_custom_call" | custom-call | flops 8000000000 | bytes 8000000 | tf_op jit(solution)/shard_map/while/body/eval_jaxpr/pallas_call | solution.py:120
  179.7 7.5 %eval_jaxpr.7 = (f32[8,128]{1,0:T(8,128)S(1)}, bf16[8,1024]{1,0:T(8,128)(2,1)S(1)}, bf16[8,1024]{1,0:T(8,128)(2,1)S(1)}, f32[8,1024]{1,0:T(8,128)S(1)}, f32[8,1024]{1,0:T(8,128)S(1)}) custom-call(f32[8,128]{1,0:T(8,128)S(1)} %get-tuple-element.266.place, ...), custom_call_target="tpu_custom_call", output_to_operand_aliasing={{0}: (0, {}), {3}: (4, {}), {4}: (5, {})} | custom-call | tf_op jit(solution)/shard_map/while/body/eval_jaxpr/pallas_call | solution.py:135
  189.2 3.9 %eval_jaxpr.6.product = f32[8,4096]{1,0:T(8,128)S(1)} custom-call(f32[8,1024]{1,0:T(8,128)S(1)} %get-tuple-element.268.h_was, bf16[32,2,1024,128]{3,2,1,0:T(8,128)(2,1)} %get-tuple-element.281.weights), custom_call_target="tpu_custom_call" | custom-call | flops 8000000000 | bytes 8000000 | tf_op jit(solution)/shard_map/while/body/eval_jaxpr/pallas_call | solution.py:120
  193.1 7.5 %eval_jaxpr.7 = (f32[8,128]{1,0:T(8,128)S(1)}, bf16[8,1024]{1,0:T(8,128)(2,1)S(1)}, bf16[8,1024]{1,0:T(8,128)(2,1)S(1)}, f32[8,1024]{1,0:T(8,128)S(1)}, f32[8,1024]{1,0:T(8,128)S(1)}) custom-call(f32[8,128]{1,0:T(8,128)S(1)} %get-tuple-element.266.place, ...), custom_call_target="tpu_custom_call", output_to_operand_aliasing={{0}: (0, {}), {3}: (4, {}), {4}: (5, {})} | custom-call | tf_op jit(solution)/shard_map/while/body/eval_jaxpr/pallas_call | solution.py:135
  202.6 3.9 %eval_jaxpr.6.product = f32[8,4096]{1,0:T(8,128)S(1)} custom-call(f32[8,1024]{1,0:T(8,128)S(1)} %get-tuple-element.268.h_was, bf16[32,2,1024,128]{3,2,1,0:T(8,128)(2,1)} %get-tuple-element.281.weights), custom_call_target="tpu_custom_call" | custom-call | flops 8000000000 | bytes 8000000 | tf_op jit(solution)/shard_map/while/body/eval_jaxpr/pallas_call | solution.py:120
  206.5 7.5 %eval_jaxpr.7 = (f32[8,128]{1,0:T(8,128)S(1)}, bf16[8,1024]{1,0:T(8,128)(2,1)S(1)}, bf16[8,1024]{1,0:T(8,128)(2,1)S(1)}, f32[8,1024]{1,0:T(8,128)S(1)}, f32[8,1024]{1,0:T(8,128)S(1)}) custom-call(f32[8,128]{1,0:T(8,128)S(1)} %get-tuple-element.266.place, ...), custom_call_target="tpu_custom_call", output_to_operand_aliasing={{0}: (0, {}), {3}: (4, {}), {4}: (5, {})} | custom-call | tf_op jit(solution)/shard_map/while/body/eval_jaxpr/pallas_call | solution.py:135
  216.0 3.9 %eval_jaxpr.6.product = f32[8,4096]{1,0:T(8,128)S(1)} custom-call(f32[8,1024]{1,0:T(8,128)S(1)} %get-tuple-element.268.h_was, bf16[32,2,1024,128]{3,2,1,0:T(8,128)(2,1)} %get-tuple-element.281.weights), custom_call_target="tpu_custom_call" | custom-call | flops 8000000000 | bytes 8000000 | tf_op jit(solution)/shard_map/while/body/eval_jaxpr/pallas_call | solution.py:120
  219.9 7.5 %eval_jaxpr.7 = (f32[8,128]{1,0:T(8,128)S(1)}, bf16[8,1024]{1,0:T(8,128)(2,1)S(1)}, bf16[8,1024]{1,0:T(8,128)(2,1)S(1)}, f32[8,1024]{1,0:T(8,128)S(1)}, f32[8,1024]{1,0:T(8,128)S(1)}) custom-call(f32[8,128]{1,0:T(8,128)S(1)} %get-tuple-element.266.place, ...), custom_call_target="tpu_custom_call", output_to_operand_aliasing={{0}: (0, {}), {3}: (4, {}), {4}: (5, {})} | custom-call | tf_op jit(solution)/shard_map/while/body/eval_jaxpr/pallas_call | solution.py:135
  234.6 9.7 %collective-permute-start = (bf16[8,1024]{1,0:T(8,128)(2,1)S(1)}, bf16[8,1024]{1,0:T(8,128)(2,1)S(1)}, u32[]{:S(2)}, u32[]{:S(2)}) collective-permute-start(bf16[8,1024]{1,0:T(8,128)(2,1)S(1)} %get-tuple-element.267), channel_id=1, source_target_pairs={{0,32},{32,64},{64,96},{96,128},{128,160},{160,192},{192,224},{1,3... | collective-permute-start | bytes 49160 | tf_op jit(solution)/shard_map/while/body/eval_jaxpr/ppermute | solution.py:19
  256.6 9.7 %collective-permute-start = (bf16[8,1024]{1,0:T(8,128)(2,1)S(1)}, bf16[8,1024]{1,0:T(8,128)(2,1)S(1)}, u32[]{:S(2)}, u32[]{:S(2)}) collective-permute-start(bf16[8,1024]{1,0:T(8,128)(2,1)S(1)} %get-tuple-element.267), channel_id=1, source_target_pairs={{0,32},{32,64},{64,96},{96,128},{128,160},{160,192},{192,224},{1,3... | collective-permute-start | bytes 49160 | tf_op jit(solution)/shard_map/while/body/eval_jaxpr/ppermute | solution.py:19
  278.6 9.7 %collective-permute-start = (bf16[8,1024]{1,0:T(8,128)(2,1)S(1)}, bf16[8,1024]{1,0:T(8,128)(2,1)S(1)}, u32[]{:S(2)}, u32[]{:S(2)}) collective-permute-start(bf16[8,1024]{1,0:T(8,128)(2,1)S(1)} %get-tuple-element.267), channel_id=1, source_target_pairs={{0,32},{32,64},{64,96},{96,128},{128,160},{160,192},{192,224},{1,3... | collective-permute-start | bytes 49160 | tf_op jit(solution)/shard_map/while/body/eval_jaxpr/ppermute | solution.py:19
  301.3 23.1 %all-to-all-start.1 = ((bf16[8,8,1024]{2,1,0:T(8,128)(2,1)}), bf16[8,8,1024]{2,1,0:T(8,128)(2,1)S(1)}, u32[]{:S(2)}, u32[]{:S(2)}) async-start(bf16[8,8,1024]{2,1,0:T(8,128)(2,1)} %slice.37), calls=%async_computation.1 | async-start | bytes 262144 | tf_op jit(solution)/shard_map/all_to_all | solution.py:187
  324.4 9.1 %all-to-all-done.1 = bf16[8,8,1024]{2,1,0:T(8,128)(2,1)S(1)} async-done(((bf16[8,8,1024]{2,1,0:T(8,128)(2,1)}), bf16[8,8,1024]{2,1,0:T(8,128)(2,1)S(1)}, u32[]{:S(2)}, u32[]{:S(2)}) %all-to-all-start.1) | async-done | bytes 131104 | tf_op jit(solution)/shard_map/all_to_all | solution.py:187
  333.9 16.3 %all_to_all.22 = f32[32,1,512]{2,1,0:T(1,128)S(1)} all-to-all(f32[32,1,512]{2,1,0:T(1,128)S(1)} %reshape.112), channel_id=1, replica_groups=mesh['dp'=2,'layer'=8,'col'=32] {'col'}, dimensions={0} | all-to-all | bytes 131072 | tf_op jit(solution)/shard_map/all_to_all | solution.py:190
  (108 shorter events, 81.7 us)
Async XLA Ops:
  7.2 112.2 %all-gather.3.cloned.1.call-start = ((), (), s32[]{:S(2)}) async-start(), calls=%async_computation.3 | async-start | bytes 17039360 | tf_op jit(solution)/shard_map/all_gather | solution.py:162
  15.1 22.8 %all-to-all-start = ((f32[32,1,2176]{2,1,0:T(1,128)}), f32[32,1,2176]{2,1,0:T(1,128)S(1)}, u32[]{:S(2)}, u32[]{:S(2)}) async-start(f32[32,1,2176]{2,1,0:T(1,128)} %copy.47), calls=%async_computation | async-start | bytes 557056 | tf_op jit(solution)/shard_map/all_to_all | solution.py:167
  119.4 7.5 %collective-permute-start = (bf16[8,1024]{1,0:T(8,128)(2,1)S(1)}, bf16[8,1024]{1,0:T(8,128)(2,1)S(1)}, u32[]{:S(2)}, u32[]{:S(2)}) collective-permute-start(bf16[8,1024]{1,0:T(8,128)(2,1)S(1)} %get-tuple-element.267), channel_id=1, source_target_pairs={{0,32},{32,64},{64,96},{96,128},{128,160},{160,192},{192,224},{1,3... | collective-permute-start | bytes 49160 | tf_op jit(solution)/shard_map/while/body/eval_jaxpr/ppermute | solution.py:19
  134.5 5.2 %collective-permute-start = (bf16[8,1024]{1,0:T(8,128)(2,1)S(1)}, bf16[8,1024]{1,0:T(8,128)(2,1)S(1)}, u32[]{:S(2)}, u32[]{:S(2)}) collective-permute-start(bf16[8,1024]{1,0:T(8,128)(2,1)S(1)} %get-tuple-element.267), channel_id=1, source_target_pairs={{0,32},{32,64},{64,96},{96,128},{128,160},{160,192},{192,224},{1,3... | collective-permute-start | bytes 49160 | tf_op jit(solution)/shard_map/while/body/eval_jaxpr/ppermute | solution.py:19
  147.2 5.6 %collective-permute-start = (bf16[8,1024]{1,0:T(8,128)(2,1)S(1)}, bf16[8,1024]{1,0:T(8,128)(2,1)S(1)}, u32[]{:S(2)}, u32[]{:S(2)}) collective-permute-start(bf16[8,1024]{1,0:T(8,128)(2,1)S(1)} %get-tuple-element.267), channel_id=1, source_target_pairs={{0,32},{32,64},{64,96},{96,128},{128,160},{160,192},{192,224},{1,3... | collective-permute-start | bytes 49160 | tf_op jit(solution)/shard_map/while/body/eval_jaxpr/ppermute | solution.py:19
  160.4 5.8 %collective-permute-start = (bf16[8,1024]{1,0:T(8,128)(2,1)S(1)}, bf16[8,1024]{1,0:T(8,128)(2,1)S(1)}, u32[]{:S(2)}, u32[]{:S(2)}) collective-permute-start(bf16[8,1024]{1,0:T(8,128)(2,1)S(1)} %get-tuple-element.267), channel_id=1, source_target_pairs={{0,32},{32,64},{64,96},{96,128},{128,160},{160,192},{192,224},{1,3... | collective-permute-start | bytes 49160 | tf_op jit(solution)/shard_map/while/body/eval_jaxpr/ppermute | solution.py:19
  173.8 5.8 %collective-permute-start = (bf16[8,1024]{1,0:T(8,128)(2,1)S(1)}, bf16[8,1024]{1,0:T(8,128)(2,1)S(1)}, u32[]{:S(2)}, u32[]{:S(2)}) collective-permute-start(bf16[8,1024]{1,0:T(8,128)(2,1)S(1)} %get-tuple-element.267), channel_id=1, source_target_pairs={{0,32},{32,64},{64,96},{96,128},{128,160},{160,192},{192,224},{1,3... | collective-permute-start | bytes 49160 | tf_op jit(solution)/shard_map/while/body/eval_jaxpr/ppermute | solution.py:19
  187.2 5.8 %collective-permute-start = (bf16[8,1024]{1,0:T(8,128)(2,1)S(1)}, bf16[8,1024]{1,0:T(8,128)(2,1)S(1)}, u32[]{:S(2)}, u32[]{:S(2)}) collective-permute-start(bf16[8,1024]{1,0:T(8,128)(2,1)S(1)} %get-tuple-element.267), channel_id=1, source_target_pairs={{0,32},{32,64},{64,96},{96,128},{128,160},{160,192},{192,224},{1,3... | collective-permute-start | bytes 49160 | tf_op jit(solution)/shard_map/while/body/eval_jaxpr/ppermute | solution.py:19
  200.7 5.8 %collective-permute-start = (bf16[8,1024]{1,0:T(8,128)(2,1)S(1)}, bf16[8,1024]{1,0:T(8,128)(2,1)S(1)}, u32[]{:S(2)}, u32[]{:S(2)}) collective-permute-start(bf16[8,1024]{1,0:T(8,128)(2,1)S(1)} %get-tuple-element.267), channel_id=1, source_target_pairs={{0,32},{32,64},{64,96},{96,128},{128,160},{160,192},{192,224},{1,3... | collective-permute-start | bytes 49160 | tf_op jit(solution)/shard_map/while/body/eval_jaxpr/ppermute | solution.py:19
  214.1 5.8 %collective-permute-start = (bf16[8,1024]{1,0:T(8,128)(2,1)S(1)}, bf16[8,1024]{1,0:T(8,128)(2,1)S(1)}, u32[]{:S(2)}, u32[]{:S(2)}) collective-permute-start(bf16[8,1024]{1,0:T(8,128)(2,1)S(1)} %get-tuple-element.267), channel_id=1, source_target_pairs={{0,32},{32,64},{64,96},{96,128},{128,160},{160,192},{192,224},{1,3... | collective-permute-start | bytes 49160 | tf_op jit(solution)/shard_map/while/body/eval_jaxpr/ppermute | solution.py:19
  227.5 6.4 %collective-permute-start = (bf16[8,1024]{1,0:T(8,128)(2,1)S(1)}, bf16[8,1024]{1,0:T(8,128)(2,1)S(1)}, u32[]{:S(2)}, u32[]{:S(2)}) collective-permute-start(bf16[8,1024]{1,0:T(8,128)(2,1)S(1)} %get-tuple-element.267), channel_id=1, source_target_pairs={{0,32},{32,64},{64,96},{96,128},{128,160},{160,192},{192,224},{1,3... | collective-permute-start | bytes 49160 | tf_op jit(solution)/shard_map/while/body/eval_jaxpr/ppermute | solution.py:19
  234.6 13.6 %collective-permute-start = (bf16[8,1024]{1,0:T(8,128)(2,1)S(1)}, bf16[8,1024]{1,0:T(8,128)(2,1)S(1)}, u32[]{:S(2)}, u32[]{:S(2)}) collective-permute-start(bf16[8,1024]{1,0:T(8,128)(2,1)S(1)} %get-tuple-element.267), channel_id=1, source_target_pairs={{0,32},{32,64},{64,96},{96,128},{128,160},{160,192},{192,224},{1,3... | collective-permute-start | bytes 49160 | tf_op jit(solution)/shard_map/while/body/eval_jaxpr/ppermute | solution.py:19
  249.0 6.8 %collective-permute-start = (bf16[8,1024]{1,0:T(8,128)(2,1)S(1)}, bf16[8,1024]{1,0:T(8,128)(2,1)S(1)}, u32[]{:S(2)}, u32[]{:S(2)}) collective-permute-start(bf16[8,1024]{1,0:T(8,128)(2,1)S(1)} %get-tuple-element.267), channel_id=1, source_target_pairs={{0,32},{32,64},{64,96},{96,128},{128,160},{160,192},{192,224},{1,3... | collective-permute-start | bytes 49160 | tf_op jit(solution)/shard_map/while/body/eval_jaxpr/ppermute | solution.py:19
  256.6 13.6 %collective-permute-start = (bf16[8,1024]{1,0:T(8,128)(2,1)S(1)}, bf16[8,1024]{1,0:T(8,128)(2,1)S(1)}, u32[]{:S(2)}, u32[]{:S(2)}) collective-permute-start(bf16[8,1024]{1,0:T(8,128)(2,1)S(1)} %get-tuple-element.267), channel_id=1, source_target_pairs={{0,32},{32,64},{64,96},{96,128},{128,160},{160,192},{192,224},{1,3... | collective-permute-start | bytes 49160 | tf_op jit(solution)/shard_map/while/body/eval_jaxpr/ppermute | solution.py:19
  271.0 6.8 %collective-permute-start = (bf16[8,1024]{1,0:T(8,128)(2,1)S(1)}, bf16[8,1024]{1,0:T(8,128)(2,1)S(1)}, u32[]{:S(2)}, u32[]{:S(2)}) collective-permute-start(bf16[8,1024]{1,0:T(8,128)(2,1)S(1)} %get-tuple-element.267), channel_id=1, source_target_pairs={{0,32},{32,64},{64,96},{96,128},{128,160},{160,192},{192,224},{1,3... | collective-permute-start | bytes 49160 | tf_op jit(solution)/shard_map/while/body/eval_jaxpr/ppermute | solution.py:19
  278.6 13.6 %collective-permute-start = (bf16[8,1024]{1,0:T(8,128)(2,1)S(1)}, bf16[8,1024]{1,0:T(8,128)(2,1)S(1)}, u32[]{:S(2)}, u32[]{:S(2)}) collective-permute-start(bf16[8,1024]{1,0:T(8,128)(2,1)S(1)} %get-tuple-element.267), channel_id=1, source_target_pairs={{0,32},{32,64},{64,96},{96,128},{128,160},{160,192},{192,224},{1,3... | collective-permute-start | bytes 49160 | tf_op jit(solution)/shard_map/while/body/eval_jaxpr/ppermute | solution.py:19
  293.0 6.8 %collective-permute-start = (bf16[8,1024]{1,0:T(8,128)(2,1)S(1)}, bf16[8,1024]{1,0:T(8,128)(2,1)S(1)}, u32[]{:S(2)}, u32[]{:S(2)}) collective-permute-start(bf16[8,1024]{1,0:T(8,128)(2,1)S(1)} %get-tuple-element.267), channel_id=1, source_target_pairs={{0,32},{32,64},{64,96},{96,128},{128,160},{160,192},{192,224},{1,3... | collective-permute-start | bytes 49160 | tf_op jit(solution)/shard_map/while/body/eval_jaxpr/ppermute | solution.py:19
  301.3 32.1 %all-to-all-start.1 = ((bf16[8,8,1024]{2,1,0:T(8,128)(2,1)}), bf16[8,8,1024]{2,1,0:T(8,128)(2,1)S(1)}, u32[]{:S(2)}, u32[]{:S(2)}) async-start(bf16[8,8,1024]{2,1,0:T(8,128)(2,1)} %slice.37), calls=%async_computation.1 | async-start | bytes 262144 | tf_op jit(solution)/shard_map/all_to_all | solution.py:187
Sparse Core Ops, SparseCore 0:
  11.3 107.9 all-gather.2

commit v4 on v3

--- a/solution.py
+++ b/solution.py
@@ -11,6 +11,7 @@
 LANES = 128
 WIDE = 512
 BLOCKS = 4 * H // WIDE
+KEPT = 2
 
 
 def passed_along(block, axis, distance):
@@ -41,6 +42,16 @@
     return close[m, :, WIDE * q : WIDE * (q + 1)]
 
 
+def keep_kernel(weights, kept, sems):
+    copies = [
+        pltpu.make_async_copy(weights.at[p, 1], kept.at[:, pl.ds(LANES * p, LANES)], sems.at[p]) for p in range(4 * KEPT)
+    ]
+    for copy in copies:
+        copy.start()
+    for copy in copies:
+        copy.wait()
+
+
 def early_kernel(h_was, weights, product_out, close, sems):
     for p in range(H // 32):
         fetch(weights, close, sems, 0, p).start()
@@ -50,7 +61,7 @@
         product_out[:, WIDE * q : WIDE * (q + 1)] = part
 
 
-def late_kernel(place, x_got, x_tokens, product, h_was, c_was, bias, weights, place_out, hs_out, x_out, h_out, c_out, gx, close, sems):
+def late_kernel(place, x_got, x_tokens, product, h_was, c_was, bias, kept, weights, place_out, hs_out, x_out, h_out, c_out, gx, close, sems):
     spot = place[...]
     chunk = jnp.max(spot[0:1, :]).astype(jnp.int32)
     level = jnp.max(spot[4:5, :]).astype(jnp.int32)
@@ -61,8 +72,8 @@
 
     @pl.when(active)
     def _():
-        for m in (1, 0):
-            for p in range(H // 32):
+        for m, done in ((1, 4 * KEPT), (0, 0)):
+            for p in range(done, H // 32):
                 fetch(weights, close, sems, m, p).start()
         x = jnp.where(level == 0, x_tokens[chunk].astype(jnp.float32), x_got[...].astype(jnp.float32))
         x_low = x.astype(jnp.bfloat16)
@@ -85,7 +96,11 @@
 
         pieces = []
         for q in range(BLOCKS):
-            part = jnp.dot(x_low, columns(weights, close, sems, 1, q), preferred_element_type=jnp.float32)
+            if q < KEPT:
+                block = kept[:, WIDE * q : WIDE * (q + 1)]
+            else:
+                block = columns(weights, close, sems, 1, q)
+            part = jnp.dot(x_low, block, preferred_element_type=jnp.float32)
             for j in range(4):
                 lanes = slice(WIDE * q + LANES * j, WIDE * q + LANES * (j + 1))
                 gx[:, lanes] = (part[:, LANES * j : LANES * (j + 1)] + bias[:, lanes]) * scale
@@ -128,14 +143,25 @@
     )(h_was, weights)
 
 
-def late(place, x_got, x_tokens, product, h_was, c_was, bias, weights):
+def keep(weights):
+    return pl.pallas_call(
+        keep_kernel,
+        out_shape=jax.ShapeDtypeStruct((H, WIDE * KEPT), jnp.bfloat16),
+        in_specs=[FAR],
+        out_specs=FULL,
+        scratch_shapes=[pltpu.SemaphoreType.DMA((4 * KEPT,))],
+        compiler_params=pltpu.CompilerParams(vmem_limit_bytes=16 * 1024 * 1024),
+    )(weights)
+
+
+def late(place, x_got, x_tokens, product, h_was, c_was, bias, kept, weights):
     def like(x):
         return jax.ShapeDtypeStruct(x.shape, x.dtype)
 
     return pl.pallas_call(
         late_kernel,
         out_shape=(like(place), like(x_got), like(x_got), like(h_was), like(c_was)),
-        in_specs=[FULL] * 7 + [FAR],
+        in_specs=[FULL] * 8 + [FAR],
         out_specs=(FULL,) * 5,
         input_output_aliases={0: 0, 4: 3, 5: 4},
         scratch_shapes=[
@@ -144,7 +170,7 @@
             pltpu.SemaphoreType.DMA((2, H // 32)),
         ],
         compiler_params=pltpu.CompilerParams(vmem_limit_bytes=24 * 1024 * 1024),
-    )(place, x_got, x_tokens, product, h_was, c_was, bias, weights)
+    )(place, x_got, x_tokens, product, h_was, c_was, bias, kept, weights)
 
 
 def shards(tokens, w_input, w_recur, bias):
@@ -161,6 +187,8 @@
     half = jnp.dot(half, order, preferred_element_type=jnp.float32).astype(jnp.bfloat16)
     weights = lax.all_gather(half, ("col", "dp")).reshape(cols, 2, H, 4 * units)
 
+    kept = keep(weights)
+
     local_bias = bias[0].reshape(units, 4).T.reshape(1, 4 * units)
     mine = tokens.reshape(steps_count, cols, ROWS, units).transpose(1, 0, 2, 3).astype(jnp.float32)
     sent = jnp.concatenate([mine.reshape(cols, -1), jnp.broadcast_to(local_bias, (cols, 4 * units))], axis=1)
@@ -173,7 +201,9 @@
         place, x_sent, hidden, cell, states = carry
         x_got = passed_along(x_sent, "layer", 1)
         product = early(hidden, weights)
-        place, hs, x_next, hidden, cell = late(place, x_got, x_first, product, hidden, cell, bias_full, weights)
+        place, hs, x_next, hidden, cell = late(
+            place, x_got, x_first, product, hidden, cell, bias_full, kept, weights
+        )
         states = lax.dynamic_update_index_in_dim(states, hs, s, 0)
         return place, x_next, hidden, cell, states
 

time: 362 us -> 357 us (0.986)
  no operation moved by 1% of the time
where the time goes in v4:
time: 357 us; the launch traced here: 356 us
  Pallas kernels  122 us (34%)
  waiting for transfers between devices  102 us (29%)
  starting transfers between devices  86.7 us (24%)
  blocking collectives  16.3 us (5%)
  between operations  14.3 us (4%)
  local copies, waits for them, and re-layouts  9.95 us (3%)
    all_gather x1, waiting for transfers between devices, shards(): weights = lax.all_gather(half, ('col', 'dp')).reshape(cols, 2, H, 4 * units)  80.1 us
    pallas_call x15, Pallas kernels, late(): pl.pallas_call(late_kernel, out_shape=(like(place), like(x_got), like(x_g...  61.7 us
    pallas_call x15, Pallas kernels, early(): pl.pallas_call(early_kernel, out_shape=jax.ShapeDtypeStruct((2 * ROWS, 4...  58.4 us
    ppermute x15, starting transfers between devices, passed_along(): return lax.ppermute(block, axis, route)  55.3 us
    all_to_all x1, starting transfers between devices, shards(): lax.all_to_all(states[layers - 1:], 'layer', 0, 0, tiled=True)[layers - 1]  21.2 us
    all_to_all x1, blocking collectives, shards(): lax.all_to_all(sent, 'col', 0, 0, tiled=True).reshape(cols, 4, ROWS, units)  16.3 us
    all_to_all x1, waiting for transfers between devices, shards(): got = lax.all_to_all(sent, 'col', 0, 0, tiled=True)  12.6 us
    all_to_all x1, starting transfers between devices, shards(): got = lax.all_to_all(sent, 'col', 0, 0, tiled=True)  10.2 us
  transfers between devices with their start and end apart: 18, of which 3 were waited for; matrix products, arithmetic and copies ran while one was open for 2% of the time, Pallas kernels for 16%

profile of v4, /device:TPU:8, one launch (start us, length us, event | category | flops | bytes accessed | tf_op | source)
XLA Modules:
  0.0 355.7 jit_solution(3721753563462758602)
XLA Ops:
  15.1 10.2 %all-to-all-start = ((f32[32,1,2176]{2,1,0:T(1,128)}), f32[32,1,2176]{2,1,0:T(1,128)S(1)}, u32[]{:S(2)}, u32[]{:S(2)}) async-start(f32[32,1,2176]{2,1,0:T(1,128)} %copy.47), calls=%async_computation | async-start | bytes 557056 | tf_op jit(solution)/shard_map/all_to_all | solution.py:195
  25.3 12.6 %all-to-all-done = f32[32,1,2176]{2,1,0:T(1,128)S(1)} async-done(((f32[32,1,2176]{2,1,0:T(1,128)}), f32[32,1,2176]{2,1,0:T(1,128)S(1)}, u32[]{:S(2)}, u32[]{:S(2)}) %all-to-all-start) | async-done | bytes 278560 | tf_op jit(solution)/shard_map/all_to_all | solution.py:195
  39.2 80.1 %all-gather.3.cloned.1.call-done = bf16[65536,128]{1,0:T(8,128)(2,1)} async-done(((bf16[1024,128]{1,0:T(8,128)(2,1)}), bf16[65536,128]{1,0:T(8,128)(2,1)}) %all-gather.3.cloned.1.call-update) | async-done | bytes 16777232 | tf_op jit(solution)/shard_map/all_gather | solution.py:188
  121.0 176.4 %while.21 = (s32[]{:T(128)}, f32[8,128]{1,0:T(8,128)S(1)}, bf16[8,1024]{1,0:T(8,128)(2,1)S(1)}, f32[8,1024]{1,0:T(8,128)S(1)}, f32[8,1024]{1,0:T(8,128)S(1)}, /*...) while((s32[]{:T(128)}, f32[8,128]{1,0:T(8,128)S(1)}, ...), condition=%wide.region_1.2_spmd, body=%wide.region_0.1_spmd.sunk | while | flops 8000000000 | bytes 8098465 | solution.py:215
  124.6 3.9 %eval_jaxpr.6.product = f32[8,4096]{1,0:T(8,128)S(1)} custom-call(f32[8,1024]{1,0:T(8,128)S(1)} %get-tuple-element.290.h_was, bf16[32,2,1024,128]{3,2,1,0:T(8,128)(2,1)} %get-tuple-element.304.weights), custom_call_target="tpu_custom_call" | custom-call | flops 8000000000 | bytes 8000000 | tf_op jit(solution)/shard_map/while/body/eval_jaxpr/pallas_call | solution.py:135
  128.5 7.1 %eval_jaxpr.7 = (f32[8,128]{1,0:T(8,128)S(1)}, bf16[8,1024]{1,0:T(8,128)(2,1)S(1)}, bf16[8,1024]{1,0:T(8,128)(2,1)S(1)}, f32[8,1024]{1,0:T(8,128)S(1)}, f32[8,1024]{1,0:T(8,128)S(1)}) custom-call(f32[8,128]{1,0:T(8,128)S(1)} %get-tuple-element.288.place, ...), custom_call_target="tpu_custom_call", output_to_operand_aliasing={{0}: (0, {}), {3}: (4, {}), {4}: (5, {})} | custom-call | tf_op jit(solution)/shard_map/while/body/eval_jaxpr/pallas_call | solution.py:161
  136.9 3.9 %eval_jaxpr.6.product = f32[8,4096]{1,0:T(8,128)S(1)} custom-call(f32[8,1024]{1,0:T(8,128)S(1)} %get-tuple-element.290.h_was, bf16[32,2,1024,128]{3,2,1,0:T(8,128)(2,1)} %get-tuple-element.304.weights), custom_call_target="tpu_custom_call" | custom-call | flops 8000000000 | bytes 8000000 | tf_op jit(solution)/shard_map/while/body/eval_jaxpr/pallas_call | solution.py:135
  140.8 7.1 %eval_jaxpr.7 = (f32[8,128]{1,0:T(8,128)S(1)}, bf16[8,1024]{1,0:T(8,128)(2,1)S(1)}, bf16[8,1024]{1,0:T(8,128)(2,1)S(1)}, f32[8,1024]{1,0:T(8,128)S(1)}, f32[8,1024]{1,0:T(8,128)S(1)}) custom-call(f32[8,128]{1,0:T(8,128)S(1)} %get-tuple-element.288.place, ...), custom_call_target="tpu_custom_call", output_to_operand_aliasing={{0}: (0, {}), {3}: (4, {}), {4}: (5, {})} | custom-call | tf_op jit(solution)/shard_map/while/body/eval_jaxpr/pallas_call | solution.py:161
  149.7 3.9 %eval_jaxpr.6.product = f32[8,4096]{1,0:T(8,128)S(1)} custom-call(f32[8,1024]{1,0:T(8,128)S(1)} %get-tuple-element.290.h_was, bf16[32,2,1024,128]{3,2,1,0:T(8,128)(2,1)} %get-tuple-element.304.weights), custom_call_target="tpu_custom_call" | custom-call | flops 8000000000 | bytes 8000000 | tf_op jit(solution)/shard_map/while/body/eval_jaxpr/pallas_call | solution.py:135
  153.6 7.1 %eval_jaxpr.7 = (f32[8,128]{1,0:T(8,128)S(1)}, bf16[8,1024]{1,0:T(8,128)(2,1)S(1)}, bf16[8,1024]{1,0:T(8,128)(2,1)S(1)}, f32[8,1024]{1,0:T(8,128)S(1)}, f32[8,1024]{1,0:T(8,128)S(1)}) custom-call(f32[8,128]{1,0:T(8,128)S(1)} %get-tuple-element.288.place, ...), custom_call_target="tpu_custom_call", output_to_operand_aliasing={{0}: (0, {}), {3}: (4, {}), {4}: (5, {})} | custom-call | tf_op jit(solution)/shard_map/while/body/eval_jaxpr/pallas_call | solution.py:161
  162.6 3.9 %eval_jaxpr.6.product = f32[8,4096]{1,0:T(8,128)S(1)} custom-call(f32[8,1024]{1,0:T(8,128)S(1)} %get-tuple-element.290.h_was, bf16[32,2,1024,128]{3,2,1,0:T(8,128)(2,1)} %get-tuple-element.304.weights), custom_call_target="tpu_custom_call" | custom-call | flops 8000000000 | bytes 8000000 | tf_op jit(solution)/shard_map/while/body/eval_jaxpr/pallas_call | solution.py:135
  166.5 7.1 %eval_jaxpr.7 = (f32[8,128]{1,0:T(8,128)S(1)}, bf16[8,1024]{1,0:T(8,128)(2,1)S(1)}, bf16[8,1024]{1,0:T(8,128)(2,1)S(1)}, f32[8,1024]{1,0:T(8,128)S(1)}, f32[8,1024]{1,0:T(8,128)S(1)}) custom-call(f32[8,128]{1,0:T(8,128)S(1)} %get-tuple-element.288.place, ...), custom_call_target="tpu_custom_call", output_to_operand_aliasing={{0}: (0, {}), {3}: (4, {}), {4}: (5, {})} | custom-call | tf_op jit(solution)/shard_map/while/body/eval_jaxpr/pallas_call | solution.py:161
  179.5 7.1 %eval_jaxpr.7 = (f32[8,128]{1,0:T(8,128)S(1)}, bf16[8,1024]{1,0:T(8,128)(2,1)S(1)}, bf16[8,1024]{1,0:T(8,128)(2,1)S(1)}, f32[8,1024]{1,0:T(8,128)S(1)}, f32[8,1024]{1,0:T(8,128)S(1)}) custom-call(f32[8,128]{1,0:T(8,128)S(1)} %get-tuple-element.288.place, ...), custom_call_target="tpu_custom_call", output_to_operand_aliasing={{0}: (0, {}), {3}: (4, {}), {4}: (5, {})} | custom-call | tf_op jit(solution)/shard_map/while/body/eval_jaxpr/pallas_call | solution.py:161
  192.5 7.1 %eval_jaxpr.7 = (f32[8,128]{1,0:T(8,128)S(1)}, bf16[8,1024]{1,0:T(8,128)(2,1)S(1)}, bf16[8,1024]{1,0:T(8,128)(2,1)S(1)}, f32[8,1024]{1,0:T(8,128)S(1)}, f32[8,1024]{1,0:T(8,128)S(1)}) custom-call(f32[8,128]{1,0:T(8,128)S(1)} %get-tuple-element.288.place, ...), custom_call_target="tpu_custom_call", output_to_operand_aliasing={{0}: (0, {}), {3}: (4, {}), {4}: (5, {})} | custom-call | tf_op jit(solution)/shard_map/while/body/eval_jaxpr/pallas_call | solution.py:161
  201.5 3.9 %eval_jaxpr.6.product = f32[8,4096]{1,0:T(8,128)S(1)} custom-call(f32[8,1024]{1,0:T(8,128)S(1)} %get-tuple-element.290.h_was, bf16[32,2,1024,128]{3,2,1,0:T(8,128)(2,1)} %get-tuple-element.304.weights), custom_call_target="tpu_custom_call" | custom-call | flops 8000000000 | bytes 8000000 | tf_op jit(solution)/shard_map/while/body/eval_jaxpr/pallas_call | solution.py:135
  205.4 7.1 %eval_jaxpr.7 = (f32[8,128]{1,0:T(8,128)S(1)}, bf16[8,1024]{1,0:T(8,128)(2,1)S(1)}, bf16[8,1024]{1,0:T(8,128)(2,1)S(1)}, f32[8,1024]{1,0:T(8,128)S(1)}, f32[8,1024]{1,0:T(8,128)S(1)}) custom-call(f32[8,128]{1,0:T(8,128)S(1)} %get-tuple-element.288.place, ...), custom_call_target="tpu_custom_call", output_to_operand_aliasing={{0}: (0, {}), {3}: (4, {}), {4}: (5, {})} | custom-call | tf_op jit(solution)/shard_map/while/body/eval_jaxpr/pallas_call | solution.py:161
  214.5 3.9 %eval_jaxpr.6.product = f32[8,4096]{1,0:T(8,128)S(1)} custom-call(f32[8,1024]{1,0:T(8,128)S(1)} %get-tuple-element.290.h_was, bf16[32,2,1024,128]{3,2,1,0:T(8,128)(2,1)} %get-tuple-element.304.weights), custom_call_target="tpu_custom_call" | custom-call | flops 8000000000 | bytes 8000000 | tf_op jit(solution)/shard_map/while/body/eval_jaxpr/pallas_call | solution.py:135
  218.4 7.1 %eval_jaxpr.7 = (f32[8,128]{1,0:T(8,128)S(1)}, bf16[8,1024]{1,0:T(8,128)(2,1)S(1)}, bf16[8,1024]{1,0:T(8,128)(2,1)S(1)}, f32[8,1024]{1,0:T(8,128)S(1)}, f32[8,1024]{1,0:T(8,128)S(1)}) custom-call(f32[8,128]{1,0:T(8,128)S(1)} %get-tuple-element.288.place, ...), custom_call_target="tpu_custom_call", output_to_operand_aliasing={{0}: (0, {}), {3}: (4, {}), {4}: (5, {})} | custom-call | tf_op jit(solution)/shard_map/while/body/eval_jaxpr/pallas_call | solution.py:161
  232.7 9.3 %collective-permute-start = (bf16[8,1024]{1,0:T(8,128)(2,1)S(1)}, bf16[8,1024]{1,0:T(8,128)(2,1)S(1)}, u32[]{:S(2)}, u32[]{:S(2)}) collective-permute-start(bf16[8,1024]{1,0:T(8,128)(2,1)S(1)} %get-tuple-element.289), channel_id=1, source_target_pairs={{0,32},{32,64},{64,96},{96,128},{128,160},{160,192},{192,224},{1,3... | collective-permute-start | bytes 49160 | tf_op jit(solution)/shard_map/while/body/eval_jaxpr/ppermute | solution.py:20
  254.3 9.3 %collective-permute-start = (bf16[8,1024]{1,0:T(8,128)(2,1)S(1)}, bf16[8,1024]{1,0:T(8,128)(2,1)S(1)}, u32[]{:S(2)}, u32[]{:S(2)}) collective-permute-start(bf16[8,1024]{1,0:T(8,128)(2,1)S(1)} %get-tuple-element.289), channel_id=1, source_target_pairs={{0,32},{32,64},{64,96},{96,128},{128,160},{160,192},{192,224},{1,3... | collective-permute-start | bytes 49160 | tf_op jit(solution)/shard_map/while/body/eval_jaxpr/ppermute | solution.py:20
  275.8 9.3 %collective-permute-start = (bf16[8,1024]{1,0:T(8,128)(2,1)S(1)}, bf16[8,1024]{1,0:T(8,128)(2,1)S(1)}, u32[]{:S(2)}, u32[]{:S(2)}) collective-permute-start(bf16[8,1024]{1,0:T(8,128)(2,1)S(1)} %get-tuple-element.289), channel_id=1, source_target_pairs={{0,32},{32,64},{64,96},{96,128},{128,160},{160,192},{192,224},{1,3... | collective-permute-start | bytes 49160 | tf_op jit(solution)/shard_map/while/body/eval_jaxpr/ppermute | solution.py:20
  298.0 21.2 %all-to-all-start.1 = ((bf16[8,8,1024]{2,1,0:T(8,128)(2,1)}), bf16[8,8,1024]{2,1,0:T(8,128)(2,1)S(1)}, u32[]{:S(2)}, u32[]{:S(2)}) async-start(bf16[8,8,1024]{2,1,0:T(8,128)(2,1)} %slice.37), calls=%async_computation.1 | async-start | bytes 262144 | tf_op jit(solution)/shard_map/all_to_all | solution.py:217
  319.2 9.1 %all-to-all-done.1 = bf16[8,8,1024]{2,1,0:T(8,128)(2,1)S(1)} async-done(((bf16[8,8,1024]{2,1,0:T(8,128)(2,1)}), bf16[8,8,1024]{2,1,0:T(8,128)(2,1)S(1)}, u32[]{:S(2)}, u32[]{:S(2)}) %all-to-all-start.1) | async-done | bytes 131104 | tf_op jit(solution)/shard_map/all_to_all | solution.py:217
  328.7 16.3 %all_to_all.22 = f32[32,1,512]{2,1,0:T(1,128)S(1)} all-to-all(f32[32,1,512]{2,1,0:T(1,128)S(1)} %reshape.112), channel_id=1, replica_groups=mesh['dp'=2,'layer'=8,'col'=32] {'col'}, dimensions={0} | all-to-all | bytes 131072 | tf_op jit(solution)/shard_map/all_to_all | solution.py:220
  (109 shorter events, 83.3 us)
Async XLA Ops:
  7.2 112.2 %all-gather.3.cloned.1.call-start = ((), (), s32[]{:S(2)}) async-start(), calls=%async_computation.3 | async-start | bytes 17039360 | tf_op jit(solution)/shard_map/all_gather | solution.py:188
  15.1 22.8 %all-to-all-start = ((f32[32,1,2176]{2,1,0:T(1,128)}), f32[32,1,2176]{2,1,0:T(1,128)S(1)}, u32[]{:S(2)}, u32[]{:S(2)}) async-start(f32[32,1,2176]{2,1,0:T(1,128)} %copy.47), calls=%async_computation | async-start | bytes 557056 | tf_op jit(solution)/shard_map/all_to_all | solution.py:195
  121.0 7.5 %collective-permute-start = (bf16[8,1024]{1,0:T(8,128)(2,1)S(1)}, bf16[8,1024]{1,0:T(8,128)(2,1)S(1)}, u32[]{:S(2)}, u32[]{:S(2)}) collective-permute-start(bf16[8,1024]{1,0:T(8,128)(2,1)S(1)} %get-tuple-element.289), channel_id=1, source_target_pairs={{0,32},{32,64},{64,96},{96,128},{128,160},{160,192},{192,224},{1,3... | collective-permute-start | bytes 49160 | tf_op jit(solution)/shard_map/while/body/eval_jaxpr/ppermute | solution.py:20
  135.6 5.2 %collective-permute-start = (bf16[8,1024]{1,0:T(8,128)(2,1)S(1)}, bf16[8,1024]{1,0:T(8,128)(2,1)S(1)}, u32[]{:S(2)}, u32[]{:S(2)}) collective-permute-start(bf16[8,1024]{1,0:T(8,128)(2,1)S(1)} %get-tuple-element.289), channel_id=1, source_target_pairs={{0,32},{32,64},{64,96},{96,128},{128,160},{160,192},{192,224},{1,3... | collective-permute-start | bytes 49160 | tf_op jit(solution)/shard_map/while/body/eval_jaxpr/ppermute | solution.py:20
  147.9 5.6 %collective-permute-start = (bf16[8,1024]{1,0:T(8,128)(2,1)S(1)}, bf16[8,1024]{1,0:T(8,128)(2,1)S(1)}, u32[]{:S(2)}, u32[]{:S(2)}) collective-permute-start(bf16[8,1024]{1,0:T(8,128)(2,1)S(1)} %get-tuple-element.289), channel_id=1, source_target_pairs={{0,32},{32,64},{64,96},{96,128},{128,160},{160,192},{192,224},{1,3... | collective-permute-start | bytes 49160 | tf_op jit(solution)/shard_map/while/body/eval_jaxpr/ppermute | solution.py:20
  160.7 5.8 %collective-permute-start = (bf16[8,1024]{1,0:T(8,128)(2,1)S(1)}, bf16[8,1024]{1,0:T(8,128)(2,1)S(1)}, u32[]{:S(2)}, u32[]{:S(2)}) collective-permute-start(bf16[8,1024]{1,0:T(8,128)(2,1)S(1)} %get-tuple-element.289), channel_id=1, source_target_pairs={{0,32},{32,64},{64,96},{96,128},{128,160},{160,192},{192,224},{1,3... | collective-permute-start | bytes 49160 | tf_op jit(solution)/shard_map/while/body/eval_jaxpr/ppermute | solution.py:20
  173.7 5.8 %collective-permute-start = (bf16[8,1024]{1,0:T(8,128)(2,1)S(1)}, bf16[8,1024]{1,0:T(8,128)(2,1)S(1)}, u32[]{:S(2)}, u32[]{:S(2)}) collective-permute-start(bf16[8,1024]{1,0:T(8,128)(2,1)S(1)} %get-tuple-element.289), channel_id=1, source_target_pairs={{0,32},{32,64},{64,96},{96,128},{128,160},{160,192},{192,224},{1,3... | collective-permute-start | bytes 49160 | tf_op jit(solution)/shard_map/while/body/eval_jaxpr/ppermute | solution.py:20
  186.6 5.8 %collective-permute-start = (bf16[8,1024]{1,0:T(8,128)(2,1)S(1)}, bf16[8,1024]{1,0:T(8,128)(2,1)S(1)}, u32[]{:S(2)}, u32[]{:S(2)}) collective-permute-start(bf16[8,1024]{1,0:T(8,128)(2,1)S(1)} %get-tuple-element.289), channel_id=1, source_target_pairs={{0,32},{32,64},{64,96},{96,128},{128,160},{160,192},{192,224},{1,3... | collective-permute-start | bytes 49160 | tf_op jit(solution)/shard_map/while/body/eval_jaxpr/ppermute | solution.py:20
  199.6 5.8 %collective-permute-start = (bf16[8,1024]{1,0:T(8,128)(2,1)S(1)}, bf16[8,1024]{1,0:T(8,128)(2,1)S(1)}, u32[]{:S(2)}, u32[]{:S(2)}) collective-permute-start(bf16[8,1024]{1,0:T(8,128)(2,1)S(1)} %get-tuple-element.289), channel_id=1, source_target_pairs={{0,32},{32,64},{64,96},{96,128},{128,160},{160,192},{192,224},{1,3... | collective-permute-start | bytes 49160 | tf_op jit(solution)/shard_map/while/body/eval_jaxpr/ppermute | solution.py:20
  212.6 5.8 %collective-permute-start = (bf16[8,1024]{1,0:T(8,128)(2,1)S(1)}, bf16[8,1024]{1,0:T(8,128)(2,1)S(1)}, u32[]{:S(2)}, u32[]{:S(2)}) collective-permute-start(bf16[8,1024]{1,0:T(8,128)(2,1)S(1)} %get-tuple-element.289), channel_id=1, source_target_pairs={{0,32},{32,64},{64,96},{96,128},{128,160},{160,192},{192,224},{1,3... | collective-permute-start | bytes 49160 | tf_op jit(solution)/shard_map/while/body/eval_jaxpr/ppermute | solution.py:20
  225.5 6.4 %collective-permute-start = (bf16[8,1024]{1,0:T(8,128)(2,1)S(1)}, bf16[8,1024]{1,0:T(8,128)(2,1)S(1)}, u32[]{:S(2)}, u32[]{:S(2)}) collective-permute-start(bf16[8,1024]{1,0:T(8,128)(2,1)S(1)} %get-tuple-element.289), channel_id=1, source_target_pairs={{0,32},{32,64},{64,96},{96,128},{128,160},{160,192},{192,224},{1,3... | collective-permute-start | bytes 49160 | tf_op jit(solution)/shard_map/while/body/eval_jaxpr/ppermute | solution.py:20
  232.7 13.2 %collective-permute-start = (bf16[8,1024]{1,0:T(8,128)(2,1)S(1)}, bf16[8,1024]{1,0:T(8,128)(2,1)S(1)}, u32[]{:S(2)}, u32[]{:S(2)}) collective-permute-start(bf16[8,1024]{1,0:T(8,128)(2,1)S(1)} %get-tuple-element.289), channel_id=1, source_target_pairs={{0,32},{32,64},{64,96},{96,128},{128,160},{160,192},{192,224},{1,3... | collective-permute-start | bytes 49160 | tf_op jit(solution)/shard_map/while/body/eval_jaxpr/ppermute | solution.py:20
  246.7 6.8 %collective-permute-start = (bf16[8,1024]{1,0:T(8,128)(2,1)S(1)}, bf16[8,1024]{1,0:T(8,128)(2,1)S(1)}, u32[]{:S(2)}, u32[]{:S(2)}) collective-permute-start(bf16[8,1024]{1,0:T(8,128)(2,1)S(1)} %get-tuple-element.289), channel_id=1, source_target_pairs={{0,32},{32,64},{64,96},{96,128},{128,160},{160,192},{192,224},{1,3... | collective-permute-start | bytes 49160 | tf_op jit(solution)/shard_map/while/body/eval_jaxpr/ppermute | solution.py:20
  254.3 13.2 %collective-permute-start = (bf16[8,1024]{1,0:T(8,128)(2,1)S(1)}, bf16[8,1024]{1,0:T(8,128)(2,1)S(1)}, u32[]{:S(2)}, u32[]{:S(2)}) collective-permute-start(bf16[8,1024]{1,0:T(8,128)(2,1)S(1)} %get-tuple-element.289), channel_id=1, source_target_pairs={{0,32},{32,64},{64,96},{96,128},{128,160},{160,192},{192,224},{1,3... | collective-permute-start | bytes 49160 | tf_op jit(solution)/shard_map/while/body/eval_jaxpr/ppermute | solution.py:20
  268.2 6.8 %collective-permute-start = (bf16[8,1024]{1,0:T(8,128)(2,1)S(1)}, bf16[8,1024]{1,0:T(8,128)(2,1)S(1)}, u32[]{:S(2)}, u32[]{:S(2)}) collective-permute-start(bf16[8,1024]{1,0:T(8,128)(2,1)S(1)} %get-tuple-element.289), channel_id=1, source_target_pairs={{0,32},{32,64},{64,96},{96,128},{128,160},{160,192},{192,224},{1,3... | collective-permute-start | bytes 49160 | tf_op jit(solution)/shard_map/while/body/eval_jaxpr/ppermute | solution.py:20
  275.8 13.2 %collective-permute-start = (bf16[8,1024]{1,0:T(8,128)(2,1)S(1)}, bf16[8,1024]{1,0:T(8,128)(2,1)S(1)}, u32[]{:S(2)}, u32[]{:S(2)}) collective-permute-start(bf16[8,1024]{1,0:T(8,128)(2,1)S(1)} %get-tuple-element.289), channel_id=1, source_target_pairs={{0,32},{32,64},{64,96},{96,128},{128,160},{160,192},{192,224},{1,3... | collective-permute-start | bytes 49160 | tf_op jit(solution)/shard_map/while/body/eval_jaxpr/ppermute | solution.py:20
  289.8 6.8 %collective-permute-start = (bf16[8,1024]{1,0:T(8,128)(2,1)S(1)}, bf16[8,1024]{1,0:T(8,128)(2,1)S(1)}, u32[]{:S(2)}, u32[]{:S(2)}) collective-permute-start(bf16[8,1024]{1,0:T(8,128)(2,1)S(1)} %get-tuple-element.289), channel_id=1, source_target_pairs={{0,32},{32,64},{64,96},{96,128},{128,160},{160,192},{192,224},{1,3... | collective-permute-start | bytes 49160 | tf_op jit(solution)/shard_map/while/body/eval_jaxpr/ppermute | solution.py:20
  298.0 30.2 %all-to-all-start.1 = ((bf16[8,8,1024]{2,1,0:T(8,128)(2,1)}), bf16[8,8,1024]{2,1,0:T(8,128)(2,1)S(1)}, u32[]{:S(2)}, u32[]{:S(2)}) async-start(bf16[8,8,1024]{2,1,0:T(8,128)(2,1)} %slice.37), calls=%async_computation.1 | async-start | bytes 262144 | tf_op jit(solution)/shard_map/all_to_all | solution.py:217
Sparse Core Ops, SparseCore 0:
  11.3 107.9 all-gather.2

commit v5 on v4

--- a/solution.py
+++ b/solution.py
@@ -204,17 +204,19 @@
         place, hs, x_next, hidden, cell = late(
             place, x_got, x_first, product, hidden, cell, bias_full, kept, weights
         )
-        states = lax.dynamic_update_index_in_dim(states, hs, s, 0)
+        states = lax.dynamic_update_index_in_dim(states, hs, jnp.maximum(s - (layers - 2), 0), 0)
         return place, x_next, hidden, cell, states
 
     row = jnp.arange(2 * ROWS)[:, None]
     place = jnp.where(row < 4, -level, level) * jnp.ones((1, LANES), jnp.float32)
     zero_x = jnp.zeros((STEPS * ROWS, H), jnp.bfloat16)
     zero_s = jnp.zeros((STEPS * ROWS, H), jnp.float32)
-    zero_t = jnp.zeros((stages, STEPS * ROWS, H), jnp.bfloat16)
-    _, _, hidden, cell, states = lax.fori_loop(0, stages, section, (place, zero_x, zero_s, zero_s, zero_t))
-
-    top = lax.all_to_all(states[layers - 1 :], "layer", 0, 0, tiled=True)[layers - 1]
+    zero_t = jnp.zeros((chunks + 1, STEPS * ROWS, H), jnp.bfloat16)
+    carry = lax.fori_loop(0, stages - 1, section, (place, zero_x, zero_s, zero_s, zero_t))
+
+    moved = lax.all_to_all(carry[4][1:], "layer", 0, 0, tiled=True)[layers - 1]
+    _, _, hidden, cell, states = section(stages - 1, carry)
+    top = jnp.where(level == layers - 1, states[chunks], moved)
     rows = jnp.concatenate([top.astype(jnp.float32), hidden[:ROWS], cell[:ROWS]], axis=0)
     sent = rows.reshape(4 * ROWS, cols, units).transpose(1, 0, 2)
     got = lax.all_to_all(sent, "col", 0, 0, tiled=True).reshape(cols, 4, ROWS, units).transpose(1, 0, 2, 3)

time: 357 us -> 354 us (level)
  the two profiles are of different devices: /device:TPU:8 before, /device:TPU:448 now
where the time goes in v5:
time: 354 us; the launch traced here: 353 us
  waiting for transfers between devices  140 us (40%)
  Pallas kernels  126 us (36%)
  starting transfers between devices  38.6 us (11%)
  blocking collectives  15.5 us (4%)
  between operations  14.3 us (4%)
  local copies, waits for them, and re-layouts  14.1 us (4%)
    all_gather x1, waiting for transfers between devices, shards(): weights = lax.all_gather(half, ('col', 'dp')).reshape(cols, 2, H, 4 * units)  75.3 us
    pallas_call x15, Pallas kernels, late(): pl.pallas_call(late_kernel, out_shape=(like(place), like(x_got), like(x_g...  65.7 us
    pallas_call x15, Pallas kernels, early(): pl.pallas_call(early_kernel, out_shape=jax.ShapeDtypeStruct((2 * ROWS, 4...  58.5 us
    ppermute x15, waiting for transfers between devices, passed_along(): return lax.ppermute(block, axis, route)  50.4 us
    ppermute x15, starting transfers between devices, passed_along(): return lax.ppermute(block, axis, route)  19.4 us
    all_to_all x1, blocking collectives, shards(): lax.all_to_all(sent, 'col', 0, 0, tiled=True).reshape(cols, 4, ROWS, units)  15.5 us
    all_to_all x1, waiting for transfers between devices, shards(): got = lax.all_to_all(sent, 'col', 0, 0, tiled=True)  14 us
    all_to_all x1, starting transfers between devices, shards(): got = lax.all_to_all(sent, 'col', 0, 0, tiled=True)  9.95 us
  transfers between devices with their start and end apart: 18, of which 16 were waited for; matrix products, arithmetic and copies ran while one was open for 2% of the time, Pallas kernels for 20%

profile of v5, /device:TPU:448, one launch (start us, length us, event | category | flops | bytes accessed | tf_op | source)
XLA Modules:
  0.0 353.0 jit_solution(448609799120525133)
XLA Ops:
  15.1 9.9 %all-to-all-start = ((f32[32,1,2176]{2,1,0:T(1,128)}), f32[32,1,2176]{2,1,0:T(1,128)S(1)}, u32[]{:S(2)}, u32[]{:S(2)}) async-start(f32[32,1,2176]{2,1,0:T(1,128)} %copy.36), calls=%async_computation | async-start | bytes 557056 | tf_op jit(solution)/shard_map/all_to_all | solution.py:195
  25.1 14.0 %all-to-all-done = f32[32,1,2176]{2,1,0:T(1,128)S(1)} async-done(((f32[32,1,2176]{2,1,0:T(1,128)}), f32[32,1,2176]{2,1,0:T(1,128)S(1)}, u32[]{:S(2)}, u32[]{:S(2)}) %all-to-all-start) | async-done | bytes 278560 | tf_op jit(solution)/shard_map/all_to_all | solution.py:195
  40.5 75.3 %all-gather.3.cloned.1.call-done = bf16[65536,128]{1,0:T(8,128)(2,1)} async-done(((bf16[1024,128]{1,0:T(8,128)(2,1)}), bf16[65536,128]{1,0:T(8,128)(2,1)}) %all-gather.3.cloned.1.call-update) | async-done | bytes 16777232 | tf_op jit(solution)/shard_map/all_gather | solution.py:188
  117.4 178.3 %while.23 = (s32[]{:T(128)}, f32[8,128]{1,0:T(8,128)S(1)}, bf16[8,1024]{1,0:T(8,128)(2,1)S(1)}, f32[8,1024]{1,0:T(8,128)S(1)}, f32[8,1024]{1,0:T(8,128)S(1)}, /*...) while((s32[]{:T(128)}, f32[8,128]{1,0:T(8,128)S(1)}, ...), condition=%wide.region_1.2_spmd, body=%wide.region_0.1_spmd.sunk | while | flops 8000000000 | bytes 8098505 | solution.py:215
  118.7 3.9 %eval_jaxpr.9.product = f32[8,4096]{1,0:T(8,128)S(1)} custom-call(f32[8,1024]{1,0:T(8,128)S(1)} %get-tuple-element.384.h_was, bf16[32,2,1024,128]{3,2,1,0:T(8,128)(2,1)} %get-tuple-element.400.weights), custom_call_target="tpu_custom_call" | custom-call | flops 8000000000 | bytes 8000000 | tf_op jit(solution)/shard_map/while/body/eval_jaxpr/pallas_call | solution.py:135
  138.3 3.9 %eval_jaxpr.9.product = f32[8,4096]{1,0:T(8,128)S(1)} custom-call(f32[8,1024]{1,0:T(8,128)S(1)} %get-tuple-element.384.h_was, bf16[32,2,1024,128]{3,2,1,0:T(8,128)(2,1)} %get-tuple-element.400.weights), custom_call_target="tpu_custom_call" | custom-call | flops 8000000000 | bytes 8000000 | tf_op jit(solution)/shard_map/while/body/eval_jaxpr/pallas_call | solution.py:135
  144.9 3.9 %eval_jaxpr.9.product = f32[8,4096]{1,0:T(8,128)S(1)} custom-call(f32[8,1024]{1,0:T(8,128)S(1)} %get-tuple-element.384.h_was, bf16[32,2,1024,128]{3,2,1,0:T(8,128)(2,1)} %get-tuple-element.400.weights), custom_call_target="tpu_custom_call" | custom-call | flops 8000000000 | bytes 8000000 | tf_op jit(solution)/shard_map/while/body/eval_jaxpr/pallas_call | solution.py:135
  151.5 3.9 %eval_jaxpr.9.product = f32[8,4096]{1,0:T(8,128)S(1)} custom-call(f32[8,1024]{1,0:T(8,128)S(1)} %get-tuple-element.384.h_was, bf16[32,2,1024,128]{3,2,1,0:T(8,128)(2,1)} %get-tuple-element.400.weights), custom_call_target="tpu_custom_call" | custom-call | flops 8000000000 | bytes 8000000 | tf_op jit(solution)/shard_map/while/body/eval_jaxpr/pallas_call | solution.py:135
  158.4 3.9 %eval_jaxpr.9.product = f32[8,4096]{1,0:T(8,128)S(1)} custom-call(f32[8,1024]{1,0:T(8,128)S(1)} %get-tuple-element.384.h_was, bf16[32,2,1024,128]{3,2,1,0:T(8,128)(2,1)} %get-tuple-element.400.weights), custom_call_target="tpu_custom_call" | custom-call | flops 8000000000 | bytes 8000000 | tf_op jit(solution)/shard_map/while/body/eval_jaxpr/pallas_call | solution.py:135
  169.9 34.9 %collective-permute-done.x_got = bf16[8,1024]{1,0:T(8,128)(2,1)S(1)} collective-permute-done((bf16[8,1024]{1,0:T(8,128)(2,1)S(1)}, bf16[8,1024]{1,0:T(8,128)(2,1)S(1)}, u32[]{:S(2)}, u32[]{:S(2)}) %collective-permute-start) | collective-permute-done | bytes 16416 | tf_op jit(solution)/shard_map/while/body/eval_jaxpr/ppermute | solution.py:20
  204.8 7.1 %eval_jaxpr.10 = (f32[8,128]{1,0:T(8,128)S(1)}, bf16[8,1024]{1,0:T(8,128)(2,1)S(1)}, bf16[8,1024]{1,0:T(8,128)(2,1)S(1)}, f32[8,1024]{1,0:T(8,128)S(1)}, f32[8,1024]{1,0:T(8,128)S(1)}) custom-call(f32[8,128]{1,0:T(8,128)S(1)} %get-tuple-element.382.place, ...), custom_call_target="tpu_custom_call", output_to_operand_aliasing={{0}: (0, {}), {3}: (4, {}), {4}: (5, {})} | custom-call | tf_op jit(solution)/shard_map/while/body/eval_jaxpr/pallas_call | solution.py:161
  213.3 3.9 %eval_jaxpr.9.product = f32[8,4096]{1,0:T(8,128)S(1)} custom-call(f32[8,1024]{1,0:T(8,128)S(1)} %get-tuple-element.384.h_was, bf16[32,2,1024,128]{3,2,1,0:T(8,128)(2,1)} %get-tuple-element.400.weights), custom_call_target="tpu_custom_call" | custom-call | flops 8000000000 | bytes 8000000 | tf_op jit(solution)/shard_map/while/body/eval_jaxpr/pallas_call | solution.py:135
  218.8 7.1 %eval_jaxpr.10 = (f32[8,128]{1,0:T(8,128)S(1)}, bf16[8,1024]{1,0:T(8,128)(2,1)S(1)}, bf16[8,1024]{1,0:T(8,128)(2,1)S(1)}, f32[8,1024]{1,0:T(8,128)S(1)}, f32[8,1024]{1,0:T(8,128)S(1)}) custom-call(f32[8,128]{1,0:T(8,128)S(1)} %get-tuple-element.382.place, ...), custom_call_target="tpu_custom_call", output_to_operand_aliasing={{0}: (0, {}), {3}: (4, {}), {4}: (5, {})} | custom-call | tf_op jit(solution)/shard_map/while/body/eval_jaxpr/pallas_call | solution.py:161
  227.2 3.9 %eval_jaxpr.9.product = f32[8,4096]{1,0:T(8,128)S(1)} custom-call(f32[8,1024]{1,0:T(8,128)S(1)} %get-tuple-element.384.h_was, bf16[32,2,1024,128]{3,2,1,0:T(8,128)(2,1)} %get-tuple-element.400.weights), custom_call_target="tpu_custom_call" | custom-call | flops 8000000000 | bytes 8000000 | tf_op jit(solution)/shard_map/while/body/eval_jaxpr/pallas_call | solution.py:135
  232.8 7.1 %eval_jaxpr.10 = (f32[8,128]{1,0:T(8,128)S(1)}, bf16[8,1024]{1,0:T(8,128)(2,1)S(1)}, bf16[8,1024]{1,0:T(8,128)(2,1)S(1)}, f32[8,1024]{1,0:T(8,128)S(1)}, f32[8,1024]{1,0:T(8,128)S(1)}) custom-call(f32[8,128]{1,0:T(8,128)S(1)} %get-tuple-element.382.place, ...), custom_call_target="tpu_custom_call", output_to_operand_aliasing={{0}: (0, {}), {3}: (4, {}), {4}: (5, {})} | custom-call | tf_op jit(solution)/shard_map/while/body/eval_jaxpr/pallas_call | solution.py:161
  246.7 7.1 %eval_jaxpr.10 = (f32[8,128]{1,0:T(8,128)S(1)}, bf16[8,1024]{1,0:T(8,128)(2,1)S(1)}, bf16[8,1024]{1,0:T(8,128)(2,1)S(1)}, f32[8,1024]{1,0:T(8,128)S(1)}, f32[8,1024]{1,0:T(8,128)S(1)}) custom-call(f32[8,128]{1,0:T(8,128)S(1)} %get-tuple-element.382.place, ...), custom_call_target="tpu_custom_call", output_to_operand_aliasing={{0}: (0, {}), {3}: (4, {}), {4}: (5, {})} | custom-call | tf_op jit(solution)/shard_map/while/body/eval_jaxpr/pallas_call | solution.py:161
  260.7 7.1 %eval_jaxpr.10 = (f32[8,128]{1,0:T(8,128)S(1)}, bf16[8,1024]{1,0:T(8,128)(2,1)S(1)}, bf16[8,1024]{1,0:T(8,128)(2,1)S(1)}, f32[8,1024]{1,0:T(8,128)S(1)}, f32[8,1024]{1,0:T(8,128)S(1)}) custom-call(f32[8,128]{1,0:T(8,128)S(1)} %get-tuple-element.382.place, ...), custom_call_target="tpu_custom_call", output_to_operand_aliasing={{0}: (0, {}), {3}: (4, {}), {4}: (5, {})} | custom-call | tf_op jit(solution)/shard_map/while/body/eval_jaxpr/pallas_call | solution.py:161
  274.7 7.1 %eval_jaxpr.10 = (f32[8,128]{1,0:T(8,128)S(1)}, bf16[8,1024]{1,0:T(8,128)(2,1)S(1)}, bf16[8,1024]{1,0:T(8,128)(2,1)S(1)}, f32[8,1024]{1,0:T(8,128)S(1)}, f32[8,1024]{1,0:T(8,128)S(1)}) custom-call(f32[8,128]{1,0:T(8,128)S(1)} %get-tuple-element.382.place, ...), custom_call_target="tpu_custom_call", output_to_operand_aliasing={{0}: (0, {}), {3}: (4, {}), {4}: (5, {})} | custom-call | tf_op jit(solution)/shard_map/while/body/eval_jaxpr/pallas_call | solution.py:161
  288.6 7.1 %eval_jaxpr.10 = (f32[8,128]{1,0:T(8,128)S(1)}, bf16[8,1024]{1,0:T(8,128)(2,1)S(1)}, bf16[8,1024]{1,0:T(8,128)(2,1)S(1)}, f32[8,1024]{1,0:T(8,128)S(1)}, f32[8,1024]{1,0:T(8,128)S(1)}) custom-call(f32[8,128]{1,0:T(8,128)S(1)} %get-tuple-element.382.place, ...), custom_call_target="tpu_custom_call", output_to_operand_aliasing={{0}: (0, {}), {3}: (4, {}), {4}: (5, {})} | custom-call | tf_op jit(solution)/shard_map/while/body/eval_jaxpr/pallas_call | solution.py:161
  297.7 9.3 %all-to-all-start.1 = ((bf16[8,8,1024]{2,1,0:T(8,128)(2,1)}), bf16[8,8,1024]{2,1,0:T(8,128)(2,1)S(1)}, u32[]{:S(2)}, u32[]{:S(2)}) async-start(bf16[8,8,1024]{2,1,0:T(8,128)(2,1)} %slice.38), calls=%async_computation.1 | async-start | bytes 262144 | tf_op jit(solution)/shard_map/all_to_all | solution.py:217
  307.0 4.0 %shard_map.68.product = f32[8,4096]{1,0:T(8,128)S(1)} custom-call(f32[8,1024]{1,0:T(8,128)S(1)} %get-tuple-element.262.h_was, bf16[32,2,1024,128]{3,2,1,0:T(8,128)(2,1)} %get-tuple-element.411), custom_call_target="tpu_custom_call" | custom-call | flops 8000000000 | bytes 8000000 | tf_op jit(solution)/shard_map/pallas_call | solution.py:135
  311.0 4.2 %copy-done = bf16[32,2,1024,128]{3,2,1,0:T(8,128)(2,1)S(1)} copy-done((bf16[32,2,1024,128]{3,2,1,0:T(8,128)(2,1)S(1)}, bf16[32,2,1024,128]{3,2,1,0:T(8,128)(2,1)}, u32[]{:S(2)}) %copy-start) | copy-done | bytes 16777240
  315.2 11.1 %shard_map.69 = (f32[8,128]{1,0:T(8,128)S(1)}, bf16[8,1024]{1,0:T(8,128)(2,1)S(1)}, bf16[8,1024]{1,0:T(8,128)(2,1)}, f32[8,1024]{1,0:T(8,128)S(1)}, f32[8,1024]{1,0:T(8,128)S(1)}) custom-call(f32[8,128]{1,0:T(8,128)S(1)} %get-tuple-element.260.place, ...), custom_call_target="tpu_custom_call", output_to_operand_aliasing={{0}: (0, {}), {3}: (4, {}), {4}: (5, {})} | custom-call | tf_op jit(solution)/shard_map/pallas_call | solution.py:161
  326.9 15.5 %all_to_all.22 = f32[32,1,512]{2,1,0:T(1,128)S(1)} all-to-all(f32[32,1,512]{2,1,0:T(1,128)S(1)} %reshape.110), channel_id=1, replica_groups=mesh['dp'=2,'layer'=8,'col'=32] {'col'}, dimensions={0} | all-to-all | bytes 131072 | tf_op jit(solution)/shard_map/all_to_all | solution.py:222
  (110 shorter events, 82.8 us)
Async XLA Ops:
  7.2 108.6 %all-gather.3.cloned.1.call-start = ((), (), s32[]{:S(2)}) async-start(), calls=%async_computation.3 | async-start | bytes 17039360 | tf_op jit(solution)/shard_map/all_gather | solution.py:188
  15.1 24.0 %all-to-all-start = ((f32[32,1,2176]{2,1,0:T(1,128)}), f32[32,1,2176]{2,1,0:T(1,128)S(1)}, u32[]{:S(2)}, u32[]{:S(2)}) async-start(f32[32,1,2176]{2,1,0:T(1,128)} %copy.36), calls=%async_computation | async-start | bytes 557056 | tf_op jit(solution)/shard_map/all_to_all | solution.py:195
  117.4 5.6 %collective-permute-start = (bf16[8,1024]{1,0:T(8,128)(2,1)S(1)}, bf16[8,1024]{1,0:T(8,128)(2,1)S(1)}, u32[]{:S(2)}, u32[]{:S(2)}) collective-permute-start(bf16[8,1024]{1,0:T(8,128)(2,1)S(1)} %get-tuple-element.383), channel_id=1, source_target_pairs={{0,32},{32,64},{64,96},{96,128},{128,160},{160,192},{192,224},{1,3... | collective-permute-start | bytes 49160 | tf_op jit(solution)/shard_map/while/body/eval_jaxpr/ppermute | solution.py:20
  123.8 5.8 %collective-permute-start = (bf16[8,1024]{1,0:T(8,128)(2,1)S(1)}, bf16[8,1024]{1,0:T(8,128)(2,1)S(1)}, u32[]{:S(2)}, u32[]{:S(2)}) collective-permute-start(bf16[8,1024]{1,0:T(8,128)(2,1)S(1)} %get-tuple-element.383), channel_id=1, source_target_pairs={{0,32},{32,64},{64,96},{96,128},{128,160},{160,192},{192,224},{1,3... | collective-permute-start | bytes 49160 | tf_op jit(solution)/shard_map/while/body/eval_jaxpr/ppermute | solution.py:20
  130.4 5.8 %collective-permute-start = (bf16[8,1024]{1,0:T(8,128)(2,1)S(1)}, bf16[8,1024]{1,0:T(8,128)(2,1)S(1)}, u32[]{:S(2)}, u32[]{:S(2)}) collective-permute-start(bf16[8,1024]{1,0:T(8,128)(2,1)S(1)} %get-tuple-element.383), channel_id=1, source_target_pairs={{0,32},{32,64},{64,96},{96,128},{128,160},{160,192},{192,224},{1,3... | collective-permute-start | bytes 49160 | tf_op jit(solution)/shard_map/while/body/eval_jaxpr/ppermute | solution.py:20
  137.0 5.8 %collective-permute-start = (bf16[8,1024]{1,0:T(8,128)(2,1)S(1)}, bf16[8,1024]{1,0:T(8,128)(2,1)S(1)}, u32[]{:S(2)}, u32[]{:S(2)}) collective-permute-start(bf16[8,1024]{1,0:T(8,128)(2,1)S(1)} %get-tuple-element.383), channel_id=1, source_target_pairs={{0,32},{32,64},{64,96},{96,128},{128,160},{160,192},{192,224},{1,3... | collective-permute-start | bytes 49160 | tf_op jit(solution)/shard_map/while/body/eval_jaxpr/ppermute | solution.py:20
  143.6 5.8 %collective-permute-start = (bf16[8,1024]{1,0:T(8,128)(2,1)S(1)}, bf16[8,1024]{1,0:T(8,128)(2,1)S(1)}, u32[]{:S(2)}, u32[]{:S(2)}) collective-permute-start(bf16[8,1024]{1,0:T(8,128)(2,1)S(1)} %get-tuple-element.383), channel_id=1, source_target_pairs={{0,32},{32,64},{64,96},{96,128},{128,160},{160,192},{192,224},{1,3... | collective-permute-start | bytes 49160 | tf_op jit(solution)/shard_map/while/body/eval_jaxpr/ppermute | solution.py:20
  150.2 6.2 %collective-permute-start = (bf16[8,1024]{1,0:T(8,128)(2,1)S(1)}, bf16[8,1024]{1,0:T(8,128)(2,1)S(1)}, u32[]{:S(2)}, u32[]{:S(2)}) collective-permute-start(bf16[8,1024]{1,0:T(8,128)(2,1)S(1)} %get-tuple-element.383), channel_id=1, source_target_pairs={{0,32},{32,64},{64,96},{96,128},{128,160},{160,192},{192,224},{1,3... | collective-permute-start | bytes 49160 | tf_op jit(solution)/shard_map/while/body/eval_jaxpr/ppermute | solution.py:20
  157.2 6.8 %collective-permute-start = (bf16[8,1024]{1,0:T(8,128)(2,1)S(1)}, bf16[8,1024]{1,0:T(8,128)(2,1)S(1)}, u32[]{:S(2)}, u32[]{:S(2)}) collective-permute-start(bf16[8,1024]{1,0:T(8,128)(2,1)S(1)} %get-tuple-element.383), channel_id=1, source_target_pairs={{0,32},{32,64},{64,96},{96,128},{128,160},{160,192},{192,224},{1,3... | collective-permute-start | bytes 49160 | tf_op jit(solution)/shard_map/while/body/eval_jaxpr/ppermute | solution.py:20
  164.7 40.1 %collective-permute-start = (bf16[8,1024]{1,0:T(8,128)(2,1)S(1)}, bf16[8,1024]{1,0:T(8,128)(2,1)S(1)}, u32[]{:S(2)}, u32[]{:S(2)}) collective-permute-start(bf16[8,1024]{1,0:T(8,128)(2,1)S(1)} %get-tuple-element.383), channel_id=1, source_target_pairs={{0,32},{32,64},{64,96},{96,128},{128,160},{160,192},{192,224},{1,3... | collective-permute-start | bytes 49160 | tf_op jit(solution)/shard_map/while/body/eval_jaxpr/ppermute | solution.py:20
  212.0 6.8 %collective-permute-start = (bf16[8,1024]{1,0:T(8,128)(2,1)S(1)}, bf16[8,1024]{1,0:T(8,128)(2,1)S(1)}, u32[]{:S(2)}, u32[]{:S(2)}) collective-permute-start(bf16[8,1024]{1,0:T(8,128)(2,1)S(1)} %get-tuple-element.383), channel_id=1, source_target_pairs={{0,32},{32,64},{64,96},{96,128},{128,160},{160,192},{192,224},{1,3... | collective-permute-start | bytes 49160 | tf_op jit(solution)/shard_map/while/body/eval_jaxpr/ppermute | solution.py:20
  225.9 6.8 %collective-permute-start = (bf16[8,1024]{1,0:T(8,128)(2,1)S(1)}, bf16[8,1024]{1,0:T(8,128)(2,1)S(1)}, u32[]{:S(2)}, u32[]{:S(2)}) collective-permute-start(bf16[8,1024]{1,0:T(8,128)(2,1)S(1)} %get-tuple-element.383), channel_id=1, source_target_pairs={{0,32},{32,64},{64,96},{96,128},{128,160},{160,192},{192,224},{1,3... | collective-permute-start | bytes 49160 | tf_op jit(solution)/shard_map/while/body/eval_jaxpr/ppermute | solution.py:20
  239.9 6.8 %collective-permute-start = (bf16[8,1024]{1,0:T(8,128)(2,1)S(1)}, bf16[8,1024]{1,0:T(8,128)(2,1)S(1)}, u32[]{:S(2)}, u32[]{:S(2)}) collective-permute-start(bf16[8,1024]{1,0:T(8,128)(2,1)S(1)} %get-tuple-element.383), channel_id=1, source_target_pairs={{0,32},{32,64},{64,96},{96,128},{128,160},{160,192},{192,224},{1,3... | collective-permute-start | bytes 49160 | tf_op jit(solution)/shard_map/while/body/eval_jaxpr/ppermute | solution.py:20
  253.9 6.8 %collective-permute-start = (bf16[8,1024]{1,0:T(8,128)(2,1)S(1)}, bf16[8,1024]{1,0:T(8,128)(2,1)S(1)}, u32[]{:S(2)}, u32[]{:S(2)}) collective-permute-start(bf16[8,1024]{1,0:T(8,128)(2,1)S(1)} %get-tuple-element.383), channel_id=1, source_target_pairs={{0,32},{32,64},{64,96},{96,128},{128,160},{160,192},{192,224},{1,3... | collective-permute-start | bytes 49160 | tf_op jit(solution)/shard_map/while/body/eval_jaxpr/ppermute | solution.py:20
  267.8 6.8 %collective-permute-start = (bf16[8,1024]{1,0:T(8,128)(2,1)S(1)}, bf16[8,1024]{1,0:T(8,128)(2,1)S(1)}, u32[]{:S(2)}, u32[]{:S(2)}) collective-permute-start(bf16[8,1024]{1,0:T(8,128)(2,1)S(1)} %get-tuple-element.383), channel_id=1, source_target_pairs={{0,32},{32,64},{64,96},{96,128},{128,160},{160,192},{192,224},{1,3... | collective-permute-start | bytes 49160 | tf_op jit(solution)/shard_map/while/body/eval_jaxpr/ppermute | solution.py:20
  281.8 6.8 %collective-permute-start = (bf16[8,1024]{1,0:T(8,128)(2,1)S(1)}, bf16[8,1024]{1,0:T(8,128)(2,1)S(1)}, u32[]{:S(2)}, u32[]{:S(2)}) collective-permute-start(bf16[8,1024]{1,0:T(8,128)(2,1)S(1)} %get-tuple-element.383), channel_id=1, source_target_pairs={{0,32},{32,64},{64,96},{96,128},{128,160},{160,192},{192,224},{1,3... | collective-permute-start | bytes 49160 | tf_op jit(solution)/shard_map/while/body/eval_jaxpr/ppermute | solution.py:20
  295.8 15.3 %collective-permute-start.1 = (bf16[8,1024]{1,0:T(8,128)(2,1)S(1)}, bf16[8,1024]{1,0:T(8,128)(2,1)S(1)}, u32[]{:S(2)}, u32[]{:S(2)}) collective-permute-start(bf16[8,1024]{1,0:T(8,128)(2,1)S(1)} %get-tuple-element.261), channel_id=1, source_target_pairs={{0,32},{32,64},{64,96},{96,128},{128,160},{160,192},{192,224},{1,3... | collective-permute-start | bytes 49160 | tf_op jit(solution)/shard_map/ppermute | solution.py:20
  297.7 28.6 %all-to-all-start.1 = ((bf16[8,8,1024]{2,1,0:T(8,128)(2,1)}), bf16[8,8,1024]{2,1,0:T(8,128)(2,1)S(1)}, u32[]{:S(2)}, u32[]{:S(2)}) async-start(bf16[8,8,1024]{2,1,0:T(8,128)(2,1)} %slice.38), calls=%async_computation.1 | async-start | bytes 262144 | tf_op jit(solution)/shard_map/all_to_all | solution.py:217
  307.0 8.2 %copy-start = (bf16[32,2,1024,128]{3,2,1,0:T(8,128)(2,1)S(1)}, bf16[32,2,1024,128]{3,2,1,0:T(8,128)(2,1)}, u32[]{:S(2)}) copy-start(bf16[32,2,1024,128]{3,2,1,0:T(8,128)(2,1)} %get-tuple-element.411) | copy-start | bytes 50331652
Sparse Core Ops, SparseCore 0:
  11.3 104.3 all-gather.2

commit v6 on v5

--- a/solution.py
+++ b/solution.py
@@ -186,6 +186,7 @@
     half = jnp.where(lax.axis_index("dp") == 0, w_recur[0], w_input[0])
     half = jnp.dot(half, order, preferred_element_type=jnp.float32).astype(jnp.bfloat16)
     weights = lax.all_gather(half, ("col", "dp")).reshape(cols, 2, H, 4 * units)
+    weights = pltpu.with_memory_space_constraint(weights, pltpu.HBM)
 
     kept = keep(weights)
 

time: 354 us -> 349 us (0.986)
  the two profiles are of different devices: /device:TPU:448 before, /device:TPU:8 now
where the time goes in v6:
time: 349 us; the launch traced here: 348 us
  Pallas kernels  122 us (35%)
  waiting for transfers between devices  96.4 us (28%)
  starting transfers between devices  83.3 us (24%)
  blocking collectives  16.3 us (5%)
  between operations  14.3 us (4%)
  local copies, waits for them, and re-layouts  9.96 us (3%)
    all_gather x1, waiting for transfers between devices, shards(): weights = lax.all_gather(half, ('col', 'dp')).reshape(cols, 2, H, 4 * units)  80.1 us
    pallas_call x15, Pallas kernels, late(): pl.pallas_call(late_kernel, out_shape=(like(place), like(x_got), like(x_g...  62.5 us
    pallas_call x15, Pallas kernels, early(): pl.pallas_call(early_kernel, out_shape=jax.ShapeDtypeStruct((2 * ROWS, 4...  58.4 us
    ppermute x15, starting transfers between devices, passed_along(): return lax.ppermute(block, axis, route)  55.3 us
    all_to_all x1, starting transfers between devices, shards(): moved = lax.all_to_all(carry[4][1:], 'layer', 0, 0, tiled=True)[layers - 1]  17.9 us
    all_to_all x1, blocking collectives, shards(): lax.all_to_all(sent, 'col', 0, 0, tiled=True).reshape(cols, 4, ROWS, units)  16.3 us
    all_to_all x1, waiting for transfers between devices, shards(): got = lax.all_to_all(sent, 'col', 0, 0, tiled=True)  12.6 us
    all_to_all x1, starting transfers between devices, shards(): got = lax.all_to_all(sent, 'col', 0, 0, tiled=True)  10.2 us
  transfers between devices with their start and end apart: 18, of which 3 were waited for; matrix products, arithmetic and copies ran while one was open for 2% of the time, Pallas kernels for 17%

profile of v6, /device:TPU:8, one launch (start us, length us, event | category | flops | bytes accessed | tf_op | source)
XLA Modules:
  0.0 347.8 jit_solution(12181650052460852509)
XLA Ops:
  15.1 10.2 %all-to-all-start = ((f32[32,1,2176]{2,1,0:T(1,128)}), f32[32,1,2176]{2,1,0:T(1,128)S(1)}, u32[]{:S(2)}, u32[]{:S(2)}) async-start(f32[32,1,2176]{2,1,0:T(1,128)} %copy.36), calls=%async_computation | async-start | bytes 557056 | tf_op jit(solution)/shard_map/all_to_all | solution.py:196
  25.3 12.6 %all-to-all-done = f32[32,1,2176]{2,1,0:T(1,128)S(1)} async-done(((f32[32,1,2176]{2,1,0:T(1,128)}), f32[32,1,2176]{2,1,0:T(1,128)S(1)}, u32[]{:S(2)}, u32[]{:S(2)}) %all-to-all-start) | async-done | bytes 278560 | tf_op jit(solution)/shard_map/all_to_all | solution.py:196
  39.2 80.1 %all-gather.3.cloned.1.call-done = bf16[65536,128]{1,0:T(8,128)(2,1)} async-done(((bf16[1024,128]{1,0:T(8,128)(2,1)}), bf16[65536,128]{1,0:T(8,128)(2,1)}) %all-gather.3.cloned.1.call-update) | async-done | bytes 16777232 | tf_op jit(solution)/shard_map/all_gather | solution.py:188
  121.0 168.8 %while.23 = (s32[]{:T(128)}, f32[8,128]{1,0:T(8,128)S(1)}, bf16[8,1024]{1,0:T(8,128)(2,1)S(1)}, f32[8,1024]{1,0:T(8,128)S(1)}, f32[8,1024]{1,0:T(8,128)S(1)}, /*...) while((s32[]{:T(128)}, f32[8,128]{1,0:T(8,128)S(1)}, ...), condition=%wide.region_1.2_spmd, body=%wide.region_0.1_spmd.sunk | while | flops 8000000000 | bytes 8098505 | solution.py:216
  124.6 3.9 %eval_jaxpr.9.product = f32[8,4096]{1,0:T(8,128)S(1)} custom-call(f32[8,1024]{1,0:T(8,128)S(1)} %get-tuple-element.384.h_was, bf16[32,2,1024,128]{3,2,1,0:T(8,128)(2,1)} %get-tuple-element.400.weights), custom_call_target="tpu_custom_call" | custom-call | flops 8000000000 | bytes 8000000 | tf_op jit(solution)/shard_map/while/body/eval_jaxpr/pallas_call | solution.py:135
  128.5 7.1 %eval_jaxpr.10 = (f32[8,128]{1,0:T(8,128)S(1)}, bf16[8,1024]{1,0:T(8,128)(2,1)S(1)}, bf16[8,1024]{1,0:T(8,128)(2,1)S(1)}, f32[8,1024]{1,0:T(8,128)S(1)}, f32[8,1024]{1,0:T(8,128)S(1)}) custom-call(f32[8,128]{1,0:T(8,128)S(1)} %get-tuple-element.382.place, ...), custom_call_target="tpu_custom_call", output_to_operand_aliasing={{0}: (0, {}), {3}: (4, {}), {4}: (5, {})} | custom-call | tf_op jit(solution)/shard_map/while/body/eval_jaxpr/pallas_call | solution.py:161
  136.9 3.9 %eval_jaxpr.9.product = f32[8,4096]{1,0:T(8,128)S(1)} custom-call(f32[8,1024]{1,0:T(8,128)S(1)} %get-tuple-element.384.h_was, bf16[32,2,1024,128]{3,2,1,0:T(8,128)(2,1)} %get-tuple-element.400.weights), custom_call_target="tpu_custom_call" | custom-call | flops 8000000000 | bytes 8000000 | tf_op jit(solution)/shard_map/while/body/eval_jaxpr/pallas_call | solution.py:135
  140.9 7.1 %eval_jaxpr.10 = (f32[8,128]{1,0:T(8,128)S(1)}, bf16[8,1024]{1,0:T(8,128)(2,1)S(1)}, bf16[8,1024]{1,0:T(8,128)(2,1)S(1)}, f32[8,1024]{1,0:T(8,128)S(1)}, f32[8,1024]{1,0:T(8,128)S(1)}) custom-call(f32[8,128]{1,0:T(8,128)S(1)} %get-tuple-element.382.place, ...), custom_call_target="tpu_custom_call", output_to_operand_aliasing={{0}: (0, {}), {3}: (4, {}), {4}: (5, {})} | custom-call | tf_op jit(solution)/shard_map/while/body/eval_jaxpr/pallas_call | solution.py:161
  149.7 3.9 %eval_jaxpr.9.product = f32[8,4096]{1,0:T(8,128)S(1)} custom-call(f32[8,1024]{1,0:T(8,128)S(1)} %get-tuple-element.384.h_was, bf16[32,2,1024,128]{3,2,1,0:T(8,128)(2,1)} %get-tuple-element.400.weights), custom_call_target="tpu_custom_call" | custom-call | flops 8000000000 | bytes 8000000 | tf_op jit(solution)/shard_map/while/body/eval_jaxpr/pallas_call | solution.py:135
  153.6 7.1 %eval_jaxpr.10 = (f32[8,128]{1,0:T(8,128)S(1)}, bf16[8,1024]{1,0:T(8,128)(2,1)S(1)}, bf16[8,1024]{1,0:T(8,128)(2,1)S(1)}, f32[8,1024]{1,0:T(8,128)S(1)}, f32[8,1024]{1,0:T(8,128)S(1)}) custom-call(f32[8,128]{1,0:T(8,128)S(1)} %get-tuple-element.382.place, ...), custom_call_target="tpu_custom_call", output_to_operand_aliasing={{0}: (0, {}), {3}: (4, {}), {4}: (5, {})} | custom-call | tf_op jit(solution)/shard_map/while/body/eval_jaxpr/pallas_call | solution.py:161
  162.7 3.9 %eval_jaxpr.9.product = f32[8,4096]{1,0:T(8,128)S(1)} custom-call(f32[8,1024]{1,0:T(8,128)S(1)} %get-tuple-element.384.h_was, bf16[32,2,1024,128]{3,2,1,0:T(8,128)(2,1)} %get-tuple-element.400.weights), custom_call_target="tpu_custom_call" | custom-call | flops 8000000000 | bytes 8000000 | tf_op jit(solution)/shard_map/while/body/eval_jaxpr/pallas_call | solution.py:135
  166.6 7.1 %eval_jaxpr.10 = (f32[8,128]{1,0:T(8,128)S(1)}, bf16[8,1024]{1,0:T(8,128)(2,1)S(1)}, bf16[8,1024]{1,0:T(8,128)(2,1)S(1)}, f32[8,1024]{1,0:T(8,128)S(1)}, f32[8,1024]{1,0:T(8,128)S(1)}) custom-call(f32[8,128]{1,0:T(8,128)S(1)} %get-tuple-element.382.place, ...), custom_call_target="tpu_custom_call", output_to_operand_aliasing={{0}: (0, {}), {3}: (4, {}), {4}: (5, {})} | custom-call | tf_op jit(solution)/shard_map/while/body/eval_jaxpr/pallas_call | solution.py:161
  179.5 7.1 %eval_jaxpr.10 = (f32[8,128]{1,0:T(8,128)S(1)}, bf16[8,1024]{1,0:T(8,128)(2,1)S(1)}, bf16[8,1024]{1,0:T(8,128)(2,1)S(1)}, f32[8,1024]{1,0:T(8,128)S(1)}, f32[8,1024]{1,0:T(8,128)S(1)}) custom-call(f32[8,128]{1,0:T(8,128)S(1)} %get-tuple-element.382.place, ...), custom_call_target="tpu_custom_call", output_to_operand_aliasing={{0}: (0, {}), {3}: (4, {}), {4}: (5, {})} | custom-call | tf_op jit(solution)/shard_map/while/body/eval_jaxpr/pallas_call | solution.py:161
  188.6 3.9 %eval_jaxpr.9.product = f32[8,4096]{1,0:T(8,128)S(1)} custom-call(f32[8,1024]{1,0:T(8,128)S(1)} %get-tuple-element.384.h_was, bf16[32,2,1024,128]{3,2,1,0:T(8,128)(2,1)} %get-tuple-element.400.weights), custom_call_target="tpu_custom_call" | custom-call | flops 8000000000 | bytes 8000000 | tf_op jit(solution)/shard_map/while/body/eval_jaxpr/pallas_call | solution.py:135
  192.5 7.1 %eval_jaxpr.10 = (f32[8,128]{1,0:T(8,128)S(1)}, bf16[8,1024]{1,0:T(8,128)(2,1)S(1)}, bf16[8,1024]{1,0:T(8,128)(2,1)S(1)}, f32[8,1024]{1,0:T(8,128)S(1)}, f32[8,1024]{1,0:T(8,128)S(1)}) custom-call(f32[8,128]{1,0:T(8,128)S(1)} %get-tuple-element.382.place, ...), custom_call_target="tpu_custom_call", output_to_operand_aliasing={{0}: (0, {}), {3}: (4, {}), {4}: (5, {})} | custom-call | tf_op jit(solution)/shard_map/while/body/eval_jaxpr/pallas_call | solution.py:161
  201.6 3.9 %eval_jaxpr.9.product = f32[8,4096]{1,0:T(8,128)S(1)} custom-call(f32[8,1024]{1,0:T(8,128)S(1)} %get-tuple-element.384.h_was, bf16[32,2,1024,128]{3,2,1,0:T(8,128)(2,1)} %get-tuple-element.400.weights), custom_call_target="tpu_custom_call" | custom-call | flops 8000000000 | bytes 8000000 | tf_op jit(solution)/shard_map/while/body/eval_jaxpr/pallas_call | solution.py:135
  205.5 7.1 %eval_jaxpr.10 = (f32[8,128]{1,0:T(8,128)S(1)}, bf16[8,1024]{1,0:T(8,128)(2,1)S(1)}, bf16[8,1024]{1,0:T(8,128)(2,1)S(1)}, f32[8,1024]{1,0:T(8,128)S(1)}, f32[8,1024]{1,0:T(8,128)S(1)}) custom-call(f32[8,128]{1,0:T(8,128)S(1)} %get-tuple-element.382.place, ...), custom_call_target="tpu_custom_call", output_to_operand_aliasing={{0}: (0, {}), {3}: (4, {}), {4}: (5, {})} | custom-call | tf_op jit(solution)/shard_map/while/body/eval_jaxpr/pallas_call | solution.py:161
  218.5 7.1 %eval_jaxpr.10 = (f32[8,128]{1,0:T(8,128)S(1)}, bf16[8,1024]{1,0:T(8,128)(2,1)S(1)}, bf16[8,1024]{1,0:T(8,128)(2,1)S(1)}, f32[8,1024]{1,0:T(8,128)S(1)}, f32[8,1024]{1,0:T(8,128)S(1)}) custom-call(f32[8,128]{1,0:T(8,128)S(1)} %get-tuple-element.382.place, ...), custom_call_target="tpu_custom_call", output_to_operand_aliasing={{0}: (0, {}), {3}: (4, {}), {4}: (5, {})} | custom-call | tf_op jit(solution)/shard_map/while/body/eval_jaxpr/pallas_call | solution.py:161
  232.8 9.3 %collective-permute-start = (bf16[8,1024]{1,0:T(8,128)(2,1)S(1)}, bf16[8,1024]{1,0:T(8,128)(2,1)S(1)}, u32[]{:S(2)}, u32[]{:S(2)}) collective-permute-start(bf16[8,1024]{1,0:T(8,128)(2,1)S(1)} %get-tuple-element.383), channel_id=1, source_target_pairs={{0,32},{32,64},{64,96},{96,128},{128,160},{160,192},{192,224},{1,3... | collective-permute-start | bytes 49160 | tf_op jit(solution)/shard_map/while/body/eval_jaxpr/ppermute | solution.py:20
  254.3 9.3 %collective-permute-start = (bf16[8,1024]{1,0:T(8,128)(2,1)S(1)}, bf16[8,1024]{1,0:T(8,128)(2,1)S(1)}, u32[]{:S(2)}, u32[]{:S(2)}) collective-permute-start(bf16[8,1024]{1,0:T(8,128)(2,1)S(1)} %get-tuple-element.383), channel_id=1, source_target_pairs={{0,32},{32,64},{64,96},{96,128},{128,160},{160,192},{192,224},{1,3... | collective-permute-start | bytes 49160 | tf_op jit(solution)/shard_map/while/body/eval_jaxpr/ppermute | solution.py:20
  263.6 3.9 %eval_jaxpr.9.product = f32[8,4096]{1,0:T(8,128)S(1)} custom-call(f32[8,1024]{1,0:T(8,128)S(1)} %get-tuple-element.384.h_was, bf16[32,2,1024,128]{3,2,1,0:T(8,128)(2,1)} %get-tuple-element.400.weights), custom_call_target="tpu_custom_call" | custom-call | flops 8000000000 | bytes 8000000 | tf_op jit(solution)/shard_map/while/body/eval_jaxpr/pallas_call | solution.py:135
  275.9 9.3 %collective-permute-start = (bf16[8,1024]{1,0:T(8,128)(2,1)S(1)}, bf16[8,1024]{1,0:T(8,128)(2,1)S(1)}, u32[]{:S(2)}, u32[]{:S(2)}) collective-permute-start(bf16[8,1024]{1,0:T(8,128)(2,1)S(1)} %get-tuple-element.383), channel_id=1, source_target_pairs={{0,32},{32,64},{64,96},{96,128},{128,160},{160,192},{192,224},{1,3... | collective-permute-start | bytes 49160 | tf_op jit(solution)/shard_map/while/body/eval_jaxpr/ppermute | solution.py:20
  293.4 17.9 %all-to-all-start.1 = ((bf16[8,8,1024]{2,1,0:T(8,128)(2,1)}), bf16[8,8,1024]{2,1,0:T(8,128)(2,1)S(1)}, u32[]{:S(2)}, u32[]{:S(2)}) async-start(bf16[8,8,1024]{2,1,0:T(8,128)(2,1)} %slice.38), calls=%async_computation.1 | async-start | bytes 262144 | tf_op jit(solution)/shard_map/all_to_all | solution.py:218
  320.9 16.3 %all_to_all.22 = f32[32,1,512]{2,1,0:T(1,128)S(1)} all-to-all(f32[32,1,512]{2,1,0:T(1,128)S(1)} %reshape.110), channel_id=1, replica_groups=mesh['dp'=2,'layer'=8,'col'=32] {'col'}, dimensions={0} | all-to-all | bytes 131072 | tf_op jit(solution)/shard_map/all_to_all | solution.py:223
  (108 shorter events, 83.8 us)
Async XLA Ops:
  7.2 112.2 %all-gather.3.cloned.1.call-start = ((), (), s32[]{:S(2)}) async-start(), calls=%async_computation.3 | async-start | bytes 17039360 | tf_op jit(solution)/shard_map/all_gather | solution.py:188
  15.1 22.8 %all-to-all-start = ((f32[32,1,2176]{2,1,0:T(1,128)}), f32[32,1,2176]{2,1,0:T(1,128)S(1)}, u32[]{:S(2)}, u32[]{:S(2)}) async-start(f32[32,1,2176]{2,1,0:T(1,128)} %copy.36), calls=%async_computation | async-start | bytes 557056 | tf_op jit(solution)/shard_map/all_to_all | solution.py:196
  121.0 7.5 %collective-permute-start = (bf16[8,1024]{1,0:T(8,128)(2,1)S(1)}, bf16[8,1024]{1,0:T(8,128)(2,1)S(1)}, u32[]{:S(2)}, u32[]{:S(2)}) collective-permute-start(bf16[8,1024]{1,0:T(8,128)(2,1)S(1)} %get-tuple-element.383), channel_id=1, source_target_pairs={{0,32},{32,64},{64,96},{96,128},{128,160},{160,192},{192,224},{1,3... | collective-permute-start | bytes 49160 | tf_op jit(solution)/shard_map/while/body/eval_jaxpr/ppermute | solution.py:20
  135.6 5.2 %collective-permute-start = (bf16[8,1024]{1,0:T(8,128)(2,1)S(1)}, bf16[8,1024]{1,0:T(8,128)(2,1)S(1)}, u32[]{:S(2)}, u32[]{:S(2)}) collective-permute-start(bf16[8,1024]{1,0:T(8,128)(2,1)S(1)} %get-tuple-element.383), channel_id=1, source_target_pairs={{0,32},{32,64},{64,96},{96,128},{128,160},{160,192},{192,224},{1,3... | collective-permute-start | bytes 49160 | tf_op jit(solution)/shard_map/while/body/eval_jaxpr/ppermute | solution.py:20
  148.0 5.6 %collective-permute-start = (bf16[8,1024]{1,0:T(8,128)(2,1)S(1)}, bf16[8,1024]{1,0:T(8,128)(2,1)S(1)}, u32[]{:S(2)}, u32[]{:S(2)}) collective-permute-start(bf16[8,1024]{1,0:T(8,128)(2,1)S(1)} %get-tuple-element.383), channel_id=1, source_target_pairs={{0,32},{32,64},{64,96},{96,128},{128,160},{160,192},{192,224},{1,3... | collective-permute-start | bytes 49160 | tf_op jit(solution)/shard_map/while/body/eval_jaxpr/ppermute | solution.py:20
  160.7 5.8 %collective-permute-start = (bf16[8,1024]{1,0:T(8,128)(2,1)S(1)}, bf16[8,1024]{1,0:T(8,128)(2,1)S(1)}, u32[]{:S(2)}, u32[]{:S(2)}) collective-permute-start(bf16[8,1024]{1,0:T(8,128)(2,1)S(1)} %get-tuple-element.383), channel_id=1, source_target_pairs={{0,32},{32,64},{64,96},{96,128},{128,160},{160,192},{192,224},{1,3... | collective-permute-start | bytes 49160 | tf_op jit(solution)/shard_map/while/body/eval_jaxpr/ppermute | solution.py:20
  173.7 5.8 %collective-permute-start = (bf16[8,1024]{1,0:T(8,128)(2,1)S(1)}, bf16[8,1024]{1,0:T(8,128)(2,1)S(1)}, u32[]{:S(2)}, u32[]{:S(2)}) collective-permute-start(bf16[8,1024]{1,0:T(8,128)(2,1)S(1)} %get-tuple-element.383), channel_id=1, source_target_pairs={{0,32},{32,64},{64,96},{96,128},{128,160},{160,192},{192,224},{1,3... | collective-permute-start | bytes 49160 | tf_op jit(solution)/shard_map/while/body/eval_jaxpr/ppermute | solution.py:20
  186.7 5.8 %collective-permute-start = (bf16[8,1024]{1,0:T(8,128)(2,1)S(1)}, bf16[8,1024]{1,0:T(8,128)(2,1)S(1)}, u32[]{:S(2)}, u32[]{:S(2)}) collective-permute-start(bf16[8,1024]{1,0:T(8,128)(2,1)S(1)} %get-tuple-element.383), channel_id=1, source_target_pairs={{0,32},{32,64},{64,96},{96,128},{128,160},{160,192},{192,224},{1,3... | collective-permute-start | bytes 49160 | tf_op jit(solution)/shard_map/while/body/eval_jaxpr/ppermute | solution.py:20
  199.6 5.8 %collective-permute-start = (bf16[8,1024]{1,0:T(8,128)(2,1)S(1)}, bf16[8,1024]{1,0:T(8,128)(2,1)S(1)}, u32[]{:S(2)}, u32[]{:S(2)}) collective-permute-start(bf16[8,1024]{1,0:T(8,128)(2,1)S(1)} %get-tuple-element.383), channel_id=1, source_target_pairs={{0,32},{32,64},{64,96},{96,128},{128,160},{160,192},{192,224},{1,3... | collective-permute-start | bytes 49160 | tf_op jit(solution)/shard_map/while/body/eval_jaxpr/ppermute | solution.py:20
  212.6 5.8 %collective-permute-start = (bf16[8,1024]{1,0:T(8,128)(2,1)S(1)}, bf16[8,1024]{1,0:T(8,128)(2,1)S(1)}, u32[]{:S(2)}, u32[]{:S(2)}) collective-permute-start(bf16[8,1024]{1,0:T(8,128)(2,1)S(1)} %get-tuple-element.383), channel_id=1, source_target_pairs={{0,32},{32,64},{64,96},{96,128},{128,160},{160,192},{192,224},{1,3... | collective-permute-start | bytes 49160 | tf_op jit(solution)/shard_map/while/body/eval_jaxpr/ppermute | solution.py:20
  225.6 6.4 %collective-permute-start = (bf16[8,1024]{1,0:T(8,128)(2,1)S(1)}, bf16[8,1024]{1,0:T(8,128)(2,1)S(1)}, u32[]{:S(2)}, u32[]{:S(2)}) collective-permute-start(bf16[8,1024]{1,0:T(8,128)(2,1)S(1)} %get-tuple-element.383), channel_id=1, source_target_pairs={{0,32},{32,64},{64,96},{96,128},{128,160},{160,192},{192,224},{1,3... | collective-permute-start | bytes 49160 | tf_op jit(solution)/shard_map/while/body/eval_jaxpr/ppermute | solution.py:20
  232.8 13.2 %collective-permute-start = (bf16[8,1024]{1,0:T(8,128)(2,1)S(1)}, bf16[8,1024]{1,0:T(8,128)(2,1)S(1)}, u32[]{:S(2)}, u32[]{:S(2)}) collective-permute-start(bf16[8,1024]{1,0:T(8,128)(2,1)S(1)} %get-tuple-element.383), channel_id=1, source_target_pairs={{0,32},{32,64},{64,96},{96,128},{128,160},{160,192},{192,224},{1,3... | collective-permute-start | bytes 49160 | tf_op jit(solution)/shard_map/while/body/eval_jaxpr/ppermute | solution.py:20
  246.7 6.8 %collective-permute-start = (bf16[8,1024]{1,0:T(8,128)(2,1)S(1)}, bf16[8,1024]{1,0:T(8,128)(2,1)S(1)}, u32[]{:S(2)}, u32[]{:S(2)}) collective-permute-start(bf16[8,1024]{1,0:T(8,128)(2,1)S(1)} %get-tuple-element.383), channel_id=1, source_target_pairs={{0,32},{32,64},{64,96},{96,128},{128,160},{160,192},{192,224},{1,3... | collective-permute-start | bytes 49160 | tf_op jit(solution)/shard_map/while/body/eval_jaxpr/ppermute | solution.py:20
  254.3 13.2 %collective-permute-start = (bf16[8,1024]{1,0:T(8,128)(2,1)S(1)}, bf16[8,1024]{1,0:T(8,128)(2,1)S(1)}, u32[]{:S(2)}, u32[]{:S(2)}) collective-permute-start(bf16[8,1024]{1,0:T(8,128)(2,1)S(1)} %get-tuple-element.383), channel_id=1, source_target_pairs={{0,32},{32,64},{64,96},{96,128},{128,160},{160,192},{192,224},{1,3... | collective-permute-start | bytes 49160 | tf_op jit(solution)/shard_map/while/body/eval_jaxpr/ppermute | solution.py:20
  268.3 6.8 %collective-permute-start = (bf16[8,1024]{1,0:T(8,128)(2,1)S(1)}, bf16[8,1024]{1,0:T(8,128)(2,1)S(1)}, u32[]{:S(2)}, u32[]{:S(2)}) collective-permute-start(bf16[8,1024]{1,0:T(8,128)(2,1)S(1)} %get-tuple-element.383), channel_id=1, source_target_pairs={{0,32},{32,64},{64,96},{96,128},{128,160},{160,192},{192,224},{1,3... | collective-permute-start | bytes 49160 | tf_op jit(solution)/shard_map/while/body/eval_jaxpr/ppermute | solution.py:20
  275.9 13.2 %collective-permute-start = (bf16[8,1024]{1,0:T(8,128)(2,1)S(1)}, bf16[8,1024]{1,0:T(8,128)(2,1)S(1)}, u32[]{:S(2)}, u32[]{:S(2)}) collective-permute-start(bf16[8,1024]{1,0:T(8,128)(2,1)S(1)} %get-tuple-element.383), channel_id=1, source_target_pairs={{0,32},{32,64},{64,96},{96,128},{128,160},{160,192},{192,224},{1,3... | collective-permute-start | bytes 49160 | tf_op jit(solution)/shard_map/while/body/eval_jaxpr/ppermute | solution.py:20
  289.8 25.4 %collective-permute-start.1 = (bf16[8,1024]{1,0:T(8,128)(2,1)S(1)}, bf16[8,1024]{1,0:T(8,128)(2,1)S(1)}, u32[]{:S(2)}, u32[]{:S(2)}) collective-permute-start(bf16[8,1024]{1,0:T(8,128)(2,1)S(1)} %get-tuple-element.261), channel_id=1, source_target_pairs={{0,32},{32,64},{64,96},{96,128},{128,160},{160,192},{192,224},{1,3... | collective-permute-start | bytes 49160 | tf_op jit(solution)/shard_map/ppermute | solution.py:20
  293.4 27.0 %all-to-all-start.1 = ((bf16[8,8,1024]{2,1,0:T(8,128)(2,1)}), bf16[8,8,1024]{2,1,0:T(8,128)(2,1)S(1)}, u32[]{:S(2)}, u32[]{:S(2)}) async-start(bf16[8,8,1024]{2,1,0:T(8,128)(2,1)} %slice.38), calls=%async_computation.1 | async-start | bytes 262144 | tf_op jit(solution)/shard_map/all_to_all | solution.py:218
Sparse Core Ops, SparseCore 0:
  11.3 107.9 all-gather.2

commit v7 on v6

--- a/solution.py
+++ b/solution.py
@@ -11,7 +11,7 @@
 LANES = 128
 WIDE = 512
 BLOCKS = 4 * H // WIDE
-KEPT = 2
+KEPT = 11
 
 
 def passed_along(block, axis, distance):
@@ -32,29 +32,29 @@
     return gates
 
 
-def fetch(weights, close, sems, m, p):
-    return pltpu.make_async_copy(weights.at[p, m], close.at[m, :, pl.ds(LANES * p, LANES)], sems.at[m, p])
-
-
-def columns(weights, close, sems, m, q):
-    for j in range(4):
-        fetch(weights, close, sems, m, 4 * q + j).wait()
-    return close[m, :, WIDE * q : WIDE * (q + 1)]
-
-
-def keep_kernel(weights, kept, sems):
-    copies = [
-        pltpu.make_async_copy(weights.at[p, 1], kept.at[:, pl.ds(LANES * p, LANES)], sems.at[p]) for p in range(4 * KEPT)
-    ]
-    for copy in copies:
-        copy.start()
-    for copy in copies:
-        copy.wait()
+def fetch(weights, close, sems, m, q):
+    first = max(4 * q, KEPT) if m == 1 else 4 * q
+    pieces = pl.ds(first, 4 * q + 4 - first)
+    return pltpu.make_async_copy(weights.at[pieces, m], close.at[m, pieces], sems.at[m, q])
+
+
+def columns(weights, close, sems, m, q, kept=None):
+    here = KEPT if m == 1 else 0
+    if here < 4 * q + 4:
+        fetch(weights, close, sems, m, q).wait()
+    pieces = [kept[p] if p < here else close[m, p] for p in range(4 * q, 4 * q + 4)]
+    return jnp.concatenate(pieces, axis=1)
+
+
+def keep_kernel(weights, kept, sem):
+    copy = pltpu.make_async_copy(weights.at[pl.ds(0, KEPT), 1], kept, sem)
+    copy.start()
+    copy.wait()
 
 
 def early_kernel(h_was, weights, product_out, close, sems):
-    for p in range(H // 32):
-        fetch(weights, close, sems, 0, p).start()
+    for q in range(BLOCKS):
+        fetch(weights, close, sems, 0, q).start()
     h_low = h_was[...].astype(jnp.bfloat16)
     for q in range(BLOCKS):
         part = jnp.dot(h_low, columns(weights, close, sems, 0, q), preferred_element_type=jnp.float32)
@@ -72,9 +72,9 @@
 
     @pl.when(active)
     def _():
-        for m, done in ((1, 4 * KEPT), (0, 0)):
-            for p in range(done, H // 32):
-                fetch(weights, close, sems, m, p).start()
+        for m, done in ((1, KEPT // 4), (0, 0)):
+            for q in range(done, BLOCKS):
+                fetch(weights, close, sems, m, q).start()
         x = jnp.where(level == 0, x_tokens[chunk].astype(jnp.float32), x_got[...].astype(jnp.float32))
         x_low = x.astype(jnp.bfloat16)
         lane = lax.broadcasted_iota(jnp.int32, (2 * ROWS, LANES), 1)
@@ -96,10 +96,7 @@
 
         pieces = []
         for q in range(BLOCKS):
-            if q < KEPT:
-                block = kept[:, WIDE * q : WIDE * (q + 1)]
-            else:
-                block = columns(weights, close, sems, 1, q)
+            block = columns(weights, close, sems, 1, q, kept)
             part = jnp.dot(x_low, block, preferred_element_type=jnp.float32)
             for j in range(4):
                 lanes = slice(WIDE * q + LANES * j, WIDE * q + LANES * (j + 1))
@@ -137,7 +134,7 @@
         out_shape=jax.ShapeDtypeStruct((2 * ROWS, 4 * H), jnp.float32),
         in_specs=[FULL, FAR],
         out_specs=FULL,
-        scratch_shapes=[pltpu.VMEM((1, H, 4 * H), jnp.bfloat16), pltpu.SemaphoreType.DMA((1, H // 32))],
+        scratch_shapes=[pltpu.VMEM((1, H // 32, H, LANES), jnp.bfloat16), pltpu.SemaphoreType.DMA((1, BLOCKS))],
         compiler_params=pltpu.CompilerParams(vmem_limit_bytes=16 * 1024 * 1024),
         cost_estimate=pl.CostEstimate(flops=8_000_000_000, bytes_accessed=8_000_000, transcendentals=0),
     )(h_was, weights)
@@ -146,10 +143,10 @@
 def keep(weights):
     return pl.pallas_call(
         keep_kernel,
-        out_shape=jax.ShapeDtypeStruct((H, WIDE * KEPT), jnp.bfloat16),
+        out_shape=jax.ShapeDtypeStruct((KEPT, H, LANES), jnp.bfloat16),
         in_specs=[FAR],
         out_specs=FULL,
-        scratch_shapes=[pltpu.SemaphoreType.DMA((4 * KEPT,))],
+        scratch_shapes=[pltpu.SemaphoreType.DMA],
         compiler_params=pltpu.CompilerParams(vmem_limit_bytes=16 * 1024 * 1024),
     )(weights)
 
@@ -166,8 +163,8 @@
         input_output_aliases={0: 0, 4: 3, 5: 4},
         scratch_shapes=[
             pltpu.VMEM((2 * ROWS, 4 * H), jnp.float32),
-            pltpu.VMEM((2, H, 4 * H), jnp.bfloat16),
-            pltpu.SemaphoreType.DMA((2, H // 32)),
+            pltpu.VMEM((2, H // 32, H, LANES), jnp.bfloat16),
+            pltpu.SemaphoreType.DMA((2, BLOCKS)),
         ],
         compiler_params=pltpu.CompilerParams(vmem_limit_bytes=24 * 1024 * 1024),
     )(place, x_got, x_tokens, product, h_was, c_was, bias, kept, weights)

time: 349 us -> 335 us (0.960)
  Pallas kernels: 122 us -> 109 us
    pallas_call x15, Pallas kernels: 62.5 us -> 51.6 us  [late(): pl.pallas_call(late_kernel, out_shape=(like(place), like(x_got), like(x_g...]
where the time goes in v7:
time: 335 us; the launch traced here: 334 us
  Pallas kernels  109 us (33%)
  waiting for transfers between devices  97 us (29%)
  starting transfers between devices  82.2 us (25%)
  blocking collectives  16.3 us (5%)
  between operations  14.3 us (4%)
  local copies, waits for them, and re-layouts  9.96 us (3%)
    all_gather x1, waiting for transfers between devices, shards(): weights = lax.all_gather(half, ('col', 'dp')).reshape(cols, 2, H, 4 * units)  80.1 us
    pallas_call x15, Pallas kernels, early(): pl.pallas_call(early_kernel, out_shape=jax.ShapeDtypeStruct((2 * ROWS, 4...  55.9 us
    ppermute x15, starting transfers between devices, passed_along(): return lax.ppermute(block, axis, route)  55.3 us
    pallas_call x15, Pallas kernels, late(): pl.pallas_call(late_kernel, out_shape=(like(place), like(x_got), like(x_g...  51.6 us
    all_to_all x1, starting transfers between devices, shards(): moved = lax.all_to_all(carry[4][1:], 'layer', 0, 0, tiled=True)[layers - 1]  16.7 us
    all_to_all x1, blocking collectives, shards(): lax.all_to_all(sent, 'col', 0, 0, tiled=True).reshape(cols, 4, ROWS, units)  16.3 us
    all_to_all x1, waiting for transfers between devices, shards(): got = lax.all_to_all(sent, 'col', 0, 0, tiled=True)  12.6 us
    all_to_all x1, starting transfers between devices, shards(): got = lax.all_to_all(sent, 'col', 0, 0, tiled=True)  10.2 us
  transfers between devices with their start and end apart: 18, of which 3 were waited for; matrix products, arithmetic and copies ran while one was open for 2% of the time, Pallas kernels for 17%

profile of v7, /device:TPU:8, one launch (start us, length us, event | category | flops | bytes accessed | tf_op | source)
XLA Modules:
  0.0 334.2 jit_solution(12117188454157104596)
XLA Ops:
  15.1 10.2 %all-to-all-start = ((f32[32,1,2176]{2,1,0:T(1,128)}), f32[32,1,2176]{2,1,0:T(1,128)S(1)}, u32[]{:S(2)}, u32[]{:S(2)}) async-start(f32[32,1,2176]{2,1,0:T(1,128)} %copy.36), calls=%async_computation | async-start | bytes 557056 | tf_op jit(solution)/shard_map/all_to_all | solution.py:193
  25.3 12.6 %all-to-all-done = f32[32,1,2176]{2,1,0:T(1,128)S(1)} async-done(((f32[32,1,2176]{2,1,0:T(1,128)}), f32[32,1,2176]{2,1,0:T(1,128)S(1)}, u32[]{:S(2)}, u32[]{:S(2)}) %all-to-all-start) | async-done | bytes 278560 | tf_op jit(solution)/shard_map/all_to_all | solution.py:193
  39.2 80.1 %all-gather.3.cloned.1.call-done = bf16[65536,128]{1,0:T(8,128)(2,1)} async-done(((bf16[1024,128]{1,0:T(8,128)(2,1)}), bf16[65536,128]{1,0:T(8,128)(2,1)}) %all-gather.3.cloned.1.call-update) | async-done | bytes 16777232 | tf_op jit(solution)/shard_map/all_gather | solution.py:185
  121.3 155.9 %while.23 = (s32[]{:T(128)}, f32[8,128]{1,0:T(8,128)S(1)}, bf16[8,1024]{1,0:T(8,128)(2,1)S(1)}, f32[8,1024]{1,0:T(8,128)S(1)}, f32[8,1024]{1,0:T(8,128)S(1)}, /*...) while((s32[]{:T(128)}, f32[8,128]{1,0:T(8,128)S(1)}, ...), condition=%wide.region_1.2_spmd, body=%wide.region_0.1_spmd.sunk | while | flops 8000000000 | bytes 8098505 | solution.py:213
  124.8 3.7 %eval_jaxpr.9.product = f32[8,4096]{1,0:T(8,128)S(1)} custom-call(f32[8,1024]{1,0:T(8,128)S(1)} %get-tuple-element.384.h_was, bf16[32,2,1024,128]{3,2,1,0:T(8,128)(2,1)} %get-tuple-element.400.weights), custom_call_target="tpu_custom_call" | custom-call | flops 8000000000 | bytes 8000000 | tf_op jit(solution)/shard_map/while/body/eval_jaxpr/pallas_call | solution.py:132
  128.6 6.1 %eval_jaxpr.10 = (f32[8,128]{1,0:T(8,128)S(1)}, bf16[8,1024]{1,0:T(8,128)(2,1)S(1)}, bf16[8,1024]{1,0:T(8,128)(2,1)S(1)}, f32[8,1024]{1,0:T(8,128)S(1)}, f32[8,1024]{1,0:T(8,128)S(1)}) custom-call(f32[8,128]{1,0:T(8,128)S(1)} %get-tuple-element.382.place, ...), custom_call_target="tpu_custom_call", output_to_operand_aliasing={{0}: (0, {}), {3}: (4, {}), {4}: (5, {})} | custom-call | tf_op jit(solution)/shard_map/while/body/eval_jaxpr/pallas_call | solution.py:158
  136.0 3.7 %eval_jaxpr.9.product = f32[8,4096]{1,0:T(8,128)S(1)} custom-call(f32[8,1024]{1,0:T(8,128)S(1)} %get-tuple-element.384.h_was, bf16[32,2,1024,128]{3,2,1,0:T(8,128)(2,1)} %get-tuple-element.400.weights), custom_call_target="tpu_custom_call" | custom-call | flops 8000000000 | bytes 8000000 | tf_op jit(solution)/shard_map/while/body/eval_jaxpr/pallas_call | solution.py:132
  139.8 6.1 %eval_jaxpr.10 = (f32[8,128]{1,0:T(8,128)S(1)}, bf16[8,1024]{1,0:T(8,128)(2,1)S(1)}, bf16[8,1024]{1,0:T(8,128)(2,1)S(1)}, f32[8,1024]{1,0:T(8,128)S(1)}, f32[8,1024]{1,0:T(8,128)S(1)}) custom-call(f32[8,128]{1,0:T(8,128)S(1)} %get-tuple-element.382.place, ...), custom_call_target="tpu_custom_call", output_to_operand_aliasing={{0}: (0, {}), {3}: (4, {}), {4}: (5, {})} | custom-call | tf_op jit(solution)/shard_map/while/body/eval_jaxpr/pallas_call | solution.py:158
  147.8 3.7 %eval_jaxpr.9.product = f32[8,4096]{1,0:T(8,128)S(1)} custom-call(f32[8,1024]{1,0:T(8,128)S(1)} %get-tuple-element.384.h_was, bf16[32,2,1024,128]{3,2,1,0:T(8,128)(2,1)} %get-tuple-element.400.weights), custom_call_target="tpu_custom_call" | custom-call | flops 8000000000 | bytes 8000000 | tf_op jit(solution)/shard_map/while/body/eval_jaxpr/pallas_call | solution.py:132
  151.6 6.1 %eval_jaxpr.10 = (f32[8,128]{1,0:T(8,128)S(1)}, bf16[8,1024]{1,0:T(8,128)(2,1)S(1)}, bf16[8,1024]{1,0:T(8,128)(2,1)S(1)}, f32[8,1024]{1,0:T(8,128)S(1)}, f32[8,1024]{1,0:T(8,128)S(1)}) custom-call(f32[8,128]{1,0:T(8,128)S(1)} %get-tuple-element.382.place, ...), custom_call_target="tpu_custom_call", output_to_operand_aliasing={{0}: (0, {}), {3}: (4, {}), {4}: (5, {})} | custom-call | tf_op jit(solution)/shard_map/while/body/eval_jaxpr/pallas_call | solution.py:158
  159.6 3.7 %eval_jaxpr.9.product = f32[8,4096]{1,0:T(8,128)S(1)} custom-call(f32[8,1024]{1,0:T(8,128)S(1)} %get-tuple-element.384.h_was, bf16[32,2,1024,128]{3,2,1,0:T(8,128)(2,1)} %get-tuple-element.400.weights), custom_call_target="tpu_custom_call" | custom-call | flops 8000000000 | bytes 8000000 | tf_op jit(solution)/shard_map/while/body/eval_jaxpr/pallas_call | solution.py:132
  163.4 6.1 %eval_jaxpr.10 = (f32[8,128]{1,0:T(8,128)S(1)}, bf16[8,1024]{1,0:T(8,128)(2,1)S(1)}, bf16[8,1024]{1,0:T(8,128)(2,1)S(1)}, f32[8,1024]{1,0:T(8,128)S(1)}, f32[8,1024]{1,0:T(8,128)S(1)}) custom-call(f32[8,128]{1,0:T(8,128)S(1)} %get-tuple-element.382.place, ...), custom_call_target="tpu_custom_call", output_to_operand_aliasing={{0}: (0, {}), {3}: (4, {}), {4}: (5, {})} | custom-call | tf_op jit(solution)/shard_map/while/body/eval_jaxpr/pallas_call | solution.py:158
  171.5 3.7 %eval_jaxpr.9.product = f32[8,4096]{1,0:T(8,128)S(1)} custom-call(f32[8,1024]{1,0:T(8,128)S(1)} %get-tuple-element.384.h_was, bf16[32,2,1024,128]{3,2,1,0:T(8,128)(2,1)} %get-tuple-element.400.weights), custom_call_target="tpu_custom_call" | custom-call | flops 8000000000 | bytes 8000000 | tf_op jit(solution)/shard_map/while/body/eval_jaxpr/pallas_call | solution.py:132
  175.2 6.1 %eval_jaxpr.10 = (f32[8,128]{1,0:T(8,128)S(1)}, bf16[8,1024]{1,0:T(8,128)(2,1)S(1)}, bf16[8,1024]{1,0:T(8,128)(2,1)S(1)}, f32[8,1024]{1,0:T(8,128)S(1)}, f32[8,1024]{1,0:T(8,128)S(1)}) custom-call(f32[8,128]{1,0:T(8,128)S(1)} %get-tuple-element.382.place, ...), custom_call_target="tpu_custom_call", output_to_operand_aliasing={{0}: (0, {}), {3}: (4, {}), {4}: (5, {})} | custom-call | tf_op jit(solution)/shard_map/while/body/eval_jaxpr/pallas_call | solution.py:158
  183.3 3.7 %eval_jaxpr.9.product = f32[8,4096]{1,0:T(8,128)S(1)} custom-call(f32[8,1024]{1,0:T(8,128)S(1)} %get-tuple-element.384.h_was, bf16[32,2,1024,128]{3,2,1,0:T(8,128)(2,1)} %get-tuple-element.400.weights), custom_call_target="tpu_custom_call" | custom-call | flops 8000000000 | bytes 8000000 | tf_op jit(solution)/shard_map/while/body/eval_jaxpr/pallas_call | solution.py:132
  187.0 6.1 %eval_jaxpr.10 = (f32[8,128]{1,0:T(8,128)S(1)}, bf16[8,1024]{1,0:T(8,128)(2,1)S(1)}, bf16[8,1024]{1,0:T(8,128)(2,1)S(1)}, f32[8,1024]{1,0:T(8,128)S(1)}, f32[8,1024]{1,0:T(8,128)S(1)}) custom-call(f32[8,128]{1,0:T(8,128)S(1)} %get-tuple-element.382.place, ...), custom_call_target="tpu_custom_call", output_to_operand_aliasing={{0}: (0, {}), {3}: (4, {}), {4}: (5, {})} | custom-call | tf_op jit(solution)/shard_map/while/body/eval_jaxpr/pallas_call | solution.py:158
  198.9 6.1 %eval_jaxpr.10 = (f32[8,128]{1,0:T(8,128)S(1)}, bf16[8,1024]{1,0:T(8,128)(2,1)S(1)}, bf16[8,1024]{1,0:T(8,128)(2,1)S(1)}, f32[8,1024]{1,0:T(8,128)S(1)}, f32[8,1024]{1,0:T(8,128)S(1)}) custom-call(f32[8,128]{1,0:T(8,128)S(1)} %get-tuple-element.382.place, ...), custom_call_target="tpu_custom_call", output_to_operand_aliasing={{0}: (0, {}), {3}: (4, {}), {4}: (5, {})} | custom-call | tf_op jit(solution)/shard_map/while/body/eval_jaxpr/pallas_call | solution.py:158
  210.7 6.1 %eval_jaxpr.10 = (f32[8,128]{1,0:T(8,128)S(1)}, bf16[8,1024]{1,0:T(8,128)(2,1)S(1)}, bf16[8,1024]{1,0:T(8,128)(2,1)S(1)}, f32[8,1024]{1,0:T(8,128)S(1)}, f32[8,1024]{1,0:T(8,128)S(1)}) custom-call(f32[8,128]{1,0:T(8,128)S(1)} %get-tuple-element.382.place, ...), custom_call_target="tpu_custom_call", output_to_operand_aliasing={{0}: (0, {}), {3}: (4, {}), {4}: (5, {})} | custom-call | tf_op jit(solution)/shard_map/while/body/eval_jaxpr/pallas_call | solution.py:158
  223.9 8.9 %collective-permute-start = (bf16[8,1024]{1,0:T(8,128)(2,1)S(1)}, bf16[8,1024]{1,0:T(8,128)(2,1)S(1)}, u32[]{:S(2)}, u32[]{:S(2)}) collective-permute-start(bf16[8,1024]{1,0:T(8,128)(2,1)S(1)} %get-tuple-element.383), channel_id=1, source_target_pairs={{0,32},{32,64},{64,96},{96,128},{128,160},{160,192},{192,224},{1,3... | collective-permute-start | bytes 49160 | tf_op jit(solution)/shard_map/while/body/eval_jaxpr/ppermute | solution.py:20
  244.1 8.9 %collective-permute-start = (bf16[8,1024]{1,0:T(8,128)(2,1)S(1)}, bf16[8,1024]{1,0:T(8,128)(2,1)S(1)}, u32[]{:S(2)}, u32[]{:S(2)}) collective-permute-start(bf16[8,1024]{1,0:T(8,128)(2,1)S(1)} %get-tuple-element.383), channel_id=1, source_target_pairs={{0,32},{32,64},{64,96},{96,128},{128,160},{160,192},{192,224},{1,3... | collective-permute-start | bytes 49160 | tf_op jit(solution)/shard_map/while/body/eval_jaxpr/ppermute | solution.py:20
  264.2 8.9 %collective-permute-start = (bf16[8,1024]{1,0:T(8,128)(2,1)S(1)}, bf16[8,1024]{1,0:T(8,128)(2,1)S(1)}, u32[]{:S(2)}, u32[]{:S(2)}) collective-permute-start(bf16[8,1024]{1,0:T(8,128)(2,1)S(1)} %get-tuple-element.383), channel_id=1, source_target_pairs={{0,32},{32,64},{64,96},{96,128},{128,160},{160,192},{192,224},{1,3... | collective-permute-start | bytes 49160 | tf_op jit(solution)/shard_map/while/body/eval_jaxpr/ppermute | solution.py:20
  280.9 16.7 %all-to-all-start.1 = ((bf16[8,8,1024]{2,1,0:T(8,128)(2,1)}), bf16[8,8,1024]{2,1,0:T(8,128)(2,1)S(1)}, u32[]{:S(2)}, u32[]{:S(2)}) async-start(bf16[8,8,1024]{2,1,0:T(8,128)(2,1)} %slice.38), calls=%async_computation.1 | async-start | bytes 262144 | tf_op jit(solution)/shard_map/all_to_all | solution.py:215
  302.5 4.2 %all-to-all-done.1 = bf16[8,8,1024]{2,1,0:T(8,128)(2,1)S(1)} async-done(((bf16[8,8,1024]{2,1,0:T(8,128)(2,1)}), bf16[8,8,1024]{2,1,0:T(8,128)(2,1)S(1)}, u32[]{:S(2)}, u32[]{:S(2)}) %all-to-all-start.1) | async-done | bytes 131104 | tf_op jit(solution)/shard_map/all_to_all | solution.py:215
  307.2 16.3 %all_to_all.22 = f32[32,1,512]{2,1,0:T(1,128)S(1)} all-to-all(f32[32,1,512]{2,1,0:T(1,128)S(1)} %reshape.110), channel_id=1, replica_groups=mesh['dp'=2,'layer'=8,'col'=32] {'col'}, dimensions={0} | all-to-all | bytes 131072 | tf_op jit(solution)/shard_map/all_to_all | solution.py:220
  (108 shorter events, 80.9 us)
Async XLA Ops:
  7.2 112.2 %all-gather.3.cloned.1.call-start = ((), (), s32[]{:S(2)}) async-start(), calls=%async_computation.3 | async-start | bytes 17039360 | tf_op jit(solution)/shard_map/all_gather | solution.py:185
  15.1 22.8 %all-to-all-start = ((f32[32,1,2176]{2,1,0:T(1,128)}), f32[32,1,2176]{2,1,0:T(1,128)S(1)}, u32[]{:S(2)}, u32[]{:S(2)}) async-start(f32[32,1,2176]{2,1,0:T(1,128)} %copy.36), calls=%async_computation | async-start | bytes 557056 | tf_op jit(solution)/shard_map/all_to_all | solution.py:193
  121.3 7.3 %collective-permute-start = (bf16[8,1024]{1,0:T(8,128)(2,1)S(1)}, bf16[8,1024]{1,0:T(8,128)(2,1)S(1)}, u32[]{:S(2)}, u32[]{:S(2)}) collective-permute-start(bf16[8,1024]{1,0:T(8,128)(2,1)S(1)} %get-tuple-element.383), channel_id=1, source_target_pairs={{0,32},{32,64},{64,96},{96,128},{128,160},{160,192},{192,224},{1,3... | collective-permute-start | bytes 49160 | tf_op jit(solution)/shard_map/while/body/eval_jaxpr/ppermute | solution.py:20
  134.7 5.0 %collective-permute-start = (bf16[8,1024]{1,0:T(8,128)(2,1)S(1)}, bf16[8,1024]{1,0:T(8,128)(2,1)S(1)}, u32[]{:S(2)}, u32[]{:S(2)}) collective-permute-start(bf16[8,1024]{1,0:T(8,128)(2,1)S(1)} %get-tuple-element.383), channel_id=1, source_target_pairs={{0,32},{32,64},{64,96},{96,128},{128,160},{160,192},{192,224},{1,3... | collective-permute-start | bytes 49160 | tf_op jit(solution)/shard_map/while/body/eval_jaxpr/ppermute | solution.py:20
  145.9 5.6 %collective-permute-start = (bf16[8,1024]{1,0:T(8,128)(2,1)S(1)}, bf16[8,1024]{1,0:T(8,128)(2,1)S(1)}, u32[]{:S(2)}, u32[]{:S(2)}) collective-permute-start(bf16[8,1024]{1,0:T(8,128)(2,1)S(1)} %get-tuple-element.383), channel_id=1, source_target_pairs={{0,32},{32,64},{64,96},{96,128},{128,160},{160,192},{192,224},{1,3... | collective-permute-start | bytes 49160 | tf_op jit(solution)/shard_map/while/body/eval_jaxpr/ppermute | solution.py:20
  157.7 5.7 %collective-permute-start = (bf16[8,1024]{1,0:T(8,128)(2,1)S(1)}, bf16[8,1024]{1,0:T(8,128)(2,1)S(1)}, u32[]{:S(2)}, u32[]{:S(2)}) collective-permute-start(bf16[8,1024]{1,0:T(8,128)(2,1)S(1)} %get-tuple-element.383), channel_id=1, source_target_pairs={{0,32},{32,64},{64,96},{96,128},{128,160},{160,192},{192,224},{1,3... | collective-permute-start | bytes 49160 | tf_op jit(solution)/shard_map/while/body/eval_jaxpr/ppermute | solution.py:20
  169.5 5.7 %collective-permute-start = (bf16[8,1024]{1,0:T(8,128)(2,1)S(1)}, bf16[8,1024]{1,0:T(8,128)(2,1)S(1)}, u32[]{:S(2)}, u32[]{:S(2)}) collective-permute-start(bf16[8,1024]{1,0:T(8,128)(2,1)S(1)} %get-tuple-element.383), channel_id=1, source_target_pairs={{0,32},{32,64},{64,96},{96,128},{128,160},{160,192},{192,224},{1,3... | collective-permute-start | bytes 49160 | tf_op jit(solution)/shard_map/while/body/eval_jaxpr/ppermute | solution.py:20
  181.4 5.7 %collective-permute-start = (bf16[8,1024]{1,0:T(8,128)(2,1)S(1)}, bf16[8,1024]{1,0:T(8,128)(2,1)S(1)}, u32[]{:S(2)}, u32[]{:S(2)}) collective-permute-start(bf16[8,1024]{1,0:T(8,128)(2,1)S(1)} %get-tuple-element.383), channel_id=1, source_target_pairs={{0,32},{32,64},{64,96},{96,128},{128,160},{160,192},{192,224},{1,3... | collective-permute-start | bytes 49160 | tf_op jit(solution)/shard_map/while/body/eval_jaxpr/ppermute | solution.py:20
  193.2 5.7 %collective-permute-start = (bf16[8,1024]{1,0:T(8,128)(2,1)S(1)}, bf16[8,1024]{1,0:T(8,128)(2,1)S(1)}, u32[]{:S(2)}, u32[]{:S(2)}) collective-permute-start(bf16[8,1024]{1,0:T(8,128)(2,1)S(1)} %get-tuple-element.383), channel_id=1, source_target_pairs={{0,32},{32,64},{64,96},{96,128},{128,160},{160,192},{192,224},{1,3... | collective-permute-start | bytes 49160 | tf_op jit(solution)/shard_map/while/body/eval_jaxpr/ppermute | solution.py:20
  205.0 5.7 %collective-permute-start = (bf16[8,1024]{1,0:T(8,128)(2,1)S(1)}, bf16[8,1024]{1,0:T(8,128)(2,1)S(1)}, u32[]{:S(2)}, u32[]{:S(2)}) collective-permute-start(bf16[8,1024]{1,0:T(8,128)(2,1)S(1)} %get-tuple-element.383), channel_id=1, source_target_pairs={{0,32},{32,64},{64,96},{96,128},{128,160},{160,192},{192,224},{1,3... | collective-permute-start | bytes 49160 | tf_op jit(solution)/shard_map/while/body/eval_jaxpr/ppermute | solution.py:20
  216.8 6.7 %collective-permute-start = (bf16[8,1024]{1,0:T(8,128)(2,1)S(1)}, bf16[8,1024]{1,0:T(8,128)(2,1)S(1)}, u32[]{:S(2)}, u32[]{:S(2)}) collective-permute-start(bf16[8,1024]{1,0:T(8,128)(2,1)S(1)} %get-tuple-element.383), channel_id=1, source_target_pairs={{0,32},{32,64},{64,96},{96,128},{128,160},{160,192},{192,224},{1,3... | collective-permute-start | bytes 49160 | tf_op jit(solution)/shard_map/while/body/eval_jaxpr/ppermute | solution.py:20
  223.9 12.7 %collective-permute-start = (bf16[8,1024]{1,0:T(8,128)(2,1)S(1)}, bf16[8,1024]{1,0:T(8,128)(2,1)S(1)}, u32[]{:S(2)}, u32[]{:S(2)}) collective-permute-start(bf16[8,1024]{1,0:T(8,128)(2,1)S(1)} %get-tuple-element.383), channel_id=1, source_target_pairs={{0,32},{32,64},{64,96},{96,128},{128,160},{160,192},{192,224},{1,3... | collective-permute-start | bytes 49160 | tf_op jit(solution)/shard_map/while/body/eval_jaxpr/ppermute | solution.py:20
  236.9 6.8 %collective-permute-start = (bf16[8,1024]{1,0:T(8,128)(2,1)S(1)}, bf16[8,1024]{1,0:T(8,128)(2,1)S(1)}, u32[]{:S(2)}, u32[]{:S(2)}) collective-permute-start(bf16[8,1024]{1,0:T(8,128)(2,1)S(1)} %get-tuple-element.383), channel_id=1, source_target_pairs={{0,32},{32,64},{64,96},{96,128},{128,160},{160,192},{192,224},{1,3... | collective-permute-start | bytes 49160 | tf_op jit(solution)/shard_map/while/body/eval_jaxpr/ppermute | solution.py:20
  244.1 12.7 %collective-permute-start = (bf16[8,1024]{1,0:T(8,128)(2,1)S(1)}, bf16[8,1024]{1,0:T(8,128)(2,1)S(1)}, u32[]{:S(2)}, u32[]{:S(2)}) collective-permute-start(bf16[8,1024]{1,0:T(8,128)(2,1)S(1)} %get-tuple-element.383), channel_id=1, source_target_pairs={{0,32},{32,64},{64,96},{96,128},{128,160},{160,192},{192,224},{1,3... | collective-permute-start | bytes 49160 | tf_op jit(solution)/shard_map/while/body/eval_jaxpr/ppermute | solution.py:20
  257.0 6.8 %collective-permute-start = (bf16[8,1024]{1,0:T(8,128)(2,1)S(1)}, bf16[8,1024]{1,0:T(8,128)(2,1)S(1)}, u32[]{:S(2)}, u32[]{:S(2)}) collective-permute-start(bf16[8,1024]{1,0:T(8,128)(2,1)S(1)} %get-tuple-element.383), channel_id=1, source_target_pairs={{0,32},{32,64},{64,96},{96,128},{128,160},{160,192},{192,224},{1,3... | collective-permute-start | bytes 49160 | tf_op jit(solution)/shard_map/while/body/eval_jaxpr/ppermute | solution.py:20
  264.2 12.7 %collective-permute-start = (bf16[8,1024]{1,0:T(8,128)(2,1)S(1)}, bf16[8,1024]{1,0:T(8,128)(2,1)S(1)}, u32[]{:S(2)}, u32[]{:S(2)}) collective-permute-start(bf16[8,1024]{1,0:T(8,128)(2,1)S(1)} %get-tuple-element.383), channel_id=1, source_target_pairs={{0,32},{32,64},{64,96},{96,128},{128,160},{160,192},{192,224},{1,3... | collective-permute-start | bytes 49160 | tf_op jit(solution)/shard_map/while/body/eval_jaxpr/ppermute | solution.py:20
  277.2 24.2 %collective-permute-start.1 = (bf16[8,1024]{1,0:T(8,128)(2,1)S(1)}, bf16[8,1024]{1,0:T(8,128)(2,1)S(1)}, u32[]{:S(2)}, u32[]{:S(2)}) collective-permute-start(bf16[8,1024]{1,0:T(8,128)(2,1)S(1)} %get-tuple-element.261), channel_id=1, source_target_pairs={{0,32},{32,64},{64,96},{96,128},{128,160},{160,192},{192,224},{1,3... | collective-permute-start | bytes 49160 | tf_op jit(solution)/shard_map/ppermute | solution.py:20
  280.9 25.8 %all-to-all-start.1 = ((bf16[8,8,1024]{2,1,0:T(8,128)(2,1)}), bf16[8,8,1024]{2,1,0:T(8,128)(2,1)S(1)}, u32[]{:S(2)}, u32[]{:S(2)}) async-start(bf16[8,8,1024]{2,1,0:T(8,128)(2,1)} %slice.38), calls=%async_computation.1 | async-start | bytes 262144 | tf_op jit(solution)/shard_map/all_to_all | solution.py:215
Sparse Core Ops, SparseCore 0:
  11.3 107.9 all-gather.2

commit v8 on v7

--- a/solution.py
+++ b/solution.py
@@ -188,12 +188,16 @@
     kept = keep(weights)
 
     local_bias = bias[0].reshape(units, 4).T.reshape(1, 4 * units)
-    mine = tokens.reshape(steps_count, cols, ROWS, units).transpose(1, 0, 2, 3).astype(jnp.float32)
-    sent = jnp.concatenate([mine.reshape(cols, -1), jnp.broadcast_to(local_bias, (cols, 4 * units))], axis=1)
+    mine = tokens.reshape(steps_count, cols, ROWS, units).transpose(1, 0, 2, 3)
+    high = lax.reduce_precision(local_bias, 8, 7)
+    middle = lax.reduce_precision(local_bias - high, 8, 7)
+    parts = jnp.concatenate([high, middle, local_bias - high - middle], axis=1).astype(jnp.bfloat16)
+    sent = jnp.concatenate([mine.reshape(cols, -1), jnp.broadcast_to(parts, (cols, 12 * units))], axis=1)
     got = lax.all_to_all(sent, "col", 0, 0, tiled=True)
     x_first = got[:, : steps_count * ROWS * units].reshape(cols, steps_count * ROWS, units).transpose(1, 0, 2)
-    x_first = x_first.reshape(chunks, STEPS * ROWS, H).astype(jnp.bfloat16)
-    bias_full = got[:, steps_count * ROWS * units :].reshape(1, 4 * H)
+    x_first = x_first.reshape(chunks, STEPS * ROWS, H)
+    parts = got[:, steps_count * ROWS * units :].astype(jnp.float32).reshape(cols, 3, 4 * units)
+    bias_full = (parts[:, 0] + parts[:, 1] + parts[:, 2]).reshape(1, 4 * H)
 
     def section(s, carry):
         place, x_sent, hidden, cell, states = carry
@@ -216,7 +220,7 @@
     _, _, hidden, cell, states = section(stages - 1, carry)
     top = jnp.where(level == layers - 1, states[chunks], moved)
     rows = jnp.concatenate([top.astype(jnp.float32), hidden[:ROWS], cell[:ROWS]], axis=0)
-    sent = rows.reshape(4 * ROWS, cols, units).transpose(1, 0, 2)
+    sent = rows.reshape(4 * ROWS, cols, units).transpose(1, 0, 2).reshape(cols, 4, ROWS * units)
     got = lax.all_to_all(sent, "col", 0, 0, tiled=True).reshape(cols, 4, ROWS, units).transpose(1, 0, 2, 3)
     got = got.reshape(4, sentences, units)
     return got[:2].astype(jnp.bfloat16), got[2:3].astype(jnp.bfloat16), got[3:]

time: 335 us -> 330 us (0.985)
  waiting for transfers between devices: 97 us -> 92.2 us
    all_to_all x1, waiting for transfers between devices: 4.24 us -> 0.5 us  [shards(): moved = lax.all_to_all(carry[4][1:], 'layer', 0, 0, tiled=True)[layers - 1]]
where the time goes in v8:
time: 330 us; the launch traced here: 329 us
  Pallas kernels  109 us (33%)
  waiting for transfers between devices  92.2 us (28%)
  starting transfers between devices  82.7 us (25%)
  blocking collectives  16.3 us (5%)
  between operations  14.3 us (4%)
  local copies, waits for them, and re-layouts  9.31 us (3%)
    all_gather x1, waiting for transfers between devices, shards(): weights = lax.all_gather(half, ('col', 'dp')).reshape(cols, 2, H, 4 * units)  81.3 us
    ppermute x15, starting transfers between devices, passed_along(): return lax.ppermute(block, axis, route)  56.1 us
    pallas_call x15, Pallas kernels, early(): pl.pallas_call(early_kernel, out_shape=jax.ShapeDtypeStruct((2 * ROWS, 4...  55.9 us
    pallas_call x15, Pallas kernels, late(): pl.pallas_call(late_kernel, out_shape=(like(place), like(x_got), like(x_g...  51.4 us
    all_to_all x1, starting transfers between devices, shards(): moved = lax.all_to_all(carry[4][1:], 'layer', 0, 0, tiled=True)[layers - 1]  16.4 us
    all_to_all x1, blocking collectives, shards(): lax.all_to_all(sent, 'col', 0, 0, tiled=True).reshape(cols, 4, ROWS, units)  16.3 us
    all_to_all x1, waiting for transfers between devices, shards(): got = lax.all_to_all(sent, 'col', 0, 0, tiled=True)  10.3 us
    all_to_all x1, starting transfers between devices, shards(): got = lax.all_to_all(sent, 'col', 0, 0, tiled=True)  10.2 us
  transfers between devices with their start and end apart: 18, of which 3 were waited for; matrix products, arithmetic and copies ran while one was open for 2% of the time, Pallas kernels for 17%

profile of v8, /device:TPU:8, one launch (start us, length us, event | category | flops | bytes accessed | tf_op | source)
XLA Modules:
  0.0 328.9 jit_solution(17823585359421278185)
XLA Ops:
  15.5 10.2 %all-to-all-start = ((bf16[32,2,1216]{2,1,0:T(2,128)(2,1)}), bf16[32,2,1216]{2,1,0:T(2,128)(2,1)S(1)}, u32[]{:S(2)}, u32[]{:S(2)}) async-start(bf16[32,2,1216]{2,1,0:T(2,128)(2,1)} %reshape.191), calls=%async_computation | async-start | bytes 327680 | tf_op jit(solution)/shard_map/all_to_all | solution.py:196
  25.7 10.3 %all-to-all-done = bf16[32,2,1216]{2,1,0:T(2,128)(2,1)S(1)} async-done(((bf16[32,2,1216]{2,1,0:T(2,128)(2,1)}), bf16[32,2,1216]{2,1,0:T(2,128)(2,1)S(1)}, u32[]{:S(2)}, u32[]{:S(2)}) %all-to-all-start) | async-done | bytes 155680 | tf_op jit(solution)/shard_map/all_to_all | solution.py:196
  37.6 81.3 %all-gather.3.cloned.1.call-done = bf16[65536,128]{1,0:T(8,128)(2,1)} async-done(((bf16[1024,128]{1,0:T(8,128)(2,1)}), bf16[65536,128]{1,0:T(8,128)(2,1)}) %all-gather.3.cloned.1.call-update) | async-done | bytes 16777232 | tf_op jit(solution)/shard_map/all_gather | solution.py:185
  120.9 155.9 %while.23 = (s32[]{:T(128)}, f32[8,128]{1,0:T(8,128)S(1)}, bf16[8,1024]{1,0:T(8,128)(2,1)S(1)}, f32[8,1024]{1,0:T(8,128)S(1)}, f32[8,1024]{1,0:T(8,128)S(1)}, /*...) while((s32[]{:T(128)}, f32[8,128]{1,0:T(8,128)S(1)}, ...), condition=%wide.region_1.2_spmd, body=%wide.region_0.1_spmd.sunk | while | flops 8000000000 | bytes 8098497 | solution.py:217
  124.4 3.7 %eval_jaxpr.9.product = f32[8,4096]{1,0:T(8,128)S(1)} custom-call(f32[8,1024]{1,0:T(8,128)S(1)} %get-tuple-element.387.h_was, bf16[32,2,1024,128]{3,2,1,0:T(8,128)(2,1)} %get-tuple-element.403.weights), custom_call_target="tpu_custom_call" | custom-call | flops 8000000000 | bytes 8000000 | tf_op jit(solution)/shard_map/while/body/eval_jaxpr/pallas_call | solution.py:132
  128.2 6.1 %eval_jaxpr.10 = (f32[8,128]{1,0:T(8,128)S(1)}, bf16[8,1024]{1,0:T(8,128)(2,1)S(1)}, bf16[8,1024]{1,0:T(8,128)(2,1)S(1)}, f32[8,1024]{1,0:T(8,128)S(1)}, f32[8,1024]{1,0:T(8,128)S(1)}) custom-call(f32[8,128]{1,0:T(8,128)S(1)} %get-tuple-element.385.place, ...), custom_call_target="tpu_custom_call", output_to_operand_aliasing={{0}: (0, {}), {3}: (4, {}), {4}: (5, {})} | custom-call | tf_op jit(solution)/shard_map/while/body/eval_jaxpr/pallas_call | solution.py:158
  135.6 3.7 %eval_jaxpr.9.product = f32[8,4096]{1,0:T(8,128)S(1)} custom-call(f32[8,1024]{1,0:T(8,128)S(1)} %get-tuple-element.387.h_was, bf16[32,2,1024,128]{3,2,1,0:T(8,128)(2,1)} %get-tuple-element.403.weights), custom_call_target="tpu_custom_call" | custom-call | flops 8000000000 | bytes 8000000 | tf_op jit(solution)/shard_map/while/body/eval_jaxpr/pallas_call | solution.py:132
  139.4 6.1 %eval_jaxpr.10 = (f32[8,128]{1,0:T(8,128)S(1)}, bf16[8,1024]{1,0:T(8,128)(2,1)S(1)}, bf16[8,1024]{1,0:T(8,128)(2,1)S(1)}, f32[8,1024]{1,0:T(8,128)S(1)}, f32[8,1024]{1,0:T(8,128)S(1)}) custom-call(f32[8,128]{1,0:T(8,128)S(1)} %get-tuple-element.385.place, ...), custom_call_target="tpu_custom_call", output_to_operand_aliasing={{0}: (0, {}), {3}: (4, {}), {4}: (5, {})} | custom-call | tf_op jit(solution)/shard_map/while/body/eval_jaxpr/pallas_call | solution.py:158
  147.4 3.7 %eval_jaxpr.9.product = f32[8,4096]{1,0:T(8,128)S(1)} custom-call(f32[8,1024]{1,0:T(8,128)S(1)} %get-tuple-element.387.h_was, bf16[32,2,1024,128]{3,2,1,0:T(8,128)(2,1)} %get-tuple-element.403.weights), custom_call_target="tpu_custom_call" | custom-call | flops 8000000000 | bytes 8000000 | tf_op jit(solution)/shard_map/while/body/eval_jaxpr/pallas_call | solution.py:132
  151.1 6.1 %eval_jaxpr.10 = (f32[8,128]{1,0:T(8,128)S(1)}, bf16[8,1024]{1,0:T(8,128)(2,1)S(1)}, bf16[8,1024]{1,0:T(8,128)(2,1)S(1)}, f32[8,1024]{1,0:T(8,128)S(1)}, f32[8,1024]{1,0:T(8,128)S(1)}) custom-call(f32[8,128]{1,0:T(8,128)S(1)} %get-tuple-element.385.place, ...), custom_call_target="tpu_custom_call", output_to_operand_aliasing={{0}: (0, {}), {3}: (4, {}), {4}: (5, {})} | custom-call | tf_op jit(solution)/shard_map/while/body/eval_jaxpr/pallas_call | solution.py:158
  159.2 3.7 %eval_jaxpr.9.product = f32[8,4096]{1,0:T(8,128)S(1)} custom-call(f32[8,1024]{1,0:T(8,128)S(1)} %get-tuple-element.387.h_was, bf16[32,2,1024,128]{3,2,1,0:T(8,128)(2,1)} %get-tuple-element.403.weights), custom_call_target="tpu_custom_call" | custom-call | flops 8000000000 | bytes 8000000 | tf_op jit(solution)/shard_map/while/body/eval_jaxpr/pallas_call | solution.py:132
  163.0 6.1 %eval_jaxpr.10 = (f32[8,128]{1,0:T(8,128)S(1)}, bf16[8,1024]{1,0:T(8,128)(2,1)S(1)}, bf16[8,1024]{1,0:T(8,128)(2,1)S(1)}, f32[8,1024]{1,0:T(8,128)S(1)}, f32[8,1024]{1,0:T(8,128)S(1)}) custom-call(f32[8,128]{1,0:T(8,128)S(1)} %get-tuple-element.385.place, ...), custom_call_target="tpu_custom_call", output_to_operand_aliasing={{0}: (0, {}), {3}: (4, {}), {4}: (5, {})} | custom-call | tf_op jit(solution)/shard_map/while/body/eval_jaxpr/pallas_call | solution.py:158
  171.0 3.7 %eval_jaxpr.9.product = f32[8,4096]{1,0:T(8,128)S(1)} custom-call(f32[8,1024]{1,0:T(8,128)S(1)} %get-tuple-element.387.h_was, bf16[32,2,1024,128]{3,2,1,0:T(8,128)(2,1)} %get-tuple-element.403.weights), custom_call_target="tpu_custom_call" | custom-call | flops 8000000000 | bytes 8000000 | tf_op jit(solution)/shard_map/while/body/eval_jaxpr/pallas_call | solution.py:132
  174.8 6.1 %eval_jaxpr.10 = (f32[8,128]{1,0:T(8,128)S(1)}, bf16[8,1024]{1,0:T(8,128)(2,1)S(1)}, bf16[8,1024]{1,0:T(8,128)(2,1)S(1)}, f32[8,1024]{1,0:T(8,128)S(1)}, f32[8,1024]{1,0:T(8,128)S(1)}) custom-call(f32[8,128]{1,0:T(8,128)S(1)} %get-tuple-element.385.place, ...), custom_call_target="tpu_custom_call", output_to_operand_aliasing={{0}: (0, {}), {3}: (4, {}), {4}: (5, {})} | custom-call | tf_op jit(solution)/shard_map/while/body/eval_jaxpr/pallas_call | solution.py:158
  186.6 6.1 %eval_jaxpr.10 = (f32[8,128]{1,0:T(8,128)S(1)}, bf16[8,1024]{1,0:T(8,128)(2,1)S(1)}, bf16[8,1024]{1,0:T(8,128)(2,1)S(1)}, f32[8,1024]{1,0:T(8,128)S(1)}, f32[8,1024]{1,0:T(8,128)S(1)}) custom-call(f32[8,128]{1,0:T(8,128)S(1)} %get-tuple-element.385.place, ...), custom_call_target="tpu_custom_call", output_to_operand_aliasing={{0}: (0, {}), {3}: (4, {}), {4}: (5, {})} | custom-call | tf_op jit(solution)/shard_map/while/body/eval_jaxpr/pallas_call | solution.py:158
  194.7 3.7 %eval_jaxpr.9.product = f32[8,4096]{1,0:T(8,128)S(1)} custom-call(f32[8,1024]{1,0:T(8,128)S(1)} %get-tuple-element.387.h_was, bf16[32,2,1024,128]{3,2,1,0:T(8,128)(2,1)} %get-tuple-element.403.weights), custom_call_target="tpu_custom_call" | custom-call | flops 8000000000 | bytes 8000000 | tf_op jit(solution)/shard_map/while/body/eval_jaxpr/pallas_call | solution.py:132
  198.4 6.1 %eval_jaxpr.10 = (f32[8,128]{1,0:T(8,128)S(1)}, bf16[8,1024]{1,0:T(8,128)(2,1)S(1)}, bf16[8,1024]{1,0:T(8,128)(2,1)S(1)}, f32[8,1024]{1,0:T(8,128)S(1)}, f32[8,1024]{1,0:T(8,128)S(1)}) custom-call(f32[8,128]{1,0:T(8,128)S(1)} %get-tuple-element.385.place, ...), custom_call_target="tpu_custom_call", output_to_operand_aliasing={{0}: (0, {}), {3}: (4, {}), {4}: (5, {})} | custom-call | tf_op jit(solution)/shard_map/while/body/eval_jaxpr/pallas_call | solution.py:158
  210.3 6.1 %eval_jaxpr.10 = (f32[8,128]{1,0:T(8,128)S(1)}, bf16[8,1024]{1,0:T(8,128)(2,1)S(1)}, bf16[8,1024]{1,0:T(8,128)(2,1)S(1)}, f32[8,1024]{1,0:T(8,128)S(1)}, f32[8,1024]{1,0:T(8,128)S(1)}) custom-call(f32[8,128]{1,0:T(8,128)S(1)} %get-tuple-element.385.place, ...), custom_call_target="tpu_custom_call", output_to_operand_aliasing={{0}: (0, {}), {3}: (4, {}), {4}: (5, {})} | custom-call | tf_op jit(solution)/shard_map/while/body/eval_jaxpr/pallas_call | solution.py:158
  223.5 8.9 %collective-permute-start = (bf16[8,1024]{1,0:T(8,128)(2,1)S(1)}, bf16[8,1024]{1,0:T(8,128)(2,1)S(1)}, u32[]{:S(2)}, u32[]{:S(2)}) collective-permute-start(bf16[8,1024]{1,0:T(8,128)(2,1)S(1)} %get-tuple-element.386), channel_id=1, source_target_pairs={{0,32},{32,64},{64,96},{96,128},{128,160},{160,192},{192,224},{1,3... | collective-permute-start | bytes 49160 | tf_op jit(solution)/shard_map/while/body/eval_jaxpr/ppermute | solution.py:20
  243.6 8.9 %collective-permute-start = (bf16[8,1024]{1,0:T(8,128)(2,1)S(1)}, bf16[8,1024]{1,0:T(8,128)(2,1)S(1)}, u32[]{:S(2)}, u32[]{:S(2)}) collective-permute-start(bf16[8,1024]{1,0:T(8,128)(2,1)S(1)} %get-tuple-element.386), channel_id=1, source_target_pairs={{0,32},{32,64},{64,96},{96,128},{128,160},{160,192},{192,224},{1,3... | collective-permute-start | bytes 49160 | tf_op jit(solution)/shard_map/while/body/eval_jaxpr/ppermute | solution.py:20
  263.8 8.9 %collective-permute-start = (bf16[8,1024]{1,0:T(8,128)(2,1)S(1)}, bf16[8,1024]{1,0:T(8,128)(2,1)S(1)}, u32[]{:S(2)}, u32[]{:S(2)}) collective-permute-start(bf16[8,1024]{1,0:T(8,128)(2,1)S(1)} %get-tuple-element.386), channel_id=1, source_target_pairs={{0,32},{32,64},{64,96},{96,128},{128,160},{160,192},{192,224},{1,3... | collective-permute-start | bytes 49160 | tf_op jit(solution)/shard_map/while/body/eval_jaxpr/ppermute | solution.py:20
  277.4 16.4 %all-to-all-start.1 = ((bf16[8,8,1024]{2,1,0:T(8,128)(2,1)}), bf16[8,8,1024]{2,1,0:T(8,128)(2,1)S(1)}, u32[]{:S(2)}, u32[]{:S(2)}) async-start(bf16[8,8,1024]{2,1,0:T(8,128)(2,1)} %slice.49), calls=%async_computation.1 | async-start | bytes 262144 | tf_op jit(solution)/shard_map/all_to_all | solution.py:219
  293.8 3.9 %collective-permute-start.1 = (bf16[8,1024]{1,0:T(8,128)(2,1)S(1)}, bf16[8,1024]{1,0:T(8,128)(2,1)S(1)}, u32[]{:S(2)}, u32[]{:S(2)}) collective-permute-start(bf16[8,1024]{1,0:T(8,128)(2,1)S(1)} %get-tuple-element.261), channel_id=1, source_target_pairs={{0,32},{32,64},{64,96},{96,128},{128,160},{160,192},{192,224},{1,3... | collective-permute-start | bytes 49160 | tf_op jit(solution)/shard_map/ppermute | solution.py:20
  303.4 16.3 %all_to_all.22 = f32[32,4,128]{2,1,0:T(4,128)S(1)} all-to-all(f32[32,4,128]{2,1,0:T(4,128)S(1)} %reshape.174), channel_id=1, replica_groups=mesh['dp'=2,'layer'=8,'col'=32] {'col'}, dimensions={0} | all-to-all | bytes 131072 | tf_op jit(solution)/shard_map/all_to_all | solution.py:224
  (108 shorter events, 77.4 us)
Async XLA Ops:
  7.2 111.8 %all-gather.3.cloned.1.call-start = ((), (), s32[]{:S(2)}) async-start(), calls=%async_computation.3 | async-start | bytes 17039360 | tf_op jit(solution)/shard_map/all_gather | solution.py:185
  15.5 20.5 %all-to-all-start = ((bf16[32,2,1216]{2,1,0:T(2,128)(2,1)}), bf16[32,2,1216]{2,1,0:T(2,128)(2,1)S(1)}, u32[]{:S(2)}, u32[]{:S(2)}) async-start(bf16[32,2,1216]{2,1,0:T(2,128)(2,1)} %reshape.191), calls=%async_computation | async-start | bytes 327680 | tf_op jit(solution)/shard_map/all_to_all | solution.py:196
  120.9 7.3 %collective-permute-start = (bf16[8,1024]{1,0:T(8,128)(2,1)S(1)}, bf16[8,1024]{1,0:T(8,128)(2,1)S(1)}, u32[]{:S(2)}, u32[]{:S(2)}) collective-permute-start(bf16[8,1024]{1,0:T(8,128)(2,1)S(1)} %get-tuple-element.386), channel_id=1, source_target_pairs={{0,32},{32,64},{64,96},{96,128},{128,160},{160,192},{192,224},{1,3... | collective-permute-start | bytes 49160 | tf_op jit(solution)/shard_map/while/body/eval_jaxpr/ppermute | solution.py:20
  134.3 5.0 %collective-permute-start = (bf16[8,1024]{1,0:T(8,128)(2,1)S(1)}, bf16[8,1024]{1,0:T(8,128)(2,1)S(1)}, u32[]{:S(2)}, u32[]{:S(2)}) collective-permute-start(bf16[8,1024]{1,0:T(8,128)(2,1)S(1)} %get-tuple-element.386), channel_id=1, source_target_pairs={{0,32},{32,64},{64,96},{96,128},{128,160},{160,192},{192,224},{1,3... | collective-permute-start | bytes 49160 | tf_op jit(solution)/shard_map/while/body/eval_jaxpr/ppermute | solution.py:20
  145.5 5.6 %collective-permute-start = (bf16[8,1024]{1,0:T(8,128)(2,1)S(1)}, bf16[8,1024]{1,0:T(8,128)(2,1)S(1)}, u32[]{:S(2)}, u32[]{:S(2)}) collective-permute-start(bf16[8,1024]{1,0:T(8,128)(2,1)S(1)} %get-tuple-element.386), channel_id=1, source_target_pairs={{0,32},{32,64},{64,96},{96,128},{128,160},{160,192},{192,224},{1,3... | collective-permute-start | bytes 49160 | tf_op jit(solution)/shard_map/while/body/eval_jaxpr/ppermute | solution.py:20
  157.3 5.7 %collective-permute-start = (bf16[8,1024]{1,0:T(8,128)(2,1)S(1)}, bf16[8,1024]{1,0:T(8,128)(2,1)S(1)}, u32[]{:S(2)}, u32[]{:S(2)}) collective-permute-start(bf16[8,1024]{1,0:T(8,128)(2,1)S(1)} %get-tuple-element.386), channel_id=1, source_target_pairs={{0,32},{32,64},{64,96},{96,128},{128,160},{160,192},{192,224},{1,3... | collective-permute-start | bytes 49160 | tf_op jit(solution)/shard_map/while/body/eval_jaxpr/ppermute | solution.py:20
  169.1 5.7 %collective-permute-start = (bf16[8,1024]{1,0:T(8,128)(2,1)S(1)}, bf16[8,1024]{1,0:T(8,128)(2,1)S(1)}, u32[]{:S(2)}, u32[]{:S(2)}) collective-permute-start(bf16[8,1024]{1,0:T(8,128)(2,1)S(1)} %get-tuple-element.386), channel_id=1, source_target_pairs={{0,32},{32,64},{64,96},{96,128},{128,160},{160,192},{192,224},{1,3... | collective-permute-start | bytes 49160 | tf_op jit(solution)/shard_map/while/body/eval_jaxpr/ppermute | solution.py:20
  180.9 5.7 %collective-permute-start = (bf16[8,1024]{1,0:T(8,128)(2,1)S(1)}, bf16[8,1024]{1,0:T(8,128)(2,1)S(1)}, u32[]{:S(2)}, u32[]{:S(2)}) collective-permute-start(bf16[8,1024]{1,0:T(8,128)(2,1)S(1)} %get-tuple-element.386), channel_id=1, source_target_pairs={{0,32},{32,64},{64,96},{96,128},{128,160},{160,192},{192,224},{1,3... | collective-permute-start | bytes 49160 | tf_op jit(solution)/shard_map/while/body/eval_jaxpr/ppermute | solution.py:20
  192.8 5.7 %collective-permute-start = (bf16[8,1024]{1,0:T(8,128)(2,1)S(1)}, bf16[8,1024]{1,0:T(8,128)(2,1)S(1)}, u32[]{:S(2)}, u32[]{:S(2)}) collective-permute-start(bf16[8,1024]{1,0:T(8,128)(2,1)S(1)} %get-tuple-element.386), channel_id=1, source_target_pairs={{0,32},{32,64},{64,96},{96,128},{128,160},{160,192},{192,224},{1,3... | collective-permute-start | bytes 49160 | tf_op jit(solution)/shard_map/while/body/eval_jaxpr/ppermute | solution.py:20
  204.6 5.7 %collective-permute-start = (bf16[8,1024]{1,0:T(8,128)(2,1)S(1)}, bf16[8,1024]{1,0:T(8,128)(2,1)S(1)}, u32[]{:S(2)}, u32[]{:S(2)}) collective-permute-start(bf16[8,1024]{1,0:T(8,128)(2,1)S(1)} %get-tuple-element.386), channel_id=1, source_target_pairs={{0,32},{32,64},{64,96},{96,128},{128,160},{160,192},{192,224},{1,3... | collective-permute-start | bytes 49160 | tf_op jit(solution)/shard_map/while/body/eval_jaxpr/ppermute | solution.py:20
  216.4 6.7 %collective-permute-start = (bf16[8,1024]{1,0:T(8,128)(2,1)S(1)}, bf16[8,1024]{1,0:T(8,128)(2,1)S(1)}, u32[]{:S(2)}, u32[]{:S(2)}) collective-permute-start(bf16[8,1024]{1,0:T(8,128)(2,1)S(1)} %get-tuple-element.386), channel_id=1, source_target_pairs={{0,32},{32,64},{64,96},{96,128},{128,160},{160,192},{192,224},{1,3... | collective-permute-start | bytes 49160 | tf_op jit(solution)/shard_map/while/body/eval_jaxpr/ppermute | solution.py:20
  223.5 12.7 %collective-permute-start = (bf16[8,1024]{1,0:T(8,128)(2,1)S(1)}, bf16[8,1024]{1,0:T(8,128)(2,1)S(1)}, u32[]{:S(2)}, u32[]{:S(2)}) collective-permute-start(bf16[8,1024]{1,0:T(8,128)(2,1)S(1)} %get-tuple-element.386), channel_id=1, source_target_pairs={{0,32},{32,64},{64,96},{96,128},{128,160},{160,192},{192,224},{1,3... | collective-permute-start | bytes 49160 | tf_op jit(solution)/shard_map/while/body/eval_jaxpr/ppermute | solution.py:20
  236.5 6.8 %collective-permute-start = (bf16[8,1024]{1,0:T(8,128)(2,1)S(1)}, bf16[8,1024]{1,0:T(8,128)(2,1)S(1)}, u32[]{:S(2)}, u32[]{:S(2)}) collective-permute-start(bf16[8,1024]{1,0:T(8,128)(2,1)S(1)} %get-tuple-element.386), channel_id=1, source_target_pairs={{0,32},{32,64},{64,96},{96,128},{128,160},{160,192},{192,224},{1,3... | collective-permute-start | bytes 49160 | tf_op jit(solution)/shard_map/while/body/eval_jaxpr/ppermute | solution.py:20
  243.6 12.7 %collective-permute-start = (bf16[8,1024]{1,0:T(8,128)(2,1)S(1)}, bf16[8,1024]{1,0:T(8,128)(2,1)S(1)}, u32[]{:S(2)}, u32[]{:S(2)}) collective-permute-start(bf16[8,1024]{1,0:T(8,128)(2,1)S(1)} %get-tuple-element.386), channel_id=1, source_target_pairs={{0,32},{32,64},{64,96},{96,128},{128,160},{160,192},{192,224},{1,3... | collective-permute-start | bytes 49160 | tf_op jit(solution)/shard_map/while/body/eval_jaxpr/ppermute | solution.py:20
  256.6 6.8 %collective-permute-start = (bf16[8,1024]{1,0:T(8,128)(2,1)S(1)}, bf16[8,1024]{1,0:T(8,128)(2,1)S(1)}, u32[]{:S(2)}, u32[]{:S(2)}) collective-permute-start(bf16[8,1024]{1,0:T(8,128)(2,1)S(1)} %get-tuple-element.386), channel_id=1, source_target_pairs={{0,32},{32,64},{64,96},{96,128},{128,160},{160,192},{192,224},{1,3... | collective-permute-start | bytes 49160 | tf_op jit(solution)/shard_map/while/body/eval_jaxpr/ppermute | solution.py:20
  263.8 12.7 %collective-permute-start = (bf16[8,1024]{1,0:T(8,128)(2,1)S(1)}, bf16[8,1024]{1,0:T(8,128)(2,1)S(1)}, u32[]{:S(2)}, u32[]{:S(2)}) collective-permute-start(bf16[8,1024]{1,0:T(8,128)(2,1)S(1)} %get-tuple-element.386), channel_id=1, source_target_pairs={{0,32},{32,64},{64,96},{96,128},{128,160},{160,192},{192,224},{1,3... | collective-permute-start | bytes 49160 | tf_op jit(solution)/shard_map/while/body/eval_jaxpr/ppermute | solution.py:20
  277.4 25.5 %all-to-all-start.1 = ((bf16[8,8,1024]{2,1,0:T(8,128)(2,1)}), bf16[8,8,1024]{2,1,0:T(8,128)(2,1)S(1)}, u32[]{:S(2)}, u32[]{:S(2)}) async-start(bf16[8,8,1024]{2,1,0:T(8,128)(2,1)} %slice.49), calls=%async_computation.1 | async-start | bytes 262144 | tf_op jit(solution)/shard_map/all_to_all | solution.py:219
  293.8 7.7 %collective-permute-start.1 = (bf16[8,1024]{1,0:T(8,128)(2,1)S(1)}, bf16[8,1024]{1,0:T(8,128)(2,1)S(1)}, u32[]{:S(2)}, u32[]{:S(2)}) collective-permute-start(bf16[8,1024]{1,0:T(8,128)(2,1)S(1)} %get-tuple-element.261), channel_id=1, source_target_pairs={{0,32},{32,64},{64,96},{96,128},{128,160},{160,192},{192,224},{1,3... | collective-permute-start | bytes 49160 | tf_op jit(solution)/shard_map/ppermute | solution.py:20
Sparse Core Ops, SparseCore 0:
  11.3 107.5 all-gather.2
